TPU v7x, 32 devices: a whole 2x2x4 slice. The times are simulated.
32 devices in a mesh: child: 4 (over y, x), tile: 8 (over z, core).
Axes of the slice: x: 2, y: 2, z: 4, core: 2. Of those that a mesh axis runs over, the one named last changes fastest.
Arguments:
- child_tiles: bfloat16 [4, 128, 512, 512], P('child', 'tile'), may hold values from -6 to 6
- panel: bfloat16 [4, 4096, 512], P('child', 'tile'), may hold values from -1 to 1
- bases: bfloat16 [4, 4096, 128], P('child', 'tile'), may hold values from -0.25 to 0.25
- tile_blocks: int32 [4, 128, 2], P('child'), may hold values from 0 to 7, as said below
- tile_dest: int32 [4, 128, 1], P('child'), may hold values from 0 to 7; in each aligned block of 16 rows (0 to 15, 16 to 31, ..., all dimensions but the last counted through in order) at most 2 rows name the same one
- tile_slot: int32 [4, 128], P('child'), may hold values from 0 to 7
- parent_tiles: bfloat16 [4, 64, 512, 512], P('child', 'tile'), may hold values from -6 to 6
- parent_blocks: int32 [4, 64, 2], P('child', 'tile'), may hold values from 0 to 7, as said below
- sketch_test: bfloat16 [4096, 128], replicated, may hold values from -0.25 to 0.25
Outputs:
- updated_tiles: bfloat16 [4, 64, 512, 512], P('child', 'tile')
- row_sketch: float32 [4096, 128], P(('child', 'tile'))
Inputs may be any that keep to these rules, and one draw needn't show every extreme that they name: `tile_blocks`: each tile's row block is not below its column block. `tile_dest`: among the tiles of one device (aligned blocks of 16 tiles of a child), at most 2 name the same owner. `parent_blocks`: each parent tile's row block is not below its column block.
All inputs are finite; a program needn't handle non-finite values.
Results may differ from a plain program's by a relative error of at most 0.0063.
Values may be sent and summed in bfloat16 or wider, within the bound.
No kernel may reach another device: no remote copies, remote signals or barrier semaphores. Data moves between devices by JAX's collectives and lax.ppermute only.
A program may use at most 192 MiB of HBM per device.

v0:
```python
import math

import jax
import jax.numpy as jnp
from jax import lax
from jax.sharding import PartitionSpec as P

CAP = 2


def shards(
    child_tiles,
    panel,
    bases,
    tile_blocks,
    tile_dest,
    tile_slot,
    parent_tiles,
    parent_blocks,
    sketch_test,
):
    owners = lax.axis_size("tile")
    myself = lax.axis_index("tile")
    tile_count = child_tiles.shape[1]
    tile_order = child_tiles.shape[2]
    rank_width = bases.shape[2]
    sketch_width = sketch_test.shape[1]
    parent_count = parent_tiles.shape[1]
    own_tiles = child_tiles[0]
    blocks_all = tile_blocks[0]
    own_blocks = lax.dynamic_slice_in_dim(blocks_all, myself * tile_count, tile_count, 0)
    row_ids = own_blocks[:, 0]
    col_ids = own_blocks[:, 1]
    whole_panel, whole_bases = (
        lax.all_gather(panel[0], "tile", axis=0, tiled=True),
        lax.all_gather(bases[0], "tile", axis=0, tiled=True),
    )
    panel_blocks = whole_panel.reshape(-1, tile_order, tile_order)
    basis_blocks = whole_bases.reshape(-1, tile_order, rank_width)
    left_basis = jnp.take(basis_blocks, row_ids, axis=0)
    right_basis = jnp.take(basis_blocks, col_ids, axis=0)
    left_proj = jnp.einsum(
        "qxr,qxy->qry",
        left_basis,
        jnp.take(panel_blocks, row_ids, axis=0),
        preferred_element_type=jnp.float32,
    ).astype(jnp.bfloat16)
    right_proj = jnp.einsum(
        "qxr,qxy->qry",
        right_basis,
        jnp.take(panel_blocks, col_ids, axis=0),
        preferred_element_type=jnp.float32,
    ).astype(jnp.bfloat16)
    half = jnp.einsum(
        "qxr,qxy->qry", left_basis, own_tiles, preferred_element_type=jnp.float32
    ).astype(jnp.bfloat16)
    encoded = jnp.einsum("qry,qys->qrs", half, right_basis, preferred_element_type=jnp.float32)
    cross = jnp.einsum("qrk,qsk->qrs", left_proj, right_proj, preferred_element_type=jnp.float32)
    cores = (encoded - cross).astype(jnp.bfloat16)
    dest_all = tile_dest[0, :, 0].reshape(owners, tile_count)
    own_dest = lax.dynamic_index_in_dim(dest_all, myself, 0, keepdims=False)
    targets = jnp.arange(owners, dtype=jnp.int32)
    slot_ids = jnp.arange(CAP, dtype=jnp.int32)
    hit_table = (own_dest[:, None] == targets[None, :]).astype(jnp.int32)
    before = jnp.cumsum(hit_table, axis=0) - hit_table
    position = jnp.sum(hit_table * before, axis=1)
    selector = (
        (own_dest[None, None, :] == targets[:, None, None])
        & (position[None, None, :] == slot_ids[None, :, None])
    ).astype(jnp.bfloat16)
    outgoing = jnp.einsum(
        "tkq,qrs->tkrs", selector, cores, preferred_element_type=jnp.float32
    ).astype(jnp.bfloat16)
    incoming = lax.all_to_all(outgoing, "tile", split_axis=0, concat_axis=0, tiled=True)
    arrive = (dest_all == myself).astype(jnp.int32)
    earlier = jnp.cumsum(arrive, axis=1) - arrive
    matched = arrive[:, None, :] * (earlier[:, None, :] == slot_ids[None, :, None]).astype(
        jnp.int32
    )
    rows_all = blocks_all[:, 0].reshape(owners, tile_count)
    cols_all = blocks_all[:, 1].reshape(owners, tile_count)
    slots_all = tile_slot[0].reshape(owners, tile_count)
    recv_rows = jnp.sum(matched * rows_all[:, None, :], axis=2).reshape(-1)
    recv_cols = jnp.sum(matched * cols_all[:, None, :], axis=2).reshape(-1)
    recv_slots = jnp.sum(matched * slots_all[:, None, :], axis=2).reshape(-1)
    recv_live = jnp.sum(matched, axis=2).reshape(-1)
    recv_slots = jnp.where(recv_live > 0, recv_slots, parent_count)
    items = owners * CAP
    group_size = math.gcd(items, 8)
    groups = items // group_size
    received = incoming.reshape(groups, group_size, rank_width, rank_width)
    left_bases = jnp.take(basis_blocks, recv_rows, axis=0).reshape(
        groups, group_size, tile_order, rank_width
    )
    right_bases = jnp.take(basis_blocks, recv_cols, axis=0).reshape(
        groups, group_size, tile_order, rank_width
    )
    slot_groups = recv_slots.reshape(groups, group_size)

    def decode(summed, pieces):
        left_group, right_group, core_group, slot_group = pieces
        left_part = jnp.einsum(
            "gxr,grs->gxs", left_group, core_group, preferred_element_type=jnp.float32
        ).astype(jnp.bfloat16)
        decoded = jnp.einsum(
            "gxs,gys->gxy", left_part, right_group, preferred_element_type=jnp.float32
        )
        return (summed + jax.ops.segment_sum(decoded, slot_group, num_segments=parent_count), None)

    summed, _ = lax.scan(
        decode,
        parent_tiles[0].astype(jnp.float32),
        (left_bases, right_bases, received, slot_groups),
    )
    updated = summed.astype(jnp.bfloat16)
    prow = parent_blocks[0, :, 0]
    pcol = parent_blocks[0, :, 1]
    test_blocks = sketch_test.reshape(-1, tile_order, sketch_width)
    block_total = test_blocks.shape[0]
    direct = jnp.einsum(
        "pxy,pyk->pxk",
        updated,
        jnp.take(test_blocks, pcol, axis=0),
        preferred_element_type=jnp.float32,
    )
    second = jnp.einsum(
        "pyx,pyk->pxk",
        updated,
        jnp.take(test_blocks, prow, axis=0),
        preferred_element_type=jnp.float32,
    )
    second = second * (prow != pcol).astype(jnp.float32)[:, None, None]
    partial_sketch = jax.ops.segment_sum(
        direct, prow, num_segments=block_total
    ) + jax.ops.segment_sum(second, pcol, num_segments=block_total)
    partial_sketch = partial_sketch.reshape(-1, sketch_width)
    by_child = lax.psum_scatter(partial_sketch, "child", scatter_dimension=0, tiled=True)
    row_sketch = lax.psum_scatter(by_child, "tile", scatter_dimension=0, tiled=True)
    return (updated[None], row_sketch)


def solution(mesh):
    return jax.shard_map(
        shards,
        mesh=mesh,
        in_specs=(
            P("child", "tile", None, None),
            P("child", "tile", None),
            P("child", "tile", None),
            P("child", None, None),
            P("child", None, None),
            P("child", None),
            P("child", "tile", None, None),
            P("child", "tile", None),
            P(),
        ),
        out_specs=(P("child", "tile", None, None), P(("child", "tile"), None)),
        check_vma=False,
    )
```

profile of v0, /device:TPU:0, one launch (start us, length us, event | category | flops | bytes accessed | tf_op | source)
XLA Modules:
  0.0 274.5 jit_solution(15704363805796798550)
XLA Ops:
  7.2 0.0 all-gather.5.cloned.1.call-start
  7.2 0.7 all-gather.5.cloned.1.call-update
  7.9 0.0 all-gather.7.cloned.1.call-start
  8.0 0.7 all-gather.7.cloned.1.call-update
  8.7 0.5 broadcast.217
  9.2 1.3 reduce.15
  10.5 0.1 reshape_squeeze.3
  10.6 0.1 fusion.63
  10.7 0.2 reduce_window_sum.22
  10.9 1.3 reduce.14
  12.2 0.1 mul.54
  12.3 0.8 slice_reduce_fusion
  13.1 0.1 mul.57
  13.1 0.1 mul.62
  13.2 0.2 fusion.62
  13.5 0.1 copy.25
  13.5 0.1 reshape.142
  13.6 0.1 copy.31
  13.7 0.1 reshape.146
  13.8 0.8 dynamic-slice_bitcast_fusion
  14.6 0.8 compare_and_fusion
  15.4 0.2 select_reduce_fusion.1
  15.6 6.6 %bitcast_convert_fusion = f32[8,512,512]{2,1,0:T(8,128)} fusion(bf16[1,8,512,512]{3,2,1,0:T(8,128)(2,1)} %param.23), kind=kLoop, calls=%fused_computation.30 | loop fusion | flops 2097152 | bytes 12582912 | tf_op jit(solution)/shard_map/convert_element_type | solution.py:112
  22.2 12.4 %all-gather.5.cloned.1.call-done = bf16[1,4096,128]{2,1,0:T(8,128)(2,1)} async-done(((bf16[1,512,128]{2,1,0:T(8,128)(2,1)}), bf16[1,4096,128]{2,1,0:T(8,128)(2,1)}) %all-gather.5.cloned.1.call-update) | async-done | bytes 1048592 | tf_op jit(solution)/shard_map/all_gather | solution.py:36
  34.6 3.5 %gather_fusion.2 = bf16[16,512,128]{2,1,0:T(8,128)(2,1)} fusion(bf16[8,512,128]{2,1,0:T(8,128)(2,1)} %bitcast.79, s32[1024]{0:T(1024)S(1)} %get-tuple-element.76), kind=kCustom, calls=%fused_computation.4.clone | custom fusion | bytes 4194368 | tf_op jit(solution)/shard_map/jit(_take)/gather | solution.py:41
  38.1 2.1 gather_fusion.1
  40.2 8.6 %fusion.27 = f32[16,128,128]{2,1,0:T(8,128)} fusion(bf16[1,16,512,512]{3,2,1,0:T(8,128)(2,1)} %param.17, bf16[16,512,128]{2,1,0:T(8,128)(2,1)} %gather_fusion.1, pred[16]{0:T(512)(128)(4,1)S(1)} %get-tuple-element.70, bf16[16,512,128]{2,1,0:T(8,128)(2,1)} %gather_fusion.2, pred[16]{0:T(512)(128)(4,1)S(1)} %get-tuple-element.60), kind=kOutput, calls=%fused_computation.36 | convolution fusion | flops 1345323008 | bytes 13631520 | tf_op jit(solution)/shard_map/qry,qys->qrs/dot_general | solution.py:57
  48.8 33.9 %all-gather.7.cloned.1.call-done = bf16[1,4096,512]{2,1,0:T(8,128)(2,1)} async-done(((bf16[1,512,512]{2,1,0:T(8,128)(2,1)}), bf16[1,4096,512]{2,1,0:T(8,128)(2,1)}) %all-gather.7.cloned.1.call-update) | async-done | bytes 4194320 | tf_op jit(solution)/shard_map/all_gather | solution.py:35
  82.7 6.9 %gather_fusion.4 = bf16[16,512,512]{2,1,0:T(8,128)(2,1)} fusion(bf16[8,512,512]{2,1,0:T(8,128)(2,1)} %bitcast.77, s32[1024]{0:T(1024)S(1)} %get-tuple-element.76), kind=kCustom, calls=%fused_computation.6.clone | custom fusion | bytes 16777280 | tf_op jit(solution)/shard_map/jit(_take)/gather | solution.py:51
  89.6 6.9 %gather_fusion.3 = bf16[16,512,512]{2,1,0:T(8,128)(2,1)} fusion(bf16[8,512,512]{2,1,0:T(8,128)(2,1)} %bitcast.78, s32[1024]{0:T(1024)S(1)} %get-tuple-element.77), kind=kCustom, calls=%fused_computation.1.clone | custom fusion | bytes 16777280 | tf_op jit(solution)/shard_map/jit(_take)/gather | solution.py:45
  96.6 7.3 %fusion.16 = bf16[16,128,512]{2,1,0:T(8,128)(2,1)} fusion(bf16[16,512,512]{2,1,0:T(8,128)(2,1)} %gather_fusion.4, pred[16]{0:T(512)(128)(4,1)S(1)} %get-tuple-element.60, bf16[16,512,128]{2,1,0:T(8,128)(2,1)} %gather_fusion.2), kind=kOutput, calls=%fused_computation.24 | convolution fusion | flops 1078984704 | bytes 12582928 | tf_op jit(solution)/shard_map/qxr,qxy->qry/dot_general | solution.py:48
  103.9 7.3 %fusion.44 = bf16[16,128,128]{2,1,0:T(8,128)(2,1)S(1)} fusion(f32[16,128,128]{2,1,0:T(8,128)} %fusion.27, bf16[16,128,512]{2,1,0:T(8,128)(2,1)} %fusion.16, bf16[16,512,512]{2,1,0:T(8,128)(2,1)} %gather_fusion.3, pred[16]{0:T(512)(128)(4,1)S(1)} %get-tuple-element.70, bf16[16,512,128]{2,1,0:T(8,128)(2,1)} %gather_fusion.1), kind=kOutput, calls=%fused_computation.44 | convolution fusion | flops 1348993024 | bytes 14155792 | tf_op jit(solution)/shard_map/qrk,qsk->qrs/dot_general | solution.py:58
  111.2 0.4 convolution_convert_fusion.1
  111.6 0.9 copy.30
  112.6 4.1 %all-to-all-start = ((bf16[8,2,128,128]{3,2,1,0:T(8,128)(2,1)}), bf16[8,2,128,128]{3,2,1,0:T(8,128)(2,1)}, u32[]{:S(2)}, u32[]{:S(2)}) async-start(bf16[8,2,128,128]{3,2,1,0:T(8,128)(2,1)} %copy.30), calls=%async_computation | async-start | bytes 1048576 | tf_op jit(solution)/shard_map/all_to_all | solution.py:74
  116.7 0.2 reduce-scatter.3.cloned.1.call-start
  117.0 0.1 copy.24
  117.1 0.1 select_n.36
  117.1 1.7 gather_fusion.7
  118.8 1.7 gather_fusion.6
  120.5 2.2 gather_fusion.5
  122.7 2.1 gather_fusion
  124.9 2.0 broadcast_select_fusion
  126.9 0.2 copy-done.5
  127.1 1.6 broadcast_select_fusion.3
  128.7 3.4 %all-to-all-done = bf16[8,2,128,128]{3,2,1,0:T(8,128)(2,1)} async-done(((bf16[8,2,128,128]{3,2,1,0:T(8,128)(2,1)}), bf16[8,2,128,128]{3,2,1,0:T(8,128)(2,1)}, u32[]{:S(2)}, u32[]{:S(2)}) %all-to-all-start) | async-done | bytes 524320 | tf_op jit(solution)/shard_map/all_to_all | solution.py:74
  132.1 46.9 %while.10 = (s32[]{:T(128)}, f32[8,512,512]{2,1,0:T(8,128)}, s32[2,8]{1,0:T(2,128)S(1)}, bf16[2,8,512,128]{3,2,1,0:T(8,128)(2,1)}, bf16[2,8,128,128]{3,2,1,0:T(8...) while((s32[]{:T(128)}, f32[8,512,512]{2,1,0:T(8,128)}, s32[2,8]{1,0:T(2,128)S(1)}, ...), condition=%wide.region_9.12_spmd, body=%wide.region_7.11_spmd.sunk | while | flops 673710080 | bytes 35915440 | solution.py:110
  132.1 6.0 %fusion.88 = f32[8,512,512]{2,1,0:T(8,128)} fusion(bf16[2,8,512,128]{3,2,1,0:T(8,128)(2,1)S(1)} %get-tuple-element.136, s32[]{:T(128)} %get-tuple-element.124, bf16[2,8,512,128]{3,2,1,0:T(8,128)(2,1)} %get-tuple-element.134, bf16[2,8,128,128]{3,2,1,0:T(8,128)(2,1)} %get-tuple-element.135), kind=kOutput, calls=%fused_computation.12.clone.1 | convolution fusion | flops 671612928 | bytes 10749440 | tf_op jit(solution)/shard_map/while/body/eval_jaxpr/gxs,gys->gxy/dot_general | solution.py:105
  138.1 17.5 %scatter_fusion = f32[8,512,512]{2,1,0:T(8,128)} fusion(f32[8,512,512]{2,1,0:T(8,128)} %get-tuple-element.125, s32[8]{0:T(128)S(1)} %fusion.87, f32[8,512,512]{2,1,0:T(8,128)} %fusion.88), kind=kCustom, calls=%fused_computation.8.clone.1 | custom fusion | flops 2097152 | bytes 25165856 | tf_op jit(solution)/shard_map/while/body/eval_jaxpr/scatter-add | solution.py:108
  155.5 6.0 %fusion.88 = f32[8,512,512]{2,1,0:T(8,128)} fusion(bf16[2,8,512,128]{3,2,1,0:T(8,128)(2,1)S(1)} %get-tuple-element.136, s32[]{:T(128)} %get-tuple-element.124, bf16[2,8,512,128]{3,2,1,0:T(8,128)(2,1)} %get-tuple-element.134, bf16[2,8,128,128]{3,2,1,0:T(8,128)(2,1)} %get-tuple-element.135), kind=kOutput, calls=%fused_computation.12.clone.1 | convolution fusion | flops 671612928 | bytes 10749440 | tf_op jit(solution)/shard_map/while/body/eval_jaxpr/gxs,gys->gxy/dot_general | solution.py:105
  161.5 17.4 %scatter_fusion = f32[8,512,512]{2,1,0:T(8,128)} fusion(f32[8,512,512]{2,1,0:T(8,128)} %get-tuple-element.125, s32[8]{0:T(128)S(1)} %fusion.87, f32[8,512,512]{2,1,0:T(8,128)} %fusion.88), kind=kCustom, calls=%fused_computation.8.clone.1 | custom fusion | flops 2097152 | bytes 25165856 | tf_op jit(solution)/shard_map/while/body/eval_jaxpr/scatter-add | solution.py:108
  178.9 6.4 %fusion.52 = f32[8,512,128]{2,1,0:T(8,128)} fusion(bf16[8,512,128]{2,1,0:T(8,128)(2,1)} %gather_fusion.6, pred[8]{0:T(512)(128)(4,1)S(1)} %get-tuple-element.66, f32[8,512,512]{2,1,0:T(8,128)} %get-tuple-element.37), kind=kOutput, calls=%fused_computation.47 | convolution fusion | flops 539492352 | bytes 11534344 | tf_op jit(solution)/shard_map/pxy,pyk->pxk/dot_general | solution.py:120
  185.4 0.5 copy-done.6
  185.9 3.0 %convolution_multiply_fusion = f32[8,512,128]{2,1,0:T(8,128)} fusion(bf16[8,512,128]{2,1,0:T(8,128)(2,1)S(1)} %copy-done.6, f32[8]{0:T(128)S(1)} %get-tuple-element.65, pred[8]{0:T(512)(128)(4,1)S(1)} %get-tuple-element.56, f32[8,512,512]{2,1,0:T(8,128)S(1)} %copy-done.2), kind=kOutput, calls=%fused_computation.42 | convolution fusion | flops 540016640 | bytes 11534376 | tf_op jit(solution)/shard_map/pyx,pyk->pxk/dot_general | solution.py:126
  188.8 0.1 broadcast.99.clone.1
  189.0 3.3 %scatter_fusion.2 = f32[8,512,128]{2,1,0:T(8,128)S(1)} fusion(f32[8,512,128]{2,1,0:T(8,128)S(1)} %broadcast.99.clone.1, s32[8]{0:T(128)S(1)} %get-tuple-element.68, f32[8,512,128]{2,1,0:T(8,128)} %convolution_multiply_fusion), kind=kCustom, calls=%fused_computation.10 | custom fusion | flops 524288 | bytes 6291488 | tf_op jit(solution)/shard_map/scatter-add | solution.py:135
  192.3 1.4 copy-done.4
  193.7 0.1 broadcast.99.clone
  193.9 3.4 %scatter_fusion.1 = f32[8,512,128]{2,1,0:T(8,128)S(1)} fusion(f32[8,512,128]{2,1,0:T(8,128)S(1)} %broadcast.99.clone, s32[8]{0:T(128)S(1)} %get-tuple-element.69, f32[8,512,128]{2,1,0:T(8,128)} %fusion.52), kind=kCustom, calls=%fused_computation.9 | custom fusion | flops 524288 | bytes 6291488 | tf_op jit(solution)/shard_map/scatter-add | solution.py:133
  197.2 3.1 %add.36 = f32[8,512,128]{2,1,0:T(8,128)} add(f32[8,512,128]{2,1,0:T(8,128)S(1)} %scatter_fusion.1, f32[8,512,128]{2,1,0:T(8,128)} %copy-done.4) | non-fusion elementwise | flops 524288 | bytes 6291456 | tf_op jit(solution)/shard_map/add | solution.py:133
  200.4 0.0 reduce-scatter.5.cloned.1.call-start
  200.4 33.6 %reduce-scatter.3.cloned.1.call-done = f32[1024,128]{1,0:T(8,128)} async-done(((f32[4096,128]{1,0:T(8,128)}), f32[1024,128]{1,0:T(8,128)}) %reduce-scatter.3.cloned.1.call-update) | async-done | bytes 524304 | tf_op jit(solution)/shard_map/reduce_scatter | solution.py:137
  234.1 6.0 %convert_bitcast_fusion = bf16[1,8,512,512]{3,2,1,0:T(8,128)(2,1)} fusion(f32[8,512,512]{2,1,0:T(8,128)} %get-tuple-element.37), kind=kLoop, calls=%fused_computation.106 | loop fusion | flops 2097152 | bytes 12582912 | tf_op jit(solution)/shard_map/broadcast_in_dim | solution.py:139
  240.1 27.9 %reduce-scatter.5.cloned.1.call-done = f32[128,128]{1,0:T(8,128)} async-done(((f32[1024,128]{1,0:T(8,128)}), f32[128,128]{1,0:T(8,128)}) %reduce-scatter.5.cloned.1.call-update) | async-done | bytes 65552 | tf_op jit(solution)/shard_map/reduce_scatter | solution.py:138
  (32 shorter events, 0.2 us)
Async XLA Ops:
  7.2 110.0 %copy-start = (bf16[4096,128]{1,0:T(8,128)(2,1)S(1)}, bf16[4096,128]{1,0:T(8,128)(2,1)}, u32[]{:S(2)}) copy-start(bf16[4096,128]{1,0:T(8,128)(2,1)} %param.25) | copy-start | bytes 3145732
  7.2 27.4 %all-gather.5.cloned.1.call-start = ((), (), s32[]{:S(2)}) async-start(), calls=%async_computation.5 | async-start | bytes 1179648 | tf_op jit(solution)/shard_map/all_gather | solution.py:36
  7.9 74.8 %all-gather.7.cloned.1.call-start = ((), (), s32[]{:S(2)}) async-start(), calls=%async_computation.6 | async-start | bytes 4718592 | tf_op jit(solution)/shard_map/all_gather | solution.py:35
  34.6 3.5 %copy-start.3 = (bf16[1,4096,128]{2,1,0:T(8,128)(2,1)S(1)}, bf16[1,4096,128]{2,1,0:T(8,128)(2,1)}, u32[]{:S(2)}) copy-start(bf16[1,4096,128]{2,1,0:T(8,128)(2,1)} %all-gather.5.cloned.1.call-done) | copy-start | bytes 3145732
  112.6 19.5 %all-to-all-start = ((bf16[8,2,128,128]{3,2,1,0:T(8,128)(2,1)}), bf16[8,2,128,128]{3,2,1,0:T(8,128)(2,1)}, u32[]{:S(2)}, u32[]{:S(2)}) async-start(bf16[8,2,128,128]{3,2,1,0:T(8,128)(2,1)} %copy.30), calls=%async_computation | async-start | bytes 1048576 | tf_op jit(solution)/shard_map/all_to_all | solution.py:74
  116.7 117.3 %reduce-scatter.3.cloned.1.call-start = ((), (), s32[]{:S(2)}) async-start(), calls=%async_computation.3 | async-start | bytes 2621440 | tf_op jit(solution)/shard_map/reduce_scatter | solution.py:137
  117.1 3.4 %copy-start.7 = (s32[1,8,2]{1,2,0:T(2,128)S(1)}, s32[1,8,2]{1,2,0:T(2,128)}, u32[]{:S(2)}) copy-start(s32[1,8,2]{1,2,0:T(2,128)} %param.24) | copy-start | bytes 196
  124.9 2.2 copy-start.5
  178.9 6.4 %copy-start.2 = (f32[8,512,512]{2,1,0:T(8,128)S(1)}, f32[8,512,512]{2,1,0:T(8,128)}, u32[]{:S(2)}) copy-start(f32[8,512,512]{2,1,0:T(8,128)} %get-tuple-element.37) | copy-start | bytes 25165828
  178.9 6.9 %copy-start.6 = (bf16[8,512,128]{2,1,0:T(8,128)(2,1)S(1)}, bf16[8,512,128]{2,1,0:T(8,128)(2,1)}, u32[]{:S(2)}) copy-start(bf16[8,512,128]{2,1,0:T(8,128)(2,1)} %gather_fusion.7) | copy-start | bytes 3145732
  192.3 1.4 copy-start.4
  200.4 67.6 %reduce-scatter.5.cloned.1.call-start = ((), (), s32[]{:S(2)}) async-start(), calls=%async_computation.4 | async-start | bytes 589824 | tf_op jit(solution)/shard_map/reduce_scatter | solution.py:138
  234.1 33.9 %copy-start.1 = (bf16[4096,128]{1,0:T(8,128)(2,1)S(1)}, bf16[4096,128]{1,0:T(8,128)(2,1)}, u32[]{:S(2)}) copy-start(bf16[4096,128]{1,0:T(8,128)(2,1)} %param.25) | copy-start | bytes 3145732
Sparse Core Ops, SparseCore 0:
  9.6 24.9 all-gather.4
  36.2 46.4 all-gather.6
  200.5 33.5 reduce-scatter.2
  236.7 31.1 reduce-scatter.4
where the time goes:
time: 275 us; the launch traced here: 274 us
  waiting for transfers between devices  113 us (41%)
  other arithmetic  65.1 us (24%)
  matrix products  45 us (16%)
  local copies, waits for them, and re-layouts  33.5 us (12%)
  between operations  13.9 us (5%)
  starting transfers between devices  4.48 us (2%)
    scatter-add x2, other arithmetic, decode(): jax.ops.segment_sum(decoded, slot_group, num_segments=parent_count)  34.9 us
    all_gather x1, waiting for transfers between devices, shards(): lax.all_gather(panel[0], 'tile', axis=0, tiled=True)  33.9 us
    reduce_scatter x1, waiting for transfers between devices, shards(): lax.psum_scatter(partial_sketch, 'child', scatter_dimension=0, tiled=True)  33.6 us
    reduce_scatter x1, waiting for transfers between devices, shards(): lax.psum_scatter(by_child, 'tile', scatter_dimension=0, tiled=True)  27.9 us
    all_gather x1, waiting for transfers between devices, shards(): lax.all_gather(bases[0], 'tile', axis=0, tiled=True)  12.4 us
    dot_general x2, matrix products, decode(): jnp.einsum('gxs,gys->gxy', left_part, right_group, preferred_element_type...  12 us
    dot_general x1, matrix products, shards(): jnp.einsum('qry,qys->qrs', half, right_basis, preferred_element_type=jnp....  8.63 us
    dot_general x1, matrix products, shards(): jnp.einsum('qxr,qxy->qry', right_basis, jnp.take(panel_blocks, col_ids, a...  7.35 us
  transfers between devices with their start and end apart: 5, of which 5 were waited for; matrix products, arithmetic and copies ran while one was open for 16% of the time, Pallas kernels for 0%

commit v1 on v0

v1 whole, which is shorter than its diff:
```python
import functools

import jax
import jax.numpy as jnp
from jax import lax
from jax.experimental import pallas as pl
from jax.experimental.pallas import tpu as pltpu
from jax.sharding import PartitionSpec as P

CAP = 2
LINE_OWNERS = 8
VMEM_BYTES = 60 * 1024 * 1024
F32 = jnp.float32
BF16 = jnp.bfloat16
NT = (((1,), (1,)), ((), ()))


def dot(x, y):
    return jnp.dot(x, y, preferred_element_type=F32)


def params():
    return pltpu.CompilerParams(
        dimension_semantics=("arbitrary",), vmem_limit_bytes=VMEM_BYTES
    )


def project_kernel(panel_ref, basis_ref, out_ref):
    rank = basis_ref.shape[2]
    flipped = basis_ref[0].T
    out_ref[0, :rank] = flipped
    out_ref[0, rank:] = dot(flipped, panel_ref[0]).astype(BF16)


def project(panel, bases, order):
    blocks = panel.shape[0] // order
    width, rank = panel.shape[1], bases.shape[1]
    return pl.pallas_call(
        project_kernel,
        grid=(blocks,),
        in_specs=[
            pl.BlockSpec((1, order, width), lambda b: (b, 0, 0)),
            pl.BlockSpec((1, order, rank), lambda b: (b, 0, 0)),
        ],
        out_specs=pl.BlockSpec((1, 2 * rank, order), lambda b: (b, 0, 0)),
        out_shape=jax.ShapeDtypeStruct((blocks, 2 * rank, order), BF16),
        compiler_params=params(),
        name="project",
    )(panel.reshape(blocks, order, width), bases.reshape(blocks, order, rank))


def along_chips(x, owners, shift):
    pairs = [(t, t + 2 * shift) for t in range(owners) if 0 <= t + 2 * shift < owners]
    return lax.ppermute(x, "tile", pairs)


def to_partner(x, owners):
    return lax.ppermute(x, "tile", [(t, t ^ 1) for t in range(owners)])


def spread(block, owners):
    if owners > LINE_OWNERS or owners % 2:
        return [lax.all_gather(block, "tile", axis=0, tiled=True)], None
    arrays, offsets = [block], [0]
    up, down = block, block
    for step in range(1, owners // 2):
        up, down = along_chips(up, owners, 1), along_chips(down, owners, -1)
        arrays += [up, down]
        offsets += [-step, step]
    return arrays + [to_partner(x, owners) for x in arrays], offsets


def encode_kernel(offsets, rows, cols, places, tile_ref, *refs):
    parts, (core_ref, flip_ref, held, sems, out_sem) = refs[:-5], refs[-5:]
    rank = core_ref.shape[1]
    step = pl.program_id(0)
    out_copy = pltpu.make_async_copy(held.at[:, :rank], flip_ref, out_sem)

    def each(act):
        if offsets is None:
            act(pltpu.make_async_copy(parts[0], held, sems.at[0]))
            return
        local = parts[0].shape[0]
        me = lax.axis_index("tile")
        chips = lax.axis_size("tile") // 2
        chip, core = me // 2, me % 2
        count = len(offsets)
        for n, part in enumerate(parts):
            source = chip + offsets[n % count]
            owner = source * 2 + (core if n < count else 1 - core)

            @pl.when((source >= 0) & (source < chips))
            def _():
                act(
                    pltpu.make_async_copy(
                        part, held.at[pl.ds(owner * local, local)], sems.at[n]
                    )
                )

    @pl.when(step == 0)
    def _():
        each(lambda copy: copy.start())
        if core_ref.shape[0] != pl.num_programs(0):
            core_ref[...] = jnp.zeros_like(core_ref)
        each(lambda copy: copy.wait())
        out_copy.start()

    row, col = rows[step], cols[step]
    half = dot(held[row, :rank], tile_ref[0]).astype(BF16)
    encoded = lax.dot_general(half, held[col, :rank], NT, preferred_element_type=F32)
    cross = lax.dot_general(
        held[row, rank:], held[col, rank:], NT, preferred_element_type=F32
    )
    core_ref[places[step]] = (encoded - cross).astype(BF16)

    @pl.when(step == pl.num_programs(0) - 1)
    def _():
        out_copy.wait()


def encode(tiles, parts, offsets, rows, cols, places, owners):
    count, order, _ = tiles.shape
    rank = parts[0].shape[1] // 2
    blocks = parts[0].shape[0] * (1 if offsets is None else owners)
    slots = owners * CAP
    return pl.pallas_call(
        functools.partial(encode_kernel, offsets),
        grid_spec=pltpu.PrefetchScalarGridSpec(
            num_scalar_prefetch=3,
            grid=(count,),
            in_specs=[pl.BlockSpec((1, order, order), lambda q, *_: (q, 0, 0))]
            + [pl.BlockSpec(memory_space=pl.ANY)] * len(parts),
            out_specs=[
                pl.BlockSpec((slots, rank, rank), lambda q, *_: (0, 0, 0)),
                pl.BlockSpec(memory_space=pl.ANY),
            ],
            scratch_shapes=[
                pltpu.VMEM((blocks, 2 * rank, order), BF16),
                pltpu.SemaphoreType.DMA((len(parts),)),
                pltpu.SemaphoreType.DMA,
            ],
        ),
        out_shape=[
            jax.ShapeDtypeStruct((slots, rank, rank), BF16),
            jax.ShapeDtypeStruct((blocks, rank, order), BF16),
        ],
        compiler_params=params(),
        name="encode",
    )(rows, cols, places, tiles, *parts)


def flip_kernel(x_ref, out_ref):
    out_ref[0] = x_ref[0].T


def flip(x, name):
    blocks, rows, cols = x.shape
    return pl.pallas_call(
        flip_kernel,
        grid=(blocks,),
        in_specs=[pl.BlockSpec((1, rows, cols), lambda b: (b, 0, 0))],
        out_specs=pl.BlockSpec((1, cols, rows), lambda b: (b, 0, 0)),
        out_shape=jax.ShapeDtypeStruct((blocks, cols, rows), x.dtype),
        compiler_params=params(),
        name=name,
    )(x)


def decode_kernel(
    rows, cols, slots, prows, pcols,
    parent_ref, core_ref, basis_ref, flip_ref, test_ref,
    updated_ref, keep_ref, send_ref, total, sketch,
):
    p = pl.program_id(0)
    rank = core_ref.shape[1]
    lanes = sketch.shape[2]
    pieces = parent_ref.shape[1] // lanes

    @pl.when(p == 0)
    def _():
        sketch[...] = jnp.zeros_like(sketch)

    total[...] = parent_ref[0].astype(F32)

    def item(s, carry):
        @pl.when(slots[s] == p)
        def _():
            left = dot(basis_ref[rows[s]], core_ref[s]).astype(BF16)
            total[...] += dot(left, flip_ref[cols[s]])

        return carry

    lax.fori_loop(0, core_ref.shape[0], item, 0)
    tile = total[...].astype(BF16)
    updated_ref[0] = tile
    prow, pcol = prows[p], pcols[p]

    def add(block, value):
        for r in range(pieces):
            sketch[block * pieces + r] += value[:, r * lanes : (r + 1) * lanes]

    add(prow, lax.dot_general(test_ref[pcol], tile, NT, preferred_element_type=F32))

    @pl.when(prow != pcol)
    def _():
        add(pcol, dot(test_ref[prow], tile))

    @pl.when(p == pl.num_programs(0) - 1)
    def _():
        core = lax.axis_index("tile") % 2
        for n in range(keep_ref.shape[0]):
            keep_ref[n] = sketch[2 * n + core].astype(BF16)
            send_ref[n] = sketch[2 * n + 1 - core].astype(BF16)


def decode(parents, cores, basis, flipped, test, rows, cols, slots, prows, pcols, lanes):
    count, order, _ = parents.shape
    width = test.shape[1]
    chunks = test.shape[0] * test.shape[2] // lanes

    def whole(x):
        return pl.BlockSpec(x.shape, lambda p, *_: (0, 0, 0))

    half = jax.ShapeDtypeStruct((chunks // 2, width, lanes), BF16)
    tile_spec = pl.BlockSpec((1, order, order), lambda p, *_: (p, 0, 0))
    return pl.pallas_call(
        decode_kernel,
        grid_spec=pltpu.PrefetchScalarGridSpec(
            num_scalar_prefetch=5,
            grid=(count,),
            in_specs=[tile_spec, whole(cores), whole(basis), whole(flipped), whole(test)],
            out_specs=[tile_spec, whole(half), whole(half)],
            scratch_shapes=[
                pltpu.VMEM((order, order), F32),
                pltpu.VMEM((chunks, width, lanes), F32),
            ],
        ),
        out_shape=[jax.ShapeDtypeStruct(parents.shape, BF16), half, half],
        compiler_params=params(),
        name="decode",
    )(rows, cols, slots, prows, pcols, parents, cores, basis, flipped, test)


def exchange_sum(pieces, axis, size, me, send, group):
    mine = lax.dynamic_slice_in_dim(pieces, me * group, group, 0)
    for shift in range(1, size):
        peer = (me + shift) % size
        out = lax.dynamic_slice_in_dim(pieces, peer * group, group, 0).astype(BF16)
        mine = mine + send(out, shift).astype(F32)
    return mine


def reduce_sketch(keep, sent, owners, children):
    child, tile = lax.axis_index("child"), lax.axis_index("tile")
    chips = owners // 2
    pieces = keep.astype(F32) + to_partner(sent, owners).astype(F32)

    def over_child(x, shift):
        return lax.ppermute(
            x, "child", [(i, (i + shift) % children) for i in range(children)]
        )

    def over_chips(x, shift):
        return lax.ppermute(
            x, "tile", [(t, (t + 2 * shift) % owners) for t in range(owners)]
        )

    pieces = exchange_sum(pieces, "child", children, child, over_child, chips)
    return exchange_sum(pieces, "tile", chips, tile // 2, over_chips, 1)[0]


def shards(
    child_tiles,
    panel,
    bases,
    tile_blocks,
    tile_dest,
    tile_slot,
    parent_tiles,
    parent_blocks,
    sketch_test,
):
    owners, children = lax.axis_size("tile"), lax.axis_size("child")
    myself = lax.axis_index("tile")
    tile_count, order = child_tiles.shape[1], child_tiles.shape[2]
    parent_count = parent_tiles.shape[1]

    block = project(panel[0], bases[0], order)
    parts, offsets = spread(block, owners)

    blocks_all = tile_blocks[0]
    own_blocks = lax.dynamic_slice_in_dim(blocks_all, myself * tile_count, tile_count, 0)
    dest_all = tile_dest[0, :, 0].reshape(owners, tile_count)
    own_dest = lax.dynamic_index_in_dim(dest_all, myself, 0, keepdims=False)
    ids = jnp.arange(tile_count, dtype=jnp.int32)
    before = (own_dest[:, None] == own_dest[None, :]) & (ids[None, :] < ids[:, None])
    places = own_dest * CAP + jnp.sum(before.astype(jnp.int32), axis=1)

    arrive = (dest_all == myself).astype(jnp.int32)
    earlier = jnp.sum(
        arrive[:, None, :] * (ids[None, None, :] < ids[None, :, None]).astype(jnp.int32), axis=2
    )
    turn = jnp.arange(CAP, dtype=jnp.int32)
    matched = arrive[:, None, :] * (earlier[:, None, :] == turn[None, :, None]).astype(jnp.int32)

    def received(values):
        return jnp.sum(matched * values.reshape(owners, 1, tile_count), axis=2).reshape(-1)

    live = jnp.sum(matched, axis=2).reshape(-1)
    recv_rows = received(blocks_all[:, 0])
    recv_cols = received(blocks_all[:, 1])
    recv_slots = jnp.where(live > 0, received(tile_slot[0]), parent_count)

    cores, flipped = encode(
        child_tiles[0], parts, offsets, own_blocks[:, 0], own_blocks[:, 1], places, owners
    )
    rank = cores.shape[1]
    incoming = lax.all_to_all(
        cores.reshape(owners, CAP, rank, rank), "tile", split_axis=0, concat_axis=0, tiled=True
    ).reshape(cores.shape)
    basis = flip(flipped, "flip_basis")
    width = sketch_test.shape[1]
    test = flip(sketch_test.reshape(-1, order, width), "flip_test")
    lanes = sketch_test.shape[0] // (owners * children)
    updated, keep, sent = decode(
        parent_tiles[0], incoming, basis, flipped, test,
        recv_rows, recv_cols, recv_slots,
        parent_blocks[0, :, 0], parent_blocks[0, :, 1], lanes,
    )
    sketch = reduce_sketch(keep, sent, owners, children)
    return updated[None], sketch.T


def solution(mesh):
    return jax.shard_map(
        shards,
        mesh=mesh,
        in_specs=(
            P("child", "tile", None, None),
            P("child", "tile", None),
            P("child", "tile", None),
            P("child", None, None),
            P("child", None, None),
            P("child", None),
            P("child", "tile", None, None),
            P("child", "tile", None),
            P(),
        ),
        out_specs=(P("child", "tile", None, None), P(("child", "tile"), None)),
        check_vma=False,
    )
```

time: 275 us -> 114 us (0.41)
  waiting for transfers between devices: 113 us -> 22.9 us
  other arithmetic: 65.1 us -> 4.47 us
  Pallas kernels: 0 us -> 45.6 us
  matrix products: 45 us -> 0 us
  starting transfers between devices: 4.48 us -> 32.1 us
  local copies, waits for them, and re-layouts: 33.5 us -> 7.14 us
  between operations: 13.9 us -> 0.92 us
    reduce_scatter x2 -> x0, waiting for transfers between devices: 61.5 us -> none  [the longest x1 33.6 us: shards(): lax.psum_scatter(partial_sketch, 'child', scatter_dimension=0, tiled=True)]
    all_gather x2 -> x0, waiting for transfers between devices: 46.3 us -> none  [the longest x1 33.9 us: shards(): lax.all_gather(panel[0], 'tile', axis=0, tiled=True)]
    pallas_call x0 -> x5, Pallas kernels: none -> 45.6 us  [the longest x1 17.2 us: decode(): pl.pallas_call(decode_kernel, grid_spec=pltpu.PrefetchScalarGridSpec(num_...]
    dot_general x8 -> x0, matrix products: 45 us -> none  [the longest x2 12 us: decode(): jnp.einsum('gxs,gys->gxy', left_part, right_group, preferred_element_type...]
    scatter-add x4 -> x0, other arithmetic: 41.6 us -> none  [the longest x2 34.9 us: decode(): jax.ops.segment_sum(decoded, slot_group, num_segments=parent_count)]
    ppermute x0 -> x20, starting transfers between devices: none -> 28.2 us  [the longest x6 17.5 us: along_chips(): return lax.ppermute(x, 'tile', pairs)]
    gather x8 -> x0, local copies, waits for them, and re-layouts: 27.2 us -> none  [the longest x1 6.95 us: shards(): jnp.take(panel_blocks, col_ids, axis=0)]
    ppermute x0 -> x20, waiting for transfers between devices: none -> 22.5 us  [the longest x6 12.1 us: along_chips(): return lax.ppermute(x, 'tile', pairs)]
  transfers between devices with their start and end apart: 5 -> 21, of which waited for: 5 -> 12; matrix products, arithmetic and copies ran while one was open for 16% -> 7% of each run, Pallas kernels for 0% -> 10%
where the time goes in v1:
time: 114 us; the launch traced here: 113 us
  Pallas kernels  45.6 us (40%)
  starting transfers between devices  32.1 us (28%)
  waiting for transfers between devices  22.9 us (20%)
  local copies, waits for them, and re-layouts  7.14 us (6%)
  other arithmetic  4.47 us (4%)
    ppermute x6, starting transfers between devices, along_chips(): return lax.ppermute(x, 'tile', pairs)  17.5 us
    pallas_call x1, Pallas kernels, decode(): pl.pallas_call(decode_kernel, grid_spec=pltpu.PrefetchScalarGridSpec(num_...  17.2 us
    pallas_call x1, Pallas kernels, encode(): pl.pallas_call(functools.partial(encode_kernel, offsets), grid_spec=pltpu...  15.5 us
    ppermute x6, waiting for transfers between devices, along_chips(): return lax.ppermute(x, 'tile', pairs)  12.1 us
    pallas_call x2, Pallas kernels, flip(): pl.pallas_call(flip_kernel, grid=(blocks,), in_specs=[pl.BlockSpec((1, ro...  10.9 us
    ppermute x3, waiting for transfers between devices, over_child(): lax.ppermute(x, 'child', [(i, (i + shift) % children) for i in range(chil...  5.47 us
    ppermute x3, starting transfers between devices, over_chips(): lax.ppermute(x, 'tile', [(t, (t + 2 * shift) % owners) for t in range(own...  4.67 us
    ppermute x3, starting transfers between devices, over_child(): lax.ppermute(x, 'child', [(i, (i + shift) % children) for i in range(chil...  4.65 us
  transfers between devices with their start and end apart: 21, of which 12 were waited for; matrix products, arithmetic and copies ran while one was open for 7% of the time, Pallas kernels for 10%

profile of v1, /device:TPU:0, one launch (start us, length us, event | category | flops | bytes accessed | tf_op | source)
XLA Modules:
  0.0 113.2 jit_solution(9036719686587832943)
XLA Ops:
  0.6 2.0 %project.1.refs_0_ = bf16[1,256,512]{2,1,0:T(8,128)(2,1)} custom-call(bf16[1,512,512]{2,1,0:T(8,128)(2,1)} %panel_ref.1, bf16[1,512,128]{2,1,0:T(8,128)(2,1)} %basis_ref.1), custom_call_target="tpu_custom_call" | custom-call | tf_op jit(solution)/shard_map/project/pallas_call | solution.py:38
  2.7 5.0 %collective-permute-start = (bf16[1,256,512]{2,1,0:T(8,128)(2,1)}, bf16[1,256,512]{2,1,0:T(8,128)(2,1)S(1)}, u32[]{:S(2)}, u32[]{:S(2)}) collective-permute-start(bf16[1,256,512]{2,1,0:T(8,128)(2,1)} %project.1.refs_0_), channel_id=1, source_target_pairs={{0,2},{1,3},{2,4},{3,5},{4,6},{5,7},{8,10},{9,11},{10,12},{11,13},... | collective-permute-start | bytes 786440 | tf_op jit(solution)/shard_map/ppermute | solution.py:54
  7.6 1.3 %collective-permute-start.1 = (bf16[1,256,512]{2,1,0:T(8,128)(2,1)}, bf16[1,256,512]{2,1,0:T(8,128)(2,1)S(1)}, u32[]{:S(2)}, u32[]{:S(2)}) collective-permute-start(bf16[1,256,512]{2,1,0:T(8,128)(2,1)} %project.1.refs_0_), channel_id=1, source_target_pairs={{2,0},{3,1},{4,2},{5,3},{6,4},{7,5},{10,8},{11,9},{12,10},{13,11},... | collective-permute-start | bytes 786440 | tf_op jit(solution)/shard_map/ppermute | solution.py:54
  8.9 4.5 %collective-permute-done.refs_1_ = bf16[1,256,512]{2,1,0:T(8,128)(2,1)S(1)} collective-permute-done((bf16[1,256,512]{2,1,0:T(8,128)(2,1)}, bf16[1,256,512]{2,1,0:T(8,128)(2,1)S(1)}, u32[]{:S(2)}, u32[]{:S(2)}) %collective-permute-start) | collective-permute-done | bytes 262176 | tf_op jit(solution)/shard_map/ppermute | solution.py:54
  13.5 4.3 %collective-permute-start.2 = (bf16[1,256,512]{2,1,0:T(8,128)(2,1)S(1)}, bf16[1,256,512]{2,1,0:T(8,128)(2,1)S(1)}, u32[]{:S(2)}, u32[]{:S(2)}) collective-permute-start(bf16[1,256,512]{2,1,0:T(8,128)(2,1)S(1)} %collective-permute-done.refs_1_), channel_id=1, source_target_pairs={{0,2},{1,3},{2,4},{3,5},{4,6},{5,7},{8,10},{9,11},{10,12},{11,13},... | collective-permute-start | bytes 786440 | tf_op jit(solution)/shard_map/ppermute | solution.py:54
  17.8 1.3 %collective-permute-start.3 = (bf16[1,256,512]{2,1,0:T(8,128)(2,1)S(1)}, bf16[1,256,512]{2,1,0:T(8,128)(2,1)S(1)}, u32[]{:S(2)}, u32[]{:S(2)}) collective-permute-start(bf16[1,256,512]{2,1,0:T(8,128)(2,1)S(1)} %collective-permute-done.1.refs_2_), channel_id=1, source_target_pairs={{2,0},{3,1},{4,2},{5,3},{6,4},{7,5},{10,8},{11,9},{12,10},{13,11},... | collective-permute-start | bytes 786440 | tf_op jit(solution)/shard_map/ppermute | solution.py:54
  19.1 0.1 collective-permute-start.6
  19.2 0.5 broadcast.55
  19.7 1.3 %reduce.14 = s32[128]{0:T(128)S(1)} reduce(s32[1,128,1]{1,2,0:T(1,128)} %param.13, s32[]{:T(128)} %broadcast.55), dimensions={0,2}, to_apply=%param.13.reduce_sub_computation.3 | reduce | bytes 1028 | tf_op args[4]
  21.0 0.1 reshape_squeeze.2
  21.1 0.2 convert_reduce_fusion
  21.3 0.6 collective-permute-start.7
  21.8 0.6 collective-permute-done.2.refs_3_
  22.5 4.4 %collective-permute-start.4 = (bf16[1,256,512]{2,1,0:T(8,128)(2,1)S(1)}, bf16[1,256,512]{2,1,0:T(8,128)(2,1)S(1)}, u32[]{:S(2)}, u32[]{:S(2)}) collective-permute-start(bf16[1,256,512]{2,1,0:T(8,128)(2,1)S(1)} %collective-permute-done.2.refs_3_), channel_id=1, source_target_pairs={{0,2},{1,3},{2,4},{3,5},{4,6},{5,7},{8,10},{9,11},{10,12},{11,13},... | collective-permute-start | bytes 786440 | tf_op jit(solution)/shard_map/ppermute | solution.py:54
  26.9 1.3 %collective-permute-start.5 = (bf16[1,256,512]{2,1,0:T(8,128)(2,1)S(1)}, bf16[1,256,512]{2,1,0:T(8,128)(2,1)S(1)}, u32[]{:S(2)}, u32[]{:S(2)}) collective-permute-start(bf16[1,256,512]{2,1,0:T(8,128)(2,1)S(1)} %collective-permute-done.3.refs_4_), channel_id=1, source_target_pairs={{2,0},{3,1},{4,2},{5,3},{6,4},{7,5},{10,8},{11,9},{12,10},{13,11},... | collective-permute-start | bytes 786440 | tf_op jit(solution)/shard_map/ppermute | solution.py:54
  28.2 0.6 multiply_add_fusion.places
  28.8 0.5 collective-permute-start.10
  29.3 0.1 collective-permute-start.9
  29.4 2.7 %collective-permute-done.4.refs_5_ = bf16[1,256,512]{2,1,0:T(8,128)(2,1)S(1)} collective-permute-done((bf16[1,256,512]{2,1,0:T(8,128)(2,1)S(1)}, bf16[1,256,512]{2,1,0:T(8,128)(2,1)S(1)}, u32[]{:S(2)}, u32[]{:S(2)}) %collective-permute-start.4) | collective-permute-done | bytes 262176 | tf_op jit(solution)/shard_map/ppermute | solution.py:54
  32.1 4.1 %collective-permute-done.5.refs_6_ = bf16[1,256,512]{2,1,0:T(8,128)(2,1)S(1)} collective-permute-done((bf16[1,256,512]{2,1,0:T(8,128)(2,1)S(1)}, bf16[1,256,512]{2,1,0:T(8,128)(2,1)S(1)}, u32[]{:S(2)}, u32[]{:S(2)}) %collective-permute-start.5) | collective-permute-done | bytes 262176 | tf_op jit(solution)/shard_map/ppermute | solution.py:54
  36.3 0.8 fusion.5
  37.0 0.5 slice_bitcast_fusion
  37.6 0.2 collective-permute-done.12.refs_13_
  37.9 0.4 copy-done.9
  38.3 0.1 copy-done.10
  38.4 0.1 copy-done.11
  38.5 0.1 copy-done.12
  38.5 0.1 copy-done.13
  38.6 15.5 %encode.1 = (bf16[16,128,128]{2,1,0:T(8,128)(2,1)}, bf16[8,128,512]{2,1,0:T(8,128)(2,1)}) custom-call(s32[16]{0:T(128)} %get-tuple-element.31.rows, s32[16]{0:T(128)} %get-tuple-element.30.cols, s32[16]{0:T(128)} %multiply_add_fusion.places, bf16[16,512,512]{2,1,0:T(8,128)(2,1)} %bitcast.26, bf16[1,256,512]{2,1,0:T(8,128)(2,1)} %project.1.refs_0_, ...), custom_call_target="tpu_custom_call" | custom-call | tf_op jit(solution)/shard_map/encode/pallas_call | solution.py:126
  54.1 4.0 %all-to-all-start = ((bf16[8,2,128,128]{3,2,1,0:T(8,128)(2,1)}), bf16[8,2,128,128]{3,2,1,0:T(8,128)(2,1)S(1)}, u32[]{:S(2)}, u32[]{:S(2)}) async-start(bf16[8,2,128,128]{3,2,1,0:T(8,128)(2,1)} %bitcast.30), calls=%async_computation | async-start | bytes 1048576 | tf_op jit(solution)/shard_map/all_to_all | solution.py:318
  58.1 0.1 mul.74
  58.2 0.1 mul.77
  58.3 0.7 reduce.15
  59.0 0.1 mul.80
  59.0 0.2 multiply_reduce_fusion
  59.3 0.2 select_reduce_fusion
  59.5 0.1 copy.15
  59.6 0.6 select_n.69.slots
  60.2 0.1 copy.13
  60.2 0.6 reshape.55.rows
  60.8 0.1 copy.14
  60.9 0.6 reshape.56.cols
  61.5 5.4 %flip_test.1.test_ref = bf16[8,128,512]{2,1,0:T(8,128)(2,1)} custom-call(bf16[8,512,128]{2,1,0:T(8,128)(2,1)} %bitcast.29), custom_call_target="tpu_custom_call" | custom-call | tf_op jit(solution)/shard_map/flip_test/pallas_call | solution.py:158
  67.0 0.6 slice_bitcast_fusion.2
  67.6 5.4 %flip_basis.1.basis_ref = bf16[8,512,128]{2,1,0:T(8,128)(2,1)} custom-call(bf16[8,128,512]{2,1,0:T(8,128)(2,1)} %get-tuple-element.8.x_ref.flip_ref), custom_call_target="tpu_custom_call" | custom-call | tf_op jit(solution)/shard_map/flip_basis/pallas_call | solution.py:158
  73.0 0.4 all-to-all-done
  73.4 0.8 copy-done
  74.2 17.2 %decode.1 = (bf16[8,512,512]{2,1,0:T(8,128)(2,1)}, bf16[16,128,128]{2,1,0:T(8,128)(2,1)}, bf16[16,128,128]{2,1,0:T(8,128)(2,1)}) custom-call(s32[16]{0:T(128)} %reshape.55.rows, s32[16]{0:T(128)} %reshape.56.cols, s32[16]{0:T(128)} %select_n.69.slots, s32[8]{0:T(128)} %get-tuple-element.33.prows, s32[8]{0:T(128)} %get-tuple-element.32.pcols, ...), custom_call_target="tpu_custom_call" | custom-call | tf_op jit(solution)/shard_map/decode/pallas_call | solution.py:226
  91.5 0.1 collective-permute-start.13
  91.6 2.0 %collective-permute-done.13 = bf16[16,128,128]{2,1,0:T(8,128)(2,1)S(1)} collective-permute-done((bf16[16,128,128]{2,1,0:T(8,128)(2,1)}, bf16[16,128,128]{2,1,0:T(8,128)(2,1)S(1)}, u32[]{:S(2)}, u32[]{:S(2)}) %collective-permute-start.13) | collective-permute-done | bytes 524320 | tf_op jit(solution)/shard_map/ppermute | solution.py:58
  93.6 1.2 %convert_add_fusion = f32[16,128,128]{2,1,0:T(8,128)S(1)} fusion(bf16[16,128,128]{2,1,0:T(8,128)(2,1)S(1)} %collective-permute-done.13, bf16[16,128,128]{2,1,0:T(8,128)(2,1)} %get-tuple-element.10), kind=kLoop, calls=%fused_computation | loop fusion | flops 786432 | bytes 2097152 | tf_op jit(solution)/shard_map/add | solution.py:256
  94.7 0.1 dynamic-slice_convert_fusion.2
  94.8 1.4 %collective-permute-start.14 = (bf16[4,128,128]{2,1,0:T(8,128)(2,1)S(1)}, bf16[4,128,128]{2,1,0:T(8,128)(2,1)S(1)}, u32[]{:S(2)}, u32[]{:S(2)}) collective-permute-start(bf16[4,128,128]{2,1,0:T(8,128)(2,1)S(1)} %get-tuple-element.24), channel_id=1, source_target_pairs={{0,8},{8,16},{16,24},{24,0},{1,9},{9,17},{17,25},{25,1},{2,10},{10... | collective-permute-start | bytes 393224 | tf_op jit(solution)/shard_map/ppermute | solution.py:259
  96.2 2.7 %collective-permute-start.15 = (bf16[4,128,128]{2,1,0:T(8,128)(2,1)S(1)}, bf16[4,128,128]{2,1,0:T(8,128)(2,1)S(1)}, u32[]{:S(2)}, u32[]{:S(2)}) collective-permute-start(bf16[4,128,128]{2,1,0:T(8,128)(2,1)S(1)} %get-tuple-element.26), channel_id=1, source_target_pairs={{0,16},{8,24},{16,0},{24,8},{1,17},{9,25},{17,1},{25,9},{2,18},{10... | collective-permute-start | bytes 393224 | tf_op jit(solution)/shard_map/ppermute | solution.py:259
  98.9 0.6 collective-permute-start.16
  99.5 3.3 %collective-permute-done.14 = bf16[4,128,128]{2,1,0:T(8,128)(2,1)S(1)} collective-permute-done((bf16[4,128,128]{2,1,0:T(8,128)(2,1)S(1)}, bf16[4,128,128]{2,1,0:T(8,128)(2,1)S(1)}, u32[]{:S(2)}, u32[]{:S(2)}) %collective-permute-start.14) | collective-permute-done | bytes 131104 | tf_op jit(solution)/shard_map/ppermute | solution.py:259
  102.7 2.2 %collective-permute-done.15 = bf16[4,128,128]{2,1,0:T(8,128)(2,1)S(1)} collective-permute-done((bf16[4,128,128]{2,1,0:T(8,128)(2,1)S(1)}, bf16[4,128,128]{2,1,0:T(8,128)(2,1)S(1)}, u32[]{:S(2)}, u32[]{:S(2)}) %collective-permute-start.15) | collective-permute-done | bytes 131104 | tf_op jit(solution)/shard_map/ppermute | solution.py:259
  105.0 1.1 %collective-permute-start.17 = (bf16[1,128,128]{2,1,0:T(8,128)(2,1)S(1)}, bf16[1,128,128]{2,1,0:T(8,128)(2,1)S(1)}, u32[]{:S(2)}, u32[]{:S(2)}) collective-permute-start(bf16[1,128,128]{2,1,0:T(8,128)(2,1)S(1)} %get-tuple-element.27), channel_id=1, source_target_pairs={{0,2},{1,3},{2,4},{3,5},{4,6},{5,7},{6,0},{7,1},{8,10},{9,11},{10,... | collective-permute-start | bytes 98312 | tf_op jit(solution)/shard_map/ppermute | solution.py:264
  106.2 2.3 %collective-permute-start.18 = (bf16[1,128,128]{2,1,0:T(8,128)(2,1)S(1)}, bf16[1,128,128]{2,1,0:T(8,128)(2,1)S(1)}, u32[]{:S(2)}, u32[]{:S(2)}) collective-permute-start(bf16[1,128,128]{2,1,0:T(8,128)(2,1)S(1)} %get-tuple-element.29), channel_id=1, source_target_pairs={{0,4},{1,5},{2,6},{3,7},{4,0},{5,1},{6,2},{7,3},{8,12},{9,13},{10,... | collective-permute-start | bytes 98312 | tf_op jit(solution)/shard_map/ppermute | solution.py:264
  108.5 1.2 %collective-permute-start.19 = (bf16[1,128,128]{2,1,0:T(8,128)(2,1)S(1)}, bf16[1,128,128]{2,1,0:T(8,128)(2,1)S(1)}, u32[]{:S(2)}, u32[]{:S(2)}) collective-permute-start(bf16[1,128,128]{2,1,0:T(8,128)(2,1)S(1)} %get-tuple-element.28), channel_id=1, source_target_pairs={{0,6},{1,7},{2,0},{3,1},{4,2},{5,3},{6,4},{7,5},{8,14},{9,15},{10,... | collective-permute-start | bytes 98312 | tf_op jit(solution)/shard_map/ppermute | solution.py:264
  109.7 1.5 %collective-permute-done.17 = bf16[1,128,128]{2,1,0:T(8,128)(2,1)S(1)} collective-permute-done((bf16[1,128,128]{2,1,0:T(8,128)(2,1)S(1)}, bf16[1,128,128]{2,1,0:T(8,128)(2,1)S(1)}, u32[]{:S(2)}, u32[]{:S(2)}) %collective-permute-start.17) | collective-permute-done | bytes 32800 | tf_op jit(solution)/shard_map/ppermute | solution.py:264
  111.2 0.6 collective-permute-done.18
  111.8 0.6 collective-permute-done.19
  112.4 0.7 copy.16
  (48 shorter events, 0.2 us)
Async XLA Ops:
  2.7 10.8 %collective-permute-start = (bf16[1,256,512]{2,1,0:T(8,128)(2,1)}, bf16[1,256,512]{2,1,0:T(8,128)(2,1)S(1)}, u32[]{:S(2)}, u32[]{:S(2)}) collective-permute-start(bf16[1,256,512]{2,1,0:T(8,128)(2,1)} %project.1.refs_0_), channel_id=1, source_target_pairs={{0,2},{1,3},{2,4},{3,5},{4,6},{5,7},{8,10},{9,11},{10,12},{11,13},... | collective-permute-start | bytes 786440 | tf_op jit(solution)/shard_map/ppermute | solution.py:54
  7.6 10.1 %collective-permute-start.1 = (bf16[1,256,512]{2,1,0:T(8,128)(2,1)}, bf16[1,256,512]{2,1,0:T(8,128)(2,1)S(1)}, u32[]{:S(2)}, u32[]{:S(2)}) collective-permute-start(bf16[1,256,512]{2,1,0:T(8,128)(2,1)} %project.1.refs_0_), channel_id=1, source_target_pairs={{2,0},{3,1},{4,2},{5,3},{6,4},{7,5},{10,8},{11,9},{12,10},{13,11},... | collective-permute-start | bytes 786440 | tf_op jit(solution)/shard_map/ppermute | solution.py:54
  13.5 24.3 %copy-start.1 = (bf16[1,256,512]{2,1,0:T(8,128)(2,1)}, bf16[1,256,512]{2,1,0:T(8,128)(2,1)S(1)}, u32[]{:S(2)}) copy-start(bf16[1,256,512]{2,1,0:T(8,128)(2,1)S(1)} %collective-permute-done.refs_1_) | copy-start | bytes 786436
  13.5 9.0 %collective-permute-start.2 = (bf16[1,256,512]{2,1,0:T(8,128)(2,1)S(1)}, bf16[1,256,512]{2,1,0:T(8,128)(2,1)S(1)}, u32[]{:S(2)}, u32[]{:S(2)}) collective-permute-start(bf16[1,256,512]{2,1,0:T(8,128)(2,1)S(1)} %collective-permute-done.refs_1_), channel_id=1, source_target_pairs={{0,2},{1,3},{2,4},{3,5},{4,6},{5,7},{8,10},{9,11},{10,12},{11,13},... | collective-permute-start | bytes 786440 | tf_op jit(solution)/shard_map/ppermute | solution.py:54
  17.8 20.0 %copy-start.2 = (bf16[1,256,512]{2,1,0:T(8,128)(2,1)}, bf16[1,256,512]{2,1,0:T(8,128)(2,1)S(1)}, u32[]{:S(2)}) copy-start(bf16[1,256,512]{2,1,0:T(8,128)(2,1)S(1)} %collective-permute-done.1.refs_2_) | copy-start | bytes 786436
  17.8 9.1 %collective-permute-start.3 = (bf16[1,256,512]{2,1,0:T(8,128)(2,1)S(1)}, bf16[1,256,512]{2,1,0:T(8,128)(2,1)S(1)}, u32[]{:S(2)}, u32[]{:S(2)}) collective-permute-start(bf16[1,256,512]{2,1,0:T(8,128)(2,1)S(1)} %collective-permute-done.1.refs_2_), channel_id=1, source_target_pairs={{2,0},{3,1},{4,2},{5,3},{6,4},{7,5},{10,8},{11,9},{12,10},{13,11},... | collective-permute-start | bytes 786440 | tf_op jit(solution)/shard_map/ppermute | solution.py:54
  19.1 9.7 %collective-permute-start.6 = (bf16[1,256,512]{2,1,0:T(8,128)(2,1)}, bf16[1,256,512]{2,1,0:T(8,128)(2,1)S(1)}, u32[]{:S(2)}, u32[]{:S(2)}) collective-permute-start(bf16[1,256,512]{2,1,0:T(8,128)(2,1)} %project.1.refs_0_), channel_id=1, source_target_pairs={{0,1},{1,0},{2,3},{3,2},{4,5},{5,4},{6,7},{7,6},{8,9},{9,8},{10,11... | collective-permute-start | bytes 786440 | tf_op jit(solution)/shard_map/ppermute | solution.py:58
  21.3 8.0 %collective-permute-start.7 = (bf16[1,256,512]{2,1,0:T(8,128)(2,1)S(1)}, bf16[1,256,512]{2,1,0:T(8,128)(2,1)S(1)}, u32[]{:S(2)}, u32[]{:S(2)}) collective-permute-start(bf16[1,256,512]{2,1,0:T(8,128)(2,1)S(1)} %collective-permute-done.refs_1_), channel_id=1, source_target_pairs={{0,1},{1,0},{2,3},{3,2},{4,5},{5,4},{6,7},{7,6},{8,9},{9,8},{10,11... | collective-permute-start | bytes 786440 | tf_op jit(solution)/shard_map/ppermute | solution.py:58
  22.4 15.4 %copy-start.3 = (bf16[1,256,512]{2,1,0:T(8,128)(2,1)}, bf16[1,256,512]{2,1,0:T(8,128)(2,1)S(1)}, u32[]{:S(2)}) copy-start(bf16[1,256,512]{2,1,0:T(8,128)(2,1)S(1)} %collective-permute-done.2.refs_3_) | copy-start | bytes 786436
  22.5 9.7 %collective-permute-start.4 = (bf16[1,256,512]{2,1,0:T(8,128)(2,1)S(1)}, bf16[1,256,512]{2,1,0:T(8,128)(2,1)S(1)}, u32[]{:S(2)}, u32[]{:S(2)}) collective-permute-start(bf16[1,256,512]{2,1,0:T(8,128)(2,1)S(1)} %collective-permute-done.2.refs_3_), channel_id=1, source_target_pairs={{0,2},{1,3},{2,4},{3,5},{4,6},{5,7},{8,10},{9,11},{10,12},{11,13},... | collective-permute-start | bytes 786440 | tf_op jit(solution)/shard_map/ppermute | solution.py:54
  26.9 11.0 %copy-start.4 = (bf16[1,256,512]{2,1,0:T(8,128)(2,1)}, bf16[1,256,512]{2,1,0:T(8,128)(2,1)S(1)}, u32[]{:S(2)}) copy-start(bf16[1,256,512]{2,1,0:T(8,128)(2,1)S(1)} %collective-permute-done.3.refs_4_) | copy-start | bytes 786436
  26.9 9.4 %collective-permute-start.5 = (bf16[1,256,512]{2,1,0:T(8,128)(2,1)S(1)}, bf16[1,256,512]{2,1,0:T(8,128)(2,1)S(1)}, u32[]{:S(2)}, u32[]{:S(2)}) collective-permute-start(bf16[1,256,512]{2,1,0:T(8,128)(2,1)S(1)} %collective-permute-done.3.refs_4_), channel_id=1, source_target_pairs={{2,0},{3,1},{4,2},{5,3},{6,4},{7,5},{10,8},{11,9},{12,10},{13,11},... | collective-permute-start | bytes 786440 | tf_op jit(solution)/shard_map/ppermute | solution.py:54
  28.8 8.8 %collective-permute-start.8 = (bf16[1,256,512]{2,1,0:T(8,128)(2,1)S(1)}, bf16[1,256,512]{2,1,0:T(8,128)(2,1)S(1)}, u32[]{:S(2)}, u32[]{:S(2)}) collective-permute-start(bf16[1,256,512]{2,1,0:T(8,128)(2,1)S(1)} %collective-permute-done.1.refs_2_), channel_id=1, source_target_pairs={{0,1},{1,0},{2,3},{3,2},{4,5},{5,4},{6,7},{7,6},{8,9},{9,8},{10,11... | collective-permute-start | bytes 786440 | tf_op jit(solution)/shard_map/ppermute | solution.py:58
  28.8 9.1 %copy-start.5 = (bf16[1,256,512]{2,1,0:T(8,128)(2,1)}, bf16[1,256,512]{2,1,0:T(8,128)(2,1)S(1)}, u32[]{:S(2)}) copy-start(bf16[1,256,512]{2,1,0:T(8,128)(2,1)S(1)} %collective-permute-done.6.refs_7_) | copy-start | bytes 786436
  28.8 8.8 %collective-permute-start.10 = (bf16[1,256,512]{2,1,0:T(8,128)(2,1)S(1)}, bf16[1,256,512]{2,1,0:T(8,128)(2,1)S(1)}, u32[]{:S(2)}, u32[]{:S(2)}) collective-permute-start(bf16[1,256,512]{2,1,0:T(8,128)(2,1)S(1)} %collective-permute-done.3.refs_4_), channel_id=1, source_target_pairs={{0,1},{1,0},{2,3},{3,2},{4,5},{5,4},{6,7},{7,6},{8,9},{9,8},{10,11... | collective-permute-start | bytes 786440 | tf_op jit(solution)/shard_map/ppermute | solution.py:58
  29.3 8.6 %copy-start.6 = (bf16[1,256,512]{2,1,0:T(8,128)(2,1)}, bf16[1,256,512]{2,1,0:T(8,128)(2,1)S(1)}, u32[]{:S(2)}) copy-start(bf16[1,256,512]{2,1,0:T(8,128)(2,1)S(1)} %collective-permute-done.7.refs_8_) | copy-start | bytes 786436
  29.3 8.3 %collective-permute-start.9 = (bf16[1,256,512]{2,1,0:T(8,128)(2,1)S(1)}, bf16[1,256,512]{2,1,0:T(8,128)(2,1)S(1)}, u32[]{:S(2)}, u32[]{:S(2)}) collective-permute-start(bf16[1,256,512]{2,1,0:T(8,128)(2,1)S(1)} %collective-permute-done.2.refs_3_), channel_id=1, source_target_pairs={{0,1},{1,0},{2,3},{3,2},{4,5},{5,4},{6,7},{7,6},{8,9},{9,8},{10,11... | collective-permute-start | bytes 786440 | tf_op jit(solution)/shard_map/ppermute | solution.py:58
  32.1 5.7 %copy-start.7 = (bf16[1,256,512]{2,1,0:T(8,128)(2,1)}, bf16[1,256,512]{2,1,0:T(8,128)(2,1)S(1)}, u32[]{:S(2)}) copy-start(bf16[1,256,512]{2,1,0:T(8,128)(2,1)S(1)} %collective-permute-done.4.refs_5_) | copy-start | bytes 786436
  32.1 5.5 %collective-permute-start.11 = (bf16[1,256,512]{2,1,0:T(8,128)(2,1)S(1)}, bf16[1,256,512]{2,1,0:T(8,128)(2,1)S(1)}, u32[]{:S(2)}, u32[]{:S(2)}) collective-permute-start(bf16[1,256,512]{2,1,0:T(8,128)(2,1)S(1)} %collective-permute-done.4.refs_5_), channel_id=1, source_target_pairs={{0,1},{1,0},{2,3},{3,2},{4,5},{5,4},{6,7},{7,6},{8,9},{9,8},{10,11... | collective-permute-start | bytes 786440 | tf_op jit(solution)/shard_map/ppermute | solution.py:58
  36.3 1.6 %copy-start.8 = (bf16[1,256,512]{2,1,0:T(8,128)(2,1)}, bf16[1,256,512]{2,1,0:T(8,128)(2,1)S(1)}, u32[]{:S(2)}) copy-start(bf16[1,256,512]{2,1,0:T(8,128)(2,1)S(1)} %collective-permute-done.5.refs_6_) | copy-start | bytes 786436
  36.3 1.5 %collective-permute-start.12 = (bf16[1,256,512]{2,1,0:T(8,128)(2,1)S(1)}, bf16[1,256,512]{2,1,0:T(8,128)(2,1)S(1)}, u32[]{:S(2)}, u32[]{:S(2)}) collective-permute-start(bf16[1,256,512]{2,1,0:T(8,128)(2,1)S(1)} %collective-permute-done.5.refs_6_), channel_id=1, source_target_pairs={{0,1},{1,0},{2,3},{3,2},{4,5},{5,4},{6,7},{7,6},{8,9},{9,8},{10,11... | collective-permute-start | bytes 786440 | tf_op jit(solution)/shard_map/ppermute | solution.py:58
  37.6 0.7 copy-start.9
  37.6 0.8 copy-start.10
  37.6 0.9 copy-start.11
  37.6 0.9 copy-start.12
  37.8 0.8 copy-start.13
  38.6 19.5 %copy-start.14 = (s32[1,128,2]{1,2,0:T(2,128)S(1)}, s32[1,128,2]{1,2,0:T(2,128)}, u32[]{:S(2)}) copy-start(s32[1,128,2]{1,2,0:T(2,128)} %param.12) | copy-start | bytes 3076
  38.6 19.6 %copy-start.16 = (s32[1,128]{1,0:T(1,128)S(1)}, s32[1,128]{1,0:T(1,128)}, u32[]{:S(2)}) copy-start(s32[1,128]{1,0:T(1,128)} %param.14) | copy-start | bytes 1540
  38.6 28.3 %copy-start.15 = (s32[1,8,2]{1,2,0:T(2,128)S(1)}, s32[1,8,2]{1,2,0:T(2,128)}, u32[]{:S(2)}) copy-start(s32[1,8,2]{1,2,0:T(2,128)} %param.16) | copy-start | bytes 196
  54.1 19.3 %all-to-all-start = ((bf16[8,2,128,128]{3,2,1,0:T(8,128)(2,1)}), bf16[8,2,128,128]{3,2,1,0:T(8,128)(2,1)S(1)}, u32[]{:S(2)}, u32[]{:S(2)}) async-start(bf16[8,2,128,128]{3,2,1,0:T(8,128)(2,1)} %bitcast.30), calls=%async_computation | async-start | bytes 1048576 | tf_op jit(solution)/shard_map/all_to_all | solution.py:318
  73.4 0.8 copy-start
  91.5 2.1 %collective-permute-start.13 = (bf16[16,128,128]{2,1,0:T(8,128)(2,1)}, bf16[16,128,128]{2,1,0:T(8,128)(2,1)S(1)}, u32[]{:S(2)}, u32[]{:S(2)}) collective-permute-start(bf16[16,128,128]{2,1,0:T(8,128)(2,1)} %get-tuple-element.11), channel_id=1, source_target_pairs={{0,1},{1,0},{2,3},{3,2},{4,5},{5,4},{6,7},{7,6},{8,9},{9,8},{10,11... | collective-permute-start | bytes 1572872 | tf_op jit(solution)/shard_map/ppermute | solution.py:58
  94.8 7.9 %collective-permute-start.14 = (bf16[4,128,128]{2,1,0:T(8,128)(2,1)S(1)}, bf16[4,128,128]{2,1,0:T(8,128)(2,1)S(1)}, u32[]{:S(2)}, u32[]{:S(2)}) collective-permute-start(bf16[4,128,128]{2,1,0:T(8,128)(2,1)S(1)} %get-tuple-element.24), channel_id=1, source_target_pairs={{0,8},{8,16},{16,24},{24,0},{1,9},{9,17},{17,25},{25,1},{2,10},{10... | collective-permute-start | bytes 393224 | tf_op jit(solution)/shard_map/ppermute | solution.py:259
  96.2 8.7 %collective-permute-start.15 = (bf16[4,128,128]{2,1,0:T(8,128)(2,1)S(1)}, bf16[4,128,128]{2,1,0:T(8,128)(2,1)S(1)}, u32[]{:S(2)}, u32[]{:S(2)}) collective-permute-start(bf16[4,128,128]{2,1,0:T(8,128)(2,1)S(1)} %get-tuple-element.26), channel_id=1, source_target_pairs={{0,16},{8,24},{16,0},{24,8},{1,17},{9,25},{17,1},{25,9},{2,18},{10... | collective-permute-start | bytes 393224 | tf_op jit(solution)/shard_map/ppermute | solution.py:259
  98.9 6.0 %collective-permute-start.16 = (bf16[4,128,128]{2,1,0:T(8,128)(2,1)S(1)}, bf16[4,128,128]{2,1,0:T(8,128)(2,1)S(1)}, u32[]{:S(2)}, u32[]{:S(2)}) collective-permute-start(bf16[4,128,128]{2,1,0:T(8,128)(2,1)S(1)} %get-tuple-element.25), channel_id=1, source_target_pairs={{0,24},{8,0},{16,8},{24,16},{1,25},{9,1},{17,9},{25,17},{2,26},{10... | collective-permute-start | bytes 393224 | tf_op jit(solution)/shard_map/ppermute | solution.py:259
  105.0 6.1 %collective-permute-start.17 = (bf16[1,128,128]{2,1,0:T(8,128)(2,1)S(1)}, bf16[1,128,128]{2,1,0:T(8,128)(2,1)S(1)}, u32[]{:S(2)}, u32[]{:S(2)}) collective-permute-start(bf16[1,128,128]{2,1,0:T(8,128)(2,1)S(1)} %get-tuple-element.27), channel_id=1, source_target_pairs={{0,2},{1,3},{2,4},{3,5},{4,6},{5,7},{6,0},{7,1},{8,10},{9,11},{10,... | collective-permute-start | bytes 98312 | tf_op jit(solution)/shard_map/ppermute | solution.py:264
  106.2 5.6 %collective-permute-start.18 = (bf16[1,128,128]{2,1,0:T(8,128)(2,1)S(1)}, bf16[1,128,128]{2,1,0:T(8,128)(2,1)S(1)}, u32[]{:S(2)}, u32[]{:S(2)}) collective-permute-start(bf16[1,128,128]{2,1,0:T(8,128)(2,1)S(1)} %get-tuple-element.29), channel_id=1, source_target_pairs={{0,4},{1,5},{2,6},{3,7},{4,0},{5,1},{6,2},{7,3},{8,12},{9,13},{10,... | collective-permute-start | bytes 98312 | tf_op jit(solution)/shard_map/ppermute | solution.py:264
  108.5 3.9 %collective-permute-start.19 = (bf16[1,128,128]{2,1,0:T(8,128)(2,1)S(1)}, bf16[1,128,128]{2,1,0:T(8,128)(2,1)S(1)}, u32[]{:S(2)}, u32[]{:S(2)}) collective-permute-start(bf16[1,128,128]{2,1,0:T(8,128)(2,1)S(1)} %get-tuple-element.28), channel_id=1, source_target_pairs={{0,6},{1,7},{2,0},{3,1},{4,2},{5,3},{6,4},{7,5},{8,14},{9,15},{10,... | collective-permute-start | bytes 98312 | tf_op jit(solution)/shard_map/ppermute | solution.py:264

commit v2 on v1

v2 whole, which is shorter than its diff:
```python
import jax
import jax.numpy as jnp
from jax import lax
from jax.experimental import pallas as pl
from jax.experimental.pallas import tpu as pltpu
from jax.sharding import PartitionSpec as P

CAP = 2
RING_OWNERS = 8
VMEM_BYTES = 58 * 1024 * 1024
F32 = jnp.float32
BF16 = jnp.bfloat16
NT = (((1,), (1,)), ((), ()))


def dot(x, y):
    return jnp.dot(x, y, preferred_element_type=F32)


def params():
    return pltpu.CompilerParams(vmem_limit_bytes=VMEM_BYTES)


def project_kernel(panel_ref, basis_ref, out_ref):
    rank = basis_ref.shape[2]
    flipped = basis_ref[0].T
    out_ref[0, :rank] = flipped
    out_ref[0, rank:] = dot(flipped, panel_ref[0]).astype(BF16)


def project(panel, bases, order):
    blocks = panel.shape[0] // order
    width, rank = panel.shape[1], bases.shape[1]
    return pl.pallas_call(
        project_kernel,
        grid=(blocks,),
        in_specs=[
            pl.BlockSpec((1, order, width), lambda b: (b, 0, 0)),
            pl.BlockSpec((1, order, rank), lambda b: (b, 0, 0)),
        ],
        out_specs=pl.BlockSpec((1, 2 * rank, order), lambda b: (b, 0, 0)),
        out_shape=jax.ShapeDtypeStruct((blocks, 2 * rank, order), BF16),
        compiler_params=params(),
        name="project",
    )(panel.reshape(blocks, order, width), bases.reshape(blocks, order, rank))


def along_chips(x, owners, shift):
    return lax.ppermute(x, "tile", [(t, (t + 2 * shift) % owners) for t in range(owners)])


def to_partner(x, owners):
    return lax.ppermute(x, "tile", [(t, t ^ 1) for t in range(owners)])


def spread(block, owners):
    if owners > RING_OWNERS or owners % 4:
        return [lax.all_gather(block, "tile", axis=0, tiled=True)], None
    far, half = owners // 4, block.shape[1] // 2
    arrays, places = [block], [(0, 0)]
    up, down = block, block
    for step in range(1, far + 1):
        if step == far:
            up, down = up[:, :half], down[:, half:]
        up, down = along_chips(up, owners, 1), along_chips(down, owners, -1)
        arrays += [up, down]
        places += [(-step, 0), (step, half if step == far else 0)]
    return arrays + [to_partner(x, owners) for x in arrays], places


def unpack(word, blocks):
    rest = word // blocks
    return rest // blocks, rest % blocks, word % blocks


SCALARS = pl.BlockSpec(memory_space=pltpu.SMEM)
ANYWHERE = pl.BlockSpec(memory_space=pl.ANY)
IN_HBM = pl.BlockSpec(memory_space=pltpu.HBM)
ON_CHIP = pl.BlockSpec(memory_space=pltpu.VMEM)


def encode_kernel(places, count, words, tiles, *refs):
    parts = refs[:-10]
    core_out, flip_out = refs[-10:-8]
    held, staged, coded, tile_sems, part_sems, core_sems, flip_sem = refs[-8:-1]
    blocks = held.shape[0]
    rank = core_out.shape[1]
    flip_copy = pltpu.make_async_copy(held.at[:, :rank], flip_out, flip_sem)

    def part_copies():
        if places is None:
            return [pltpu.make_async_copy(parts[0], held, part_sems.at[0])]
        local = parts[0].shape[0]
        me = lax.axis_index("tile")
        chips = lax.axis_size("tile") // 2
        chip, core = me // 2, me % 2
        copies = []
        for n, part in enumerate(parts):
            offset, first = places[n % len(places)]
            owner = ((chip + chips + offset) % chips) * 2
            owner = owner + (core if n < len(places) else 1 - core)
            copies.append(
                pltpu.make_async_copy(
                    part,
                    held.at[pl.ds(owner * local, local), pl.ds(first, part.shape[1])],
                    part_sems.at[n],
                )
            )
        return copies

    def tile_copy(q):
        return pltpu.make_async_copy(tiles.at[q], staged.at[q], tile_sems.at[q])

    def core_copy(q, place):
        return pltpu.make_async_copy(coded.at[q], core_out.at[place], core_sems.at[q])

    copies = part_copies()
    for copy in copies:
        copy.start()
    for q in range(count):
        tile_copy(q).start()
    for copy in copies:
        copy.wait()
    flip_copy.start()

    def one(q, carry):
        place, row, col = unpack(words[q], blocks)
        tile_copy(q).wait()
        half = dot(held[row, :rank], staged[q]).astype(BF16)
        encoded = lax.dot_general(half, held[col, :rank], NT, preferred_element_type=F32)
        cross = lax.dot_general(
            held[row, rank:], held[col, rank:], NT, preferred_element_type=F32
        )
        coded[q] = (encoded - cross).astype(BF16)
        core_copy(q, place).start()
        return carry

    lax.fori_loop(0, count, one, 0, unroll=4)
    for q in range(count):
        core_copy(q, 0).wait()
    flip_copy.wait()


def encode(tiles, parts, places, words, owners):
    count, order, _ = tiles.shape
    rank = parts[0].shape[1] // 2
    blocks = parts[0].shape[0] * (1 if places is None else owners)
    slots = owners * CAP

    def body(words, tiles, *refs):
        encode_kernel(places, count, words, tiles, *refs, None)

    return pl.pallas_call(
        body,
        in_specs=[SCALARS, IN_HBM] + [ANYWHERE] * len(parts),
        out_specs=[ANYWHERE, ANYWHERE],
        scratch_shapes=[
            pltpu.VMEM((blocks, 2 * rank, order), BF16),
            pltpu.VMEM(tiles.shape, BF16),
            pltpu.VMEM((count, rank, rank), BF16),
            pltpu.SemaphoreType.DMA((count,)),
            pltpu.SemaphoreType.DMA((len(parts),)),
            pltpu.SemaphoreType.DMA((count,)),
            pltpu.SemaphoreType.DMA,
        ],
        out_shape=[
            jax.ShapeDtypeStruct((slots, rank, rank), BF16),
            jax.ShapeDtypeStruct((blocks, rank, order), BF16),
        ],
        compiler_params=params(),
        name="encode",
    )(words, tiles, *parts)


def add_rows(sketch, block, value):
    lanes = sketch.shape[2]
    pieces = value.shape[1] // lanes
    for r in range(pieces):
        sketch[block * pieces + r] += value[:, r * lanes : (r + 1) * lanes]


def prepare_kernel(words, pwords, flip_ref, test_ref, parents, basis_ref, west, vest, sketch, turned):
    blocks, tests = flip_ref.shape[0], test_ref.shape[0]
    count = parents.shape[0]
    sketch[...] = jnp.zeros_like(sketch)
    for b in range(tests):
        turned[b] = test_ref[b].T
    for b in range(blocks):
        basis_ref[b] = flip_ref[b].T

    def parent(p, carry):
        prow, pcol = pwords[2 * p], pwords[2 * p + 1]
        add_rows(
            sketch,
            prow,
            lax.dot_general(turned[pcol], parents[p], NT, preferred_element_type=F32),
        )

        @pl.when(prow != pcol)
        def _():
            add_rows(sketch, pcol, dot(turned[prow], parents[p]))

        return carry

    lax.fori_loop(0, count, parent, 0)

    def item(s, carry):
        slot, row, col = unpack(words[s], blocks)

        @pl.when(slot > 0)
        def _():
            prow, pcol = pwords[2 * slot - 2], pwords[2 * slot - 1]
            west[s] = lax.dot_general(
                turned[pcol], flip_ref[col], NT, preferred_element_type=F32
            ).astype(BF16)
            vest[s] = lax.dot_general(
                turned[prow], flip_ref[row], NT, preferred_element_type=F32
            ).astype(BF16)

        return carry

    lax.fori_loop(0, west.shape[0], item, 0)


def prepare(words, pwords, flipped, test, parents, lanes):
    blocks, rank, order = flipped.shape
    tests, _, width = test.shape
    items = words.shape[0]
    return pl.pallas_call(
        prepare_kernel,
        in_specs=[SCALARS, SCALARS, ON_CHIP, ON_CHIP, ON_CHIP],
        out_specs=[ON_CHIP] * 4,
        scratch_shapes=[pltpu.VMEM((tests, width, order), BF16)],
        out_shape=[
            jax.ShapeDtypeStruct((blocks, order, rank), BF16),
            jax.ShapeDtypeStruct((items, width, rank), BF16),
            jax.ShapeDtypeStruct((items, width, rank), BF16),
            jax.ShapeDtypeStruct((tests * order // lanes, width, lanes), F32),
        ],
        compiler_params=params(),
        cost_estimate=pl.CostEstimate(
            flops=4 * parents.size * width, bytes_accessed=2 * parents.size, transcendentals=0
        ),
        name="prepare",
    )(words, pwords, flipped, test, parents)


def fold_kernel(
    words, pwords, core_ref, west, vest, flip_ref, start, keep_ref, send_ref, sketch, base, sem
):
    blocks = flip_ref.shape[0]
    base_copy = pltpu.make_async_copy(start, base, sem)
    base_copy.start()
    sketch[...] = jnp.zeros_like(sketch)

    def item(s, carry):
        slot, row, col = unpack(words[s], blocks)

        @pl.when(slot > 0)
        def _():
            prow, pcol = pwords[2 * slot - 2], pwords[2 * slot - 1]
            first = lax.dot_general(west[s], core_ref[s], NT, preferred_element_type=F32)
            add_rows(sketch, prow, dot(first.astype(BF16), flip_ref[row]))

            @pl.when(prow != pcol)
            def _():
                second = dot(vest[s], core_ref[s]).astype(BF16)
                add_rows(sketch, pcol, dot(second, flip_ref[col]))

        return carry

    lax.fori_loop(0, core_ref.shape[0], item, 0)
    base_copy.wait()
    core = lax.axis_index("tile") % 2
    for n in range(keep_ref.shape[0]):
        mine, other = 2 * n + core, 2 * n + 1 - core
        keep_ref[n] = (sketch[mine] + base[mine]).astype(BF16)
        send_ref[n] = (sketch[other] + base[other]).astype(BF16)


def fold(words, pwords, cores, west, vest, flipped, start):
    chunks, width, lanes = start.shape
    half = jax.ShapeDtypeStruct((chunks // 2, width, lanes), BF16)
    return pl.pallas_call(
        fold_kernel,
        in_specs=[SCALARS, SCALARS] + [ON_CHIP] * 4 + [ANYWHERE],
        out_specs=[ON_CHIP, ON_CHIP],
        scratch_shapes=[
            pltpu.VMEM(start.shape, F32),
            pltpu.VMEM(start.shape, F32),
            pltpu.SemaphoreType.DMA,
        ],
        out_shape=[half, half],
        compiler_params=params(),
        name="fold",
    )(words, pwords, cores, west, vest, flipped, start)


def update_kernel(
    words, parents, core_ref, basis_ref, flip_ref, updated, held, total, made, in_sems, out_sems
):
    count, blocks = held.shape[0], basis_ref.shape[0]

    def in_copy(p):
        return pltpu.make_async_copy(parents.at[p], held.at[p], in_sems.at[p])

    def out_copy(p):
        return pltpu.make_async_copy(made.at[p], updated.at[p], out_sems.at[p])

    for p in range(count):
        in_copy(p).start()

    def one(p, carry):
        in_copy(p).wait()
        total[...] = held[p].astype(F32)

        def item(s, carry):
            slot, row, col = unpack(words[s], blocks)

            @pl.when(slot == p + 1)
            def _():
                left = dot(basis_ref[row], core_ref[s]).astype(BF16)
                total[...] += dot(left, flip_ref[col])

            return carry

        lax.fori_loop(0, core_ref.shape[0], item, 0)
        made[p] = total[...].astype(BF16)
        out_copy(p).start()
        return carry

    lax.fori_loop(0, count, one, 0)
    for p in range(count):
        out_copy(p).wait()


def update(words, parents, cores, basis, flipped):
    count, order, _ = parents.shape
    rank = basis.shape[2]
    return pl.pallas_call(
        update_kernel,
        in_specs=[SCALARS, IN_HBM, ON_CHIP, ON_CHIP, ON_CHIP],
        out_specs=IN_HBM,
        scratch_shapes=[
            pltpu.VMEM(parents.shape, BF16),
            pltpu.VMEM((order, order), F32),
            pltpu.VMEM(parents.shape, BF16),
            pltpu.SemaphoreType.DMA((count,)),
            pltpu.SemaphoreType.DMA((count,)),
        ],
        out_shape=jax.ShapeDtypeStruct(parents.shape, BF16),
        compiler_params=params(),
        cost_estimate=pl.CostEstimate(
            flops=8 * parents.size * rank, bytes_accessed=4 * parents.size, transcendentals=0
        ),
        name="update",
    )(words, parents, cores, basis, flipped)


def exchange_sum(pieces, size, me, send, group):
    mine = lax.dynamic_slice_in_dim(pieces, me * group, group, 0)
    for shift in range(1, size):
        peer = (me + shift) % size
        out = lax.dynamic_slice_in_dim(pieces, peer * group, group, 0).astype(BF16)
        mine = mine + send(out, shift).astype(F32)
    return mine


def reduce_sketch(keep, sent, updated, owners, children):
    child, tile = lax.axis_index("child"), lax.axis_index("tile")
    chips = owners // 2
    pieces = keep.astype(F32) + to_partner(sent, owners).astype(F32)

    def over_child(x, shift):
        return lax.ppermute(
            x, "child", [(i, (i + shift) % children) for i in range(children)]
        )

    def over_chips(x, shift):
        return lax.ppermute(
            x, "tile", [(t, (t + 2 * shift) % owners) for t in range(owners)]
        )

    pieces = exchange_sum(pieces, children, child, over_child, chips)
    pieces, updated = lax.optimization_barrier((pieces, updated))
    return exchange_sum(pieces, chips, tile // 2, over_chips, 1)[0], updated


def shards(
    child_tiles,
    panel,
    bases,
    tile_blocks,
    tile_dest,
    tile_slot,
    parent_tiles,
    parent_blocks,
    sketch_test,
):
    owners, children = lax.axis_size("tile"), lax.axis_size("child")
    myself = lax.axis_index("tile")
    tile_count, order = child_tiles.shape[1], child_tiles.shape[2]

    block = project(panel[0], bases[0], order)
    parts, places = spread(block, owners)

    blocks = owners * panel.shape[1] // order
    pair_all = (tile_blocks[0, :, 0] * blocks + tile_blocks[0, :, 1]).reshape(owners, tile_count)
    dest_all = tile_dest[0, :, 0].reshape(owners, tile_count)
    own_pair = lax.dynamic_index_in_dim(pair_all, myself, 0, keepdims=False)
    own_dest = lax.dynamic_index_in_dim(dest_all, myself, 0, keepdims=False)
    ids = jnp.arange(tile_count, dtype=jnp.int32)
    lower = ids[None, :] < ids[:, None]
    before = (own_dest[:, None] == own_dest[None, :]) & lower
    place = own_dest * CAP + jnp.sum(before.astype(jnp.int32), axis=1)
    own_words = place * (blocks * blocks) + own_pair

    arrive = dest_all == myself
    earlier = jnp.sum((arrive[:, None, :] & lower[None]).astype(jnp.int32), axis=2)
    turn = jnp.arange(CAP, dtype=jnp.int32)
    matched = arrive[:, None, :] & (earlier[:, None, :] == turn[None, :, None])
    word_all = (tile_slot[0].reshape(owners, tile_count) + 1) * (blocks * blocks) + pair_all
    words = jnp.sum(jnp.where(matched, word_all[:, None, :], 0), axis=2).reshape(-1)
    pwords = parent_blocks[0].reshape(-1)

    cores, flipped = encode(child_tiles[0], parts, places, own_words, owners)
    rank = cores.shape[1]
    incoming = lax.all_to_all(
        cores.reshape(owners, CAP, rank, rank), "tile", split_axis=0, concat_axis=0, tiled=True
    ).reshape(cores.shape)
    width = sketch_test.shape[1]
    lanes = sketch_test.shape[0] // (owners * children)
    basis, west, vest, start = prepare(
        words, pwords, flipped, sketch_test.reshape(-1, order, width), parent_tiles[0], lanes
    )
    keep, sent = fold(words, pwords, incoming, west, vest, flipped, start)
    updated = update(words, parent_tiles[0], incoming, basis, flipped)
    sketch, updated = reduce_sketch(keep, sent, updated, owners, children)
    return updated[None], sketch.T


def solution(mesh):
    return jax.shard_map(
        shards,
        mesh=mesh,
        in_specs=(
            P("child", "tile", None, None),
            P("child", "tile", None),
            P("child", "tile", None),
            P("child", None, None),
            P("child", None, None),
            P("child", None),
            P("child", "tile", None, None),
            P("child", "tile", None),
            P(),
        ),
        out_specs=(P("child", "tile", None, None), P(("child", "tile"), None)),
        check_vma=False,
    )
```

time: 114 us -> 105 us (0.921)
  starting transfers between devices: 32.1 us -> 23 us
  Pallas kernels: 45.6 us -> 52.7 us
  waiting for transfers between devices: 22.9 us -> 18.7 us
  local copies, waits for them, and re-layouts: 7.14 us -> 4.41 us
    ppermute x6 -> x4, starting transfers between devices: 17.5 us -> 8.21 us  [along_chips(): lax.ppermute(x, 'tile', [(t, (t + 2 * shift) % owners) for t in range(own...]
    pallas_call x4, Pallas kernels: 43.6 us -> 50.7 us  [the longest x1 14.3 us: update(): pl.pallas_call(update_kernel, in_specs=[SCALARS, IN_HBM, ON_CHIP, ON_CHIP...]
    ppermute x3, waiting for transfers between devices: 5.47 us -> 0.01 us  [over_child(): lax.ppermute(x, 'child', [(i, (i + shift) % children) for i in range(chil...]
    ppermute x8 -> x6, waiting for transfers between devices: 2.22 us -> 2.73 us  [to_partner(): return lax.ppermute(x, 'tile', [(t, t ^ 1) for t in range(owners)])]
    ppermute x6 -> x4, waiting for transfers between devices: 12.1 us -> 11.9 us  [along_chips(): lax.ppermute(x, 'tile', [(t, (t + 2 * shift) % owners) for t in range(own...]
    unnamed x36 -> x27, local copies, waits for them, and re-layouts: 2.82 us -> 2.76 us
  transfers between devices with their start and end apart: 21 -> 17, of which waited for: 12 -> 9; matrix products, arithmetic and copies ran while one was open for 7% -> 5% of each run, Pallas kernels for 10% -> 26%
where the time goes in v2:
time: 105 us; the launch traced here: 104 us
  Pallas kernels  52.7 us (50%)
  starting transfers between devices  23 us (22%)
  waiting for transfers between devices  18.7 us (18%)
  other arithmetic  4.45 us (4%)
  local copies, waits for them, and re-layouts  4.41 us (4%)
    pallas_call x1, Pallas kernels, update(): pl.pallas_call(update_kernel, in_specs=[SCALARS, IN_HBM, ON_CHIP, ON_CHIP...  14.3 us
    pallas_call x1, Pallas kernels, prepare(): pl.pallas_call(prepare_kernel, in_specs=[SCALARS, SCALARS, ON_CHIP, ON_CH...  13.1 us
    ppermute x4, waiting for transfers between devices, along_chips(): lax.ppermute(x, 'tile', [(t, (t + 2 * shift) % owners) for t in range(own...  11.9 us
    pallas_call x1, Pallas kernels, encode(): pl.pallas_call(body, in_specs=[SCALARS, IN_HBM] + [ANYWHERE] * len(parts)...  11.8 us
    pallas_call x1, Pallas kernels, fold(): pl.pallas_call(fold_kernel, in_specs=[SCALARS, SCALARS] + [ON_CHIP] * 4 +...  11.5 us
    ppermute x4, starting transfers between devices, along_chips(): lax.ppermute(x, 'tile', [(t, (t + 2 * shift) % owners) for t in range(own...  8.21 us
    ppermute x3, starting transfers between devices, over_chips(): lax.ppermute(x, 'tile', [(t, (t + 2 * shift) % owners) for t in range(own...  5.34 us
    ppermute x3, starting transfers between devices, over_child(): lax.ppermute(x, 'child', [(i, (i + shift) % children) for i in range(chil...  4.46 us
  transfers between devices with their start and end apart: 17, of which 9 were waited for; matrix products, arithmetic and copies ran while one was open for 5% of the time, Pallas kernels for 26%

profile of v2, /device:TPU:0, one launch (start us, length us, event | category | flops | bytes accessed | tf_op | source)
XLA Modules:
  0.0 104.4 jit_solution(9501847858420661127)
XLA Ops:
  0.6 2.0 %project.1.refs_0_ = bf16[1,256,512]{2,1,0:T(8,128)(2,1)} custom-call(bf16[1,512,512]{2,1,0:T(8,128)(2,1)} %panel_ref.1, bf16[1,512,128]{2,1,0:T(8,128)(2,1)} %basis_ref.1), custom_call_target="tpu_custom_call" | custom-call | tf_op jit(solution)/shard_map/project/pallas_call | solution.py:34
  2.7 3.1 %collective-permute-start = (bf16[1,256,512]{2,1,0:T(8,128)(2,1)}, bf16[1,256,512]{2,1,0:T(8,128)(2,1)S(1)}, u32[]{:S(2)}, u32[]{:S(2)}) collective-permute-start(bf16[1,256,512]{2,1,0:T(8,128)(2,1)} %project.1.refs_0_), channel_id=1, source_target_pairs={{0,2},{1,3},{2,4},{3,5},{4,6},{5,7},{6,0},{7,1},{8,10},{9,11},{10,... | collective-permute-start | bytes 786440 | tf_op jit(solution)/shard_map/ppermute | solution.py:49
  5.7 2.0 %collective-permute-start.1 = (bf16[1,256,512]{2,1,0:T(8,128)(2,1)}, bf16[1,256,512]{2,1,0:T(8,128)(2,1)S(1)}, u32[]{:S(2)}, u32[]{:S(2)}) collective-permute-start(bf16[1,256,512]{2,1,0:T(8,128)(2,1)} %project.1.refs_0_), channel_id=1, source_target_pairs={{0,6},{1,7},{2,0},{3,1},{4,2},{5,3},{6,4},{7,5},{8,14},{9,15},{10,... | collective-permute-start | bytes 786440 | tf_op jit(solution)/shard_map/ppermute | solution.py:49
  7.7 0.0 collective-permute-start.4
  7.7 0.5 broadcast.55
  8.2 1.3 %reduce.11 = s32[128]{0:T(128)S(1)} reduce(s32[1,128,1]{1,2,0:T(1,128)} %param.13, s32[]{:T(128)} %broadcast.55), dimensions={0,2}, to_apply=%param.13.reduce_sub_computation.3 | reduce | bytes 1028 | tf_op args[4]
  9.6 0.1 reshape_squeeze.7
  9.7 5.5 %collective-permute-done.refs_1_ = bf16[1,256,512]{2,1,0:T(8,128)(2,1)S(1)} collective-permute-done((bf16[1,256,512]{2,1,0:T(8,128)(2,1)}, bf16[1,256,512]{2,1,0:T(8,128)(2,1)S(1)}, u32[]{:S(2)}, u32[]{:S(2)}) %collective-permute-start) | collective-permute-done | bytes 262176 | tf_op jit(solution)/shard_map/ppermute | solution.py:49
  15.2 0.1 collective-permute-start.2
  15.2 4.3 %collective-permute-done.1.refs_2_ = bf16[1,256,512]{2,1,0:T(8,128)(2,1)S(1)} collective-permute-done((bf16[1,256,512]{2,1,0:T(8,128)(2,1)}, bf16[1,256,512]{2,1,0:T(8,128)(2,1)S(1)}, u32[]{:S(2)}, u32[]{:S(2)}) %collective-permute-start.1) | collective-permute-done | bytes 262176 | tf_op jit(solution)/shard_map/ppermute | solution.py:49
  19.6 3.1 %collective-permute-start.3 = (bf16[1,128,512]{2,1,0:T(8,128)(2,1)S(1)}, bf16[1,128,512]{2,1,0:T(8,128)(2,1)S(1)}, u32[]{:S(2)}, u32[]{:S(2)}) collective-permute-start(bf16[1,128,512]{2,1,0:T(8,128)(2,1)S(1)} %slice.17), channel_id=1, source_target_pairs={{0,6},{1,7},{2,0},{3,1},{4,2},{5,3},{6,4},{7,5},{8,14},{9,15},{10,... | collective-permute-start | bytes 393224 | tf_op jit(solution)/shard_map/ppermute | solution.py:49
  22.6 0.2 convert_reduce_fusion.1
  22.8 0.1 collective-permute-start.5
  22.9 0.5 collective-permute-start.6
  23.4 0.8 add_reduce_fusion
  24.1 0.1 add.126
  24.2 0.5 collective-permute-done.2.refs_3_
  24.7 0.0 collective-permute-start.7
  24.8 1.5 %collective-permute-done.3.refs_4_ = bf16[1,128,512]{2,1,0:T(8,128)(2,1)S(1)} collective-permute-done((bf16[1,128,512]{2,1,0:T(8,128)(2,1)S(1)}, bf16[1,128,512]{2,1,0:T(8,128)(2,1)S(1)}, u32[]{:S(2)}, u32[]{:S(2)}) %collective-permute-start.3) | collective-permute-done | bytes 131104 | tf_op jit(solution)/shard_map/ppermute | solution.py:49
  26.3 0.0 collective-permute-start.8
  26.3 0.5 fusion.3.words
  26.8 0.0 collective-permute-done.4.refs_5_
  26.8 0.0 collective-permute-done.5.refs_6_
  26.8 0.0 copy-start.4
  26.9 0.0 collective-permute-done.6.refs_7_
  26.9 0.0 copy-start.5
  26.9 0.0 collective-permute-done.7.refs_8_
  26.9 0.7 collective-permute-done.8.refs_9_
  27.6 0.0 copy-done.1
  27.7 0.1 copy-done.5
  27.8 0.1 copy-done.8
  27.8 0.4 copy-done.9
  28.3 11.8 %encode.1 = (bf16[16,128,128]{2,1,0:T(8,128)(2,1)}, bf16[8,128,512]{2,1,0:T(8,128)(2,1)}) custom-call(s32[16]{0:T(128)} %fusion.3.words, bf16[16,512,512]{2,1,0:T(8,128)(2,1)} %bitcast.21, bf16[1,256,512]{2,1,0:T(8,128)(2,1)} %project.1.refs_0_, bf16[1,256,512]{2,1,0:T(8,128)(2,1)} %copy-done.1, bf16[1,256,512]{2,1,0:T(8,128)(2,1)} %copy-done.2, ...), custom_call_target="tpu_custom_call" | custom-call | tf_op jit(solution)/shard_map/encode/pallas_call | solution.py:153
  40.1 4.4 %all-to-all-start = ((bf16[8,2,128,128]{3,2,1,0:T(8,128)(2,1)}), bf16[8,2,128,128]{3,2,1,0:T(8,128)(2,1)S(1)}, u32[]{:S(2)}, u32[]{:S(2)}) async-start(bf16[8,2,128,128]{3,2,1,0:T(8,128)(2,1)} %bitcast.26), calls=%async_computation | async-start | bytes 1048576 | tf_op jit(solution)/shard_map/all_to_all | solution.py:428
  44.5 0.1 mul.45
  44.6 0.2 convert_reduce_fusion
  44.9 0.1 select_reduce_fusion
  45.0 0.1 copy.15
  45.1 0.6 reshape.63.words
  45.7 0.1 copy.16
  45.8 0.6 reshape_squeeze.8.pwords
  46.4 13.1 %prepare.1 = (bf16[8,512,128]{2,1,0:T(8,128)(2,1)}, bf16[16,128,128]{2,1,0:T(8,128)(2,1)}, bf16[16,128,128]{2,1,0:T(8,128)(2,1)}, f32[32,128,128]{2,1,0:T(8,128)}) custom-call(s32[16]{0:T(128)} %reshape.63.words, s32[16]{0:T(128)} %reshape_squeeze.8.pwords, bf16[8,128,512]{2,1,0:T(8,128)(2,1)} %get-tuple-element.13.flip_ref, bf16[8,512,128]{2,1,0:T(8,128)(2,1)} %bitcast.25, ...), custom_call_target="tpu_custom_call" | custom-call | flops 1073741824 | bytes 4194304 | tf_op jit(solution)/shard_map/prepare/pallas_call | solution.py:229
  59.4 0.4 all-to-all-done
  59.8 0.8 copy-done
  60.6 11.5 %fold.1 = (bf16[16,128,128]{2,1,0:T(8,128)(2,1)}, bf16[16,128,128]{2,1,0:T(8,128)(2,1)}) custom-call(s32[16]{0:T(128)} %reshape.63.words, s32[16]{0:T(128)} %reshape_squeeze.8.pwords, bf16[16,128,128]{2,1,0:T(8,128)(2,1)} %bitcast.22, bf16[16,128,128]{2,1,0:T(8,128)(2,1)} %get-tuple-element.14.west, bf16[16,128,128]{2,1,0:T(8,128)(2,1)} %get-tuple-element.15.vest, ...), custom_call_target="tpu_custom_call" | custom-call | tf_op jit(solution)/shard_map/fold/pallas_call | solution.py:284
  72.2 0.1 collective-permute-start.9
  72.4 2.0 %collective-permute-done.9 = bf16[16,128,128]{2,1,0:T(8,128)(2,1)S(1)} collective-permute-done((bf16[16,128,128]{2,1,0:T(8,128)(2,1)}, bf16[16,128,128]{2,1,0:T(8,128)(2,1)S(1)}, u32[]{:S(2)}, u32[]{:S(2)}) %collective-permute-start.9) | collective-permute-done | bytes 524320 | tf_op jit(solution)/shard_map/ppermute | solution.py:53
  74.4 1.2 %convert_add_fusion = f32[16,128,128]{2,1,0:T(8,128)S(1)} fusion(bf16[16,128,128]{2,1,0:T(8,128)(2,1)S(1)} %collective-permute-done.9, bf16[16,128,128]{2,1,0:T(8,128)(2,1)} %get-tuple-element.17), kind=kLoop, calls=%fused_computation | loop fusion | flops 786432 | bytes 2097152 | tf_op jit(solution)/shard_map/add | solution.py:372
  75.5 0.1 dynamic-slice_convert_fusion.2
  75.6 2.5 %collective-permute-start.12 = (bf16[4,128,128]{2,1,0:T(8,128)(2,1)S(1)}, bf16[4,128,128]{2,1,0:T(8,128)(2,1)S(1)}, u32[]{:S(2)}, u32[]{:S(2)}) collective-permute-start(bf16[4,128,128]{2,1,0:T(8,128)(2,1)S(1)} %get-tuple-element.29), channel_id=1, source_target_pairs={{0,24},{8,0},{16,8},{24,16},{1,25},{9,1},{17,9},{25,17},{2,26},{10... | collective-permute-start | bytes 393224 | tf_op jit(solution)/shard_map/ppermute | solution.py:375
  78.1 1.9 %collective-permute-start.11 = (bf16[4,128,128]{2,1,0:T(8,128)(2,1)S(1)}, bf16[4,128,128]{2,1,0:T(8,128)(2,1)S(1)}, u32[]{:S(2)}, u32[]{:S(2)}) collective-permute-start(bf16[4,128,128]{2,1,0:T(8,128)(2,1)S(1)} %get-tuple-element.30), channel_id=1, source_target_pairs={{0,16},{8,24},{16,0},{24,8},{1,17},{9,25},{17,1},{25,9},{2,18},{10... | collective-permute-start | bytes 393224 | tf_op jit(solution)/shard_map/ppermute | solution.py:375
  80.1 0.0 collective-permute-start.10
  80.1 14.3 %update.1 = bf16[8,512,512]{2,1,0:T(8,128)(2,1)} custom-call(s32[16]{0:T(128)} %reshape.63.words, bf16[8,512,512]{2,1,0:T(8,128)(2,1)} %bitcast.20, bf16[16,128,128]{2,1,0:T(8,128)(2,1)} %bitcast.23, bf16[8,512,128]{2,1,0:T(8,128)(2,1)} %get-tuple-element.19.basis_ref, bf16[8,128,512]{2,1,0:T(8,128)(2,1)} %get-tuple-element.13.flip_ref), custom_call_target="tpu_custom_call" | custom-call | flops 2147483648 | bytes 8388608 | tf_op jit(solution)/shard_map/update/pallas_call | solution.py:340
  94.4 0.0 collective-permute-done.12
  94.4 0.0 collective-permute-done.11
  94.4 0.0 collective-permute-done.10
  94.4 0.1 convert_add_fusion.1
  94.5 3.2 %collective-permute-start.15 = (bf16[1,128,128]{2,1,0:T(8,128)(2,1)S(1)}, bf16[1,128,128]{2,1,0:T(8,128)(2,1)S(1)}, u32[]{:S(2)}, u32[]{:S(2)}) collective-permute-start(bf16[1,128,128]{2,1,0:T(8,128)(2,1)S(1)} %get-tuple-element.32), channel_id=1, source_target_pairs={{0,6},{1,7},{2,0},{3,1},{4,2},{5,3},{6,4},{7,5},{8,14},{9,15},{10,... | collective-permute-start | bytes 98312 | tf_op jit(solution)/shard_map/ppermute | solution.py:380
  97.7 0.2 collective-permute-start.14
  97.9 1.9 %collective-permute-start.13 = (bf16[1,128,128]{2,1,0:T(8,128)(2,1)S(1)}, bf16[1,128,128]{2,1,0:T(8,128)(2,1)S(1)}, u32[]{:S(2)}, u32[]{:S(2)}) collective-permute-start(bf16[1,128,128]{2,1,0:T(8,128)(2,1)S(1)} %get-tuple-element.31), channel_id=1, source_target_pairs={{0,2},{1,3},{2,4},{3,5},{4,6},{5,7},{6,0},{7,1},{8,10},{9,11},{10,... | collective-permute-start | bytes 98312 | tf_op jit(solution)/shard_map/ppermute | solution.py:380
  99.8 0.0 collective-permute-done.15
  99.9 2.6 %collective-permute-done.14 = bf16[1,128,128]{2,1,0:T(8,128)(2,1)S(1)} collective-permute-done((bf16[1,128,128]{2,1,0:T(8,128)(2,1)S(1)}, bf16[1,128,128]{2,1,0:T(8,128)(2,1)S(1)}, u32[]{:S(2)}, u32[]{:S(2)}) %collective-permute-start.14) | collective-permute-done | bytes 32800 | tf_op jit(solution)/shard_map/ppermute | solution.py:380
  102.5 1.1 %collective-permute-done.13 = bf16[1,128,128]{2,1,0:T(8,128)(2,1)S(1)} collective-permute-done((bf16[1,128,128]{2,1,0:T(8,128)(2,1)S(1)}, bf16[1,128,128]{2,1,0:T(8,128)(2,1)S(1)}, u32[]{:S(2)}, u32[]{:S(2)}) %collective-permute-start.13) | collective-permute-done | bytes 32800 | tf_op jit(solution)/shard_map/ppermute | solution.py:380
  103.6 0.7 copy.17
  (26 shorter events, 0.1 us)
Async XLA Ops:
  2.7 12.5 %collective-permute-start = (bf16[1,256,512]{2,1,0:T(8,128)(2,1)}, bf16[1,256,512]{2,1,0:T(8,128)(2,1)S(1)}, u32[]{:S(2)}, u32[]{:S(2)}) collective-permute-start(bf16[1,256,512]{2,1,0:T(8,128)(2,1)} %project.1.refs_0_), channel_id=1, source_target_pairs={{0,2},{1,3},{2,4},{3,5},{4,6},{5,7},{6,0},{7,1},{8,10},{9,11},{10,... | collective-permute-start | bytes 786440 | tf_op jit(solution)/shard_map/ppermute | solution.py:49
  5.7 13.8 %collective-permute-start.1 = (bf16[1,256,512]{2,1,0:T(8,128)(2,1)}, bf16[1,256,512]{2,1,0:T(8,128)(2,1)S(1)}, u32[]{:S(2)}, u32[]{:S(2)}) collective-permute-start(bf16[1,256,512]{2,1,0:T(8,128)(2,1)} %project.1.refs_0_), channel_id=1, source_target_pairs={{0,6},{1,7},{2,0},{3,1},{4,2},{5,3},{6,4},{7,5},{8,14},{9,15},{10,... | collective-permute-start | bytes 786440 | tf_op jit(solution)/shard_map/ppermute | solution.py:49
  7.7 19.1 %collective-permute-start.4 = (bf16[1,256,512]{2,1,0:T(8,128)(2,1)}, bf16[1,256,512]{2,1,0:T(8,128)(2,1)S(1)}, u32[]{:S(2)}, u32[]{:S(2)}) collective-permute-start(bf16[1,256,512]{2,1,0:T(8,128)(2,1)} %project.1.refs_0_), channel_id=1, source_target_pairs={{0,1},{1,0},{2,3},{3,2},{4,5},{5,4},{6,7},{7,6},{8,9},{9,8},{10,11... | collective-permute-start | bytes 786440 | tf_op jit(solution)/shard_map/ppermute | solution.py:53
  15.1 12.5 %copy-start.1 = (bf16[1,256,512]{2,1,0:T(8,128)(2,1)}, bf16[1,256,512]{2,1,0:T(8,128)(2,1)S(1)}, u32[]{:S(2)}) copy-start(bf16[1,256,512]{2,1,0:T(8,128)(2,1)S(1)} %collective-permute-done.refs_1_) | copy-start | bytes 786436
  15.2 9.6 %collective-permute-start.2 = (bf16[1,128,512]{2,1,0:T(8,128)(2,1)S(1)}, bf16[1,128,512]{2,1,0:T(8,128)(2,1)S(1)}, u32[]{:S(2)}, u32[]{:S(2)}) collective-permute-start(bf16[1,128,512]{2,1,0:T(8,128)(2,1)S(1)} %slice.16), channel_id=1, source_target_pairs={{0,2},{1,3},{2,4},{3,5},{4,6},{5,7},{6,0},{7,1},{8,10},{9,11},{10,... | collective-permute-start | bytes 393224 | tf_op jit(solution)/shard_map/ppermute | solution.py:49
  19.5 8.1 %copy-start.2 = (bf16[1,256,512]{2,1,0:T(8,128)(2,1)}, bf16[1,256,512]{2,1,0:T(8,128)(2,1)S(1)}, u32[]{:S(2)}) copy-start(bf16[1,256,512]{2,1,0:T(8,128)(2,1)S(1)} %collective-permute-done.1.refs_2_) | copy-start | bytes 786436
  19.6 6.7 %collective-permute-start.3 = (bf16[1,128,512]{2,1,0:T(8,128)(2,1)S(1)}, bf16[1,128,512]{2,1,0:T(8,128)(2,1)S(1)}, u32[]{:S(2)}, u32[]{:S(2)}) collective-permute-start(bf16[1,128,512]{2,1,0:T(8,128)(2,1)S(1)} %slice.17), channel_id=1, source_target_pairs={{0,6},{1,7},{2,0},{3,1},{4,2},{5,3},{6,4},{7,5},{8,14},{9,15},{10,... | collective-permute-start | bytes 393224 | tf_op jit(solution)/shard_map/ppermute | solution.py:49
  22.8 4.0 %collective-permute-start.5 = (bf16[1,256,512]{2,1,0:T(8,128)(2,1)S(1)}, bf16[1,256,512]{2,1,0:T(8,128)(2,1)S(1)}, u32[]{:S(2)}, u32[]{:S(2)}) collective-permute-start(bf16[1,256,512]{2,1,0:T(8,128)(2,1)S(1)} %collective-permute-done.refs_1_), channel_id=1, source_target_pairs={{0,1},{1,0},{2,3},{3,2},{4,5},{5,4},{6,7},{7,6},{8,9},{9,8},{10,11... | collective-permute-start | bytes 786440 | tf_op jit(solution)/shard_map/ppermute | solution.py:53
  22.9 4.0 %collective-permute-start.6 = (bf16[1,256,512]{2,1,0:T(8,128)(2,1)S(1)}, bf16[1,256,512]{2,1,0:T(8,128)(2,1)S(1)}, u32[]{:S(2)}, u32[]{:S(2)}) collective-permute-start(bf16[1,256,512]{2,1,0:T(8,128)(2,1)S(1)} %collective-permute-done.1.refs_2_), channel_id=1, source_target_pairs={{0,1},{1,0},{2,3},{3,2},{4,5},{5,4},{6,7},{7,6},{8,9},{9,8},{10,11... | collective-permute-start | bytes 786440 | tf_op jit(solution)/shard_map/ppermute | solution.py:53
  24.7 2.9 %copy-start.6 = (bf16[1,128,512]{2,1,0:T(8,128)(2,1)}, bf16[1,128,512]{2,1,0:T(8,128)(2,1)S(1)}, u32[]{:S(2)}) copy-start(bf16[1,128,512]{2,1,0:T(8,128)(2,1)S(1)} %collective-permute-done.2.refs_3_) | copy-start | bytes 393220
  24.7 2.1 %collective-permute-start.7 = (bf16[1,128,512]{2,1,0:T(8,128)(2,1)S(1)}, bf16[1,128,512]{2,1,0:T(8,128)(2,1)S(1)}, u32[]{:S(2)}, u32[]{:S(2)}) collective-permute-start(bf16[1,128,512]{2,1,0:T(8,128)(2,1)S(1)} %collective-permute-done.2.refs_3_), channel_id=1, source_target_pairs={{0,1},{1,0},{2,3},{3,2},{4,5},{5,4},{6,7},{7,6},{8,9},{9,8},{10,11... | collective-permute-start | bytes 393224 | tf_op jit(solution)/shard_map/ppermute | solution.py:53
  26.3 1.4 %copy-start.7 = (bf16[1,128,512]{2,1,0:T(8,128)(2,1)}, bf16[1,128,512]{2,1,0:T(8,128)(2,1)S(1)}, u32[]{:S(2)}) copy-start(bf16[1,128,512]{2,1,0:T(8,128)(2,1)S(1)} %collective-permute-done.3.refs_4_) | copy-start | bytes 393220
  26.3 1.3 %collective-permute-start.8 = (bf16[1,128,512]{2,1,0:T(8,128)(2,1)S(1)}, bf16[1,128,512]{2,1,0:T(8,128)(2,1)S(1)}, u32[]{:S(2)}, u32[]{:S(2)}) collective-permute-start(bf16[1,128,512]{2,1,0:T(8,128)(2,1)S(1)} %collective-permute-done.3.refs_4_), channel_id=1, source_target_pairs={{0,1},{1,0},{2,3},{3,2},{4,5},{5,4},{6,7},{7,6},{8,9},{9,8},{10,11... | collective-permute-start | bytes 393224 | tf_op jit(solution)/shard_map/ppermute | solution.py:53
  26.8 0.8 copy-start.3
  26.8 0.8 copy-start.4
  26.9 0.9 copy-start.5
  26.9 0.9 copy-start.8
  27.6 0.6 copy-start.9
  28.3 16.2 %copy-start.11 = (s32[1,128]{1,0:T(1,128)S(1)}, s32[1,128]{1,0:T(1,128)}, u32[]{:S(2)}) copy-start(s32[1,128]{1,0:T(1,128)} %param.14) | copy-start | bytes 1540
  28.3 17.4 %copy-start.10 = (s32[1,8,2]{1,2,0:T(2,128)S(1)}, s32[1,8,2]{1,2,0:T(2,128)}, u32[]{:S(2)}) copy-start(s32[1,8,2]{1,2,0:T(2,128)} %param.16) | copy-start | bytes 196
  40.1 19.7 %all-to-all-start = ((bf16[8,2,128,128]{3,2,1,0:T(8,128)(2,1)}), bf16[8,2,128,128]{3,2,1,0:T(8,128)(2,1)S(1)}, u32[]{:S(2)}, u32[]{:S(2)}) async-start(bf16[8,2,128,128]{3,2,1,0:T(8,128)(2,1)} %bitcast.26), calls=%async_computation | async-start | bytes 1048576 | tf_op jit(solution)/shard_map/all_to_all | solution.py:428
  59.8 0.8 copy-start
  72.2 2.2 %collective-permute-start.9 = (bf16[16,128,128]{2,1,0:T(8,128)(2,1)}, bf16[16,128,128]{2,1,0:T(8,128)(2,1)S(1)}, u32[]{:S(2)}, u32[]{:S(2)}) collective-permute-start(bf16[16,128,128]{2,1,0:T(8,128)(2,1)} %get-tuple-element.18), channel_id=1, source_target_pairs={{0,1},{1,0},{2,3},{3,2},{4,5},{5,4},{6,7},{7,6},{8,9},{9,8},{10,11... | collective-permute-start | bytes 1572872 | tf_op jit(solution)/shard_map/ppermute | solution.py:53
  75.6 18.8 %collective-permute-start.12 = (bf16[4,128,128]{2,1,0:T(8,128)(2,1)S(1)}, bf16[4,128,128]{2,1,0:T(8,128)(2,1)S(1)}, u32[]{:S(2)}, u32[]{:S(2)}) collective-permute-start(bf16[4,128,128]{2,1,0:T(8,128)(2,1)S(1)} %get-tuple-element.29), channel_id=1, source_target_pairs={{0,24},{8,0},{16,8},{24,16},{1,25},{9,1},{17,9},{25,17},{2,26},{10... | collective-permute-start | bytes 393224 | tf_op jit(solution)/shard_map/ppermute | solution.py:375
  78.1 16.2 %collective-permute-start.11 = (bf16[4,128,128]{2,1,0:T(8,128)(2,1)S(1)}, bf16[4,128,128]{2,1,0:T(8,128)(2,1)S(1)}, u32[]{:S(2)}, u32[]{:S(2)}) collective-permute-start(bf16[4,128,128]{2,1,0:T(8,128)(2,1)S(1)} %get-tuple-element.30), channel_id=1, source_target_pairs={{0,16},{8,24},{16,0},{24,8},{1,17},{9,25},{17,1},{25,9},{2,18},{10... | collective-permute-start | bytes 393224 | tf_op jit(solution)/shard_map/ppermute | solution.py:375
  80.1 14.3 %collective-permute-start.10 = (bf16[4,128,128]{2,1,0:T(8,128)(2,1)S(1)}, bf16[4,128,128]{2,1,0:T(8,128)(2,1)S(1)}, u32[]{:S(2)}, u32[]{:S(2)}) collective-permute-start(bf16[4,128,128]{2,1,0:T(8,128)(2,1)S(1)} %get-tuple-element.28), channel_id=1, source_target_pairs={{0,8},{8,16},{16,24},{24,0},{1,9},{9,17},{17,25},{25,1},{2,10},{10... | collective-permute-start | bytes 393224 | tf_op jit(solution)/shard_map/ppermute | solution.py:375
  94.5 5.3 %collective-permute-start.15 = (bf16[1,128,128]{2,1,0:T(8,128)(2,1)S(1)}, bf16[1,128,128]{2,1,0:T(8,128)(2,1)S(1)}, u32[]{:S(2)}, u32[]{:S(2)}) collective-permute-start(bf16[1,128,128]{2,1,0:T(8,128)(2,1)S(1)} %get-tuple-element.32), channel_id=1, source_target_pairs={{0,6},{1,7},{2,0},{3,1},{4,2},{5,3},{6,4},{7,5},{8,14},{9,15},{10,... | collective-permute-start | bytes 98312 | tf_op jit(solution)/shard_map/ppermute | solution.py:380
  97.7 4.8 %collective-permute-start.14 = (bf16[1,128,128]{2,1,0:T(8,128)(2,1)S(1)}, bf16[1,128,128]{2,1,0:T(8,128)(2,1)S(1)}, u32[]{:S(2)}, u32[]{:S(2)}) collective-permute-start(bf16[1,128,128]{2,1,0:T(8,128)(2,1)S(1)} %get-tuple-element.33), channel_id=1, source_target_pairs={{0,4},{1,5},{2,6},{3,7},{4,0},{5,1},{6,2},{7,3},{8,12},{9,13},{10,... | collective-permute-start | bytes 98312 | tf_op jit(solution)/shard_map/ppermute | solution.py:380
  97.9 5.7 %collective-permute-start.13 = (bf16[1,128,128]{2,1,0:T(8,128)(2,1)S(1)}, bf16[1,128,128]{2,1,0:T(8,128)(2,1)S(1)}, u32[]{:S(2)}, u32[]{:S(2)}) collective-permute-start(bf16[1,128,128]{2,1,0:T(8,128)(2,1)S(1)} %get-tuple-element.31), channel_id=1, source_target_pairs={{0,2},{1,3},{2,4},{3,5},{4,6},{5,7},{6,0},{7,1},{8,10},{9,11},{10,... | collective-permute-start | bytes 98312 | tf_op jit(solution)/shard_map/ppermute | solution.py:380

commit v3 on v2

--- a/solution.py
+++ b/solution.py
@@ -68,6 +68,10 @@
     return arrays + [to_partner(x, owners) for x in arrays], places
 
 
+def grouped(count):
+    return 4 if count % 4 == 0 else 1
+
+
 def unpack(word, blocks):
     rest = word // blocks
     return rest // blocks, rest % blocks, word % blocks
@@ -80,9 +84,10 @@
 
 
 def encode_kernel(places, count, words, tiles, *refs):
-    parts = refs[:-10]
-    core_out, flip_out = refs[-10:-8]
-    held, staged, coded, tile_sems, part_sems, core_sems, flip_sem = refs[-8:-1]
+    parts = refs[:-11]
+    core_out, flip_out = refs[-11:-9]
+    held, staged, crossed, tile_sems, part_sems, core_sems, flip_sem = refs[-9:-2]
+    coded = refs[-2]
     blocks = held.shape[0]
     rank = core_out.shape[1]
     flip_copy = pltpu.make_async_copy(held.at[:, :rank], flip_out, flip_sem)
@@ -123,19 +128,37 @@
         copy.wait()
     flip_copy.start()
 
-    def one(q, carry):
-        place, row, col = unpack(words[q], blocks)
-        tile_copy(q).wait()
-        half = dot(held[row, :rank], staged[q]).astype(BF16)
-        encoded = lax.dot_general(half, held[col, :rank], NT, preferred_element_type=F32)
-        cross = lax.dot_general(
-            held[row, rank:], held[col, rank:], NT, preferred_element_type=F32
-        )
-        coded[q] = (encoded - cross).astype(BF16)
-        core_copy(q, place).start()
-        return carry
-
-    lax.fori_loop(0, count, one, 0, unroll=4)
+    group = grouped(count)
+
+    def cross(g, carry):
+        for q in [g * group + n for n in range(group)]:
+            _, row, col = unpack(words[q], blocks)
+            crossed[q] = lax.dot_general(
+                held[row, rank:], held[col, rank:], NT, preferred_element_type=F32
+            )
+        return carry
+
+    def one(g, carry):
+        tiles_now = [g * group + n for n in range(group)]
+        keys = [unpack(words[q], blocks) for q in tiles_now]
+        for q in tiles_now:
+            tile_copy(q).wait()
+        halves = [
+            dot(held[row, :rank], staged[q]).astype(BF16)
+            for q, (_, row, _) in zip(tiles_now, keys)
+        ]
+        cores = [
+            lax.dot_general(half, held[col, :rank], NT, preferred_element_type=F32)
+            for half, (_, _, col) in zip(halves, keys)
+        ]
+        for q, core in zip(tiles_now, cores):
+            coded[q] = (core - crossed[q]).astype(BF16)
+        for q, (place, _, _) in zip(tiles_now, keys):
+            core_copy(q, place).start()
+        return carry
+
+    lax.fori_loop(0, count // group, cross, 0)
+    lax.fori_loop(0, count // group, one, 0)
     for q in range(count):
         core_copy(q, 0).wait()
     flip_copy.wait()
@@ -157,11 +180,12 @@
         scratch_shapes=[
             pltpu.VMEM((blocks, 2 * rank, order), BF16),
             pltpu.VMEM(tiles.shape, BF16),
-            pltpu.VMEM((count, rank, rank), BF16),
+            pltpu.VMEM((count, rank, rank), F32),
             pltpu.SemaphoreType.DMA((count,)),
             pltpu.SemaphoreType.DMA((len(parts),)),
             pltpu.SemaphoreType.DMA((count,)),
             pltpu.SemaphoreType.DMA,
+            pltpu.VMEM((count, rank, rank), BF16),
         ],
         out_shape=[
             jax.ShapeDtypeStruct((slots, rank, rank), BF16),
@@ -204,22 +228,21 @@
 
     lax.fori_loop(0, count, parent, 0)
 
-    def item(s, carry):
-        slot, row, col = unpack(words[s], blocks)
-
-        @pl.when(slot > 0)
-        def _():
-            prow, pcol = pwords[2 * slot - 2], pwords[2 * slot - 1]
+    group = grouped(west.shape[0])
+
+    def item(g, carry):
+        for s in [g * group + n for n in range(group)]:
+            slot, row, col = unpack(words[s], blocks)
+            at = 2 * jnp.maximum(slot - 1, 0)
             west[s] = lax.dot_general(
-                turned[pcol], flip_ref[col], NT, preferred_element_type=F32
+                turned[pwords[at + 1]], flip_ref[col], NT, preferred_element_type=F32
             ).astype(BF16)
             vest[s] = lax.dot_general(
-                turned[prow], flip_ref[row], NT, preferred_element_type=F32
+                turned[pwords[at]], flip_ref[row], NT, preferred_element_type=F32
             ).astype(BF16)
-
-        return carry
-
-    lax.fori_loop(0, west.shape[0], item, 0)
+        return carry
+
+    lax.fori_loop(0, west.shape[0] // group, item, 0)
 
 
 def prepare(words, pwords, flipped, test, parents, lanes):
@@ -253,23 +276,25 @@
     base_copy.start()
     sketch[...] = jnp.zeros_like(sketch)
 
-    def item(s, carry):
-        slot, row, col = unpack(words[s], blocks)
-
-        @pl.when(slot > 0)
-        def _():
-            prow, pcol = pwords[2 * slot - 2], pwords[2 * slot - 1]
-            first = lax.dot_general(west[s], core_ref[s], NT, preferred_element_type=F32)
-            add_rows(sketch, prow, dot(first.astype(BF16), flip_ref[row]))
-
-            @pl.when(prow != pcol)
-            def _():
-                second = dot(vest[s], core_ref[s]).astype(BF16)
-                add_rows(sketch, pcol, dot(second, flip_ref[col]))
-
-        return carry
-
-    lax.fori_loop(0, core_ref.shape[0], item, 0)
+    group = grouped(core_ref.shape[0])
+
+    def item(g, carry):
+        targets, values = [], []
+        for s in [g * group + n for n in range(group)]:
+            slot, row, col = unpack(words[s], blocks)
+            at = 2 * jnp.maximum(slot - 1, 0)
+            prow, pcol = pwords[at], pwords[at + 1]
+            core = jnp.where(slot > 0, core_ref[s], jnp.zeros_like(core_ref[s]))
+            first = lax.dot_general(west[s], core, NT, preferred_element_type=F32)
+            second = jnp.where(prow != pcol, dot(vest[s], core), 0.0)
+            targets += [prow, pcol]
+            values += [(first.astype(BF16), row), (second.astype(BF16), col)]
+        values = [dot(value, flip_ref[block]) for value, block in values]
+        for target, value in zip(targets, values):
+            add_rows(sketch, target, value)
+        return carry
+
+    lax.fori_loop(0, core_ref.shape[0] // group, item, 0)
     base_copy.wait()
     core = lax.axis_index("tile") % 2
     for n in range(keep_ref.shape[0]):
@@ -297,64 +322,79 @@
 
 
 def update_kernel(
-    words, parents, core_ref, basis_ref, flip_ref, updated, held, total, made, in_sems, out_sems
+    low, words, parents, partial, core_ref, basis_ref, flip_ref, updated,
+    held, total, mixed, made, in_sems, out_sems,
 ):
-    count, blocks = held.shape[0], basis_ref.shape[0]
+    count, blocks, items = held.shape[0], basis_ref.shape[0], core_ref.shape[0]
+    group = grouped(items)
 
     def in_copy(p):
-        return pltpu.make_async_copy(parents.at[p], held.at[p], in_sems.at[p])
+        return pltpu.make_async_copy(parents.at[low + p], held.at[p], in_sems.at[p])
 
     def out_copy(p):
-        return pltpu.make_async_copy(made.at[p], updated.at[p], out_sems.at[p])
+        return pltpu.make_async_copy(made.at[p], updated.at[low + p], out_sems.at[p])
 
     for p in range(count):
         in_copy(p).start()
 
-    def one(p, carry):
+    def mix(g, carry):
+        for s in [g * group + n for n in range(group)]:
+            _, _, col = unpack(words[s], blocks)
+            mixed[s] = dot(core_ref[s], flip_ref[col]).astype(BF16)
+        return carry
+
+    lax.fori_loop(0, items // group, mix, 0)
+    for p in range(count):
         in_copy(p).wait()
-        total[...] = held[p].astype(F32)
-
-        def item(s, carry):
-            slot, row, col = unpack(words[s], blocks)
-
-            @pl.when(slot == p + 1)
-            def _():
-                left = dot(basis_ref[row], core_ref[s]).astype(BF16)
-                total[...] += dot(left, flip_ref[col])
-
-            return carry
-
-        lax.fori_loop(0, core_ref.shape[0], item, 0)
-        made[p] = total[...].astype(BF16)
+        total[p] = held[p].astype(F32)
+
+    def item(s, carry):
+        slot, row, _ = unpack(words[s], blocks)
+
+        @pl.when((slot > low) & (slot <= low + count))
+        def _():
+            total[slot - 1 - low] += dot(basis_ref[row], mixed[s])
+
+        return carry
+
+    lax.fori_loop(0, items, item, 0)
+    for p in range(count):
+        made[p] = total[p].astype(BF16)
         out_copy(p).start()
-        return carry
-
-    lax.fori_loop(0, count, one, 0)
     for p in range(count):
         out_copy(p).wait()
 
 
-def update(words, parents, cores, basis, flipped):
-    count, order, _ = parents.shape
+def update(low, count, words, parents, partial, cores, basis, flipped):
+    order = parents.shape[1]
     rank = basis.shape[2]
+    items = cores.shape[0]
+    first = partial is None
+    given = [] if first else [partial]
+
+    def body(words, parents, *refs):
+        update_kernel(low, words, parents, *([None] if first else []), *refs)
+
     return pl.pallas_call(
-        update_kernel,
-        in_specs=[SCALARS, IN_HBM, ON_CHIP, ON_CHIP, ON_CHIP],
+        body,
+        in_specs=[SCALARS, IN_HBM] + [IN_HBM] * len(given) + [ON_CHIP] * 3,
         out_specs=IN_HBM,
         scratch_shapes=[
-            pltpu.VMEM(parents.shape, BF16),
-            pltpu.VMEM((order, order), F32),
-            pltpu.VMEM(parents.shape, BF16),
+            pltpu.VMEM((count, order, order), BF16),
+            pltpu.VMEM((count, order, order), F32),
+            pltpu.VMEM((items, rank, order), BF16),
+            pltpu.VMEM((count, order, order), BF16),
             pltpu.SemaphoreType.DMA((count,)),
             pltpu.SemaphoreType.DMA((count,)),
         ],
         out_shape=jax.ShapeDtypeStruct(parents.shape, BF16),
+        input_output_aliases={} if first else {2: 0},
         compiler_params=params(),
         cost_estimate=pl.CostEstimate(
             flops=8 * parents.size * rank, bytes_accessed=4 * parents.size, transcendentals=0
         ),
         name="update",
-    )(words, parents, cores, basis, flipped)
+    )(words, parents, *given, cores, basis, flipped)
 
 
 def exchange_sum(pieces, size, me, send, group):
@@ -366,7 +406,7 @@
     return mine
 
 
-def reduce_sketch(keep, sent, updated, owners, children):
+def reduce_sketch(keep, sent, decode, cores, owners, children):
     child, tile = lax.axis_index("child"), lax.axis_index("tile")
     chips = owners // 2
     pieces = keep.astype(F32) + to_partner(sent, owners).astype(F32)
@@ -382,8 +422,8 @@
         )
 
     pieces = exchange_sum(pieces, children, child, over_child, chips)
-    pieces, updated = lax.optimization_barrier((pieces, updated))
-    return exchange_sum(pieces, chips, tile // 2, over_chips, 1)[0], updated
+    pieces, updated, cores = lax.optimization_barrier((pieces, decode(None, cores), cores))
+    return exchange_sum(pieces, chips, tile // 2, over_chips, 1)[0], decode(updated, cores)
 
 
 def shards(
@@ -434,8 +474,14 @@
         words, pwords, flipped, sketch_test.reshape(-1, order, width), parent_tiles[0], lanes
     )
     keep, sent = fold(words, pwords, incoming, west, vest, flipped, start)
-    updated = update(words, parent_tiles[0], incoming, basis, flipped)
-    sketch, updated = reduce_sketch(keep, sent, updated, owners, children)
+
+    def decode(partial, cores):
+        count = parent_tiles.shape[1]
+        early = count - count // 2
+        low, size = (0, early) if partial is None else (early, count - early)
+        return update(low, size, words, parent_tiles[0], partial, cores, basis, flipped)
+
+    sketch, updated = reduce_sketch(keep, sent, decode, incoming, owners, children)
     return updated[None], sketch.T
 
 

time: 105 us -> 91.7 us (0.87)
  Pallas kernels: 52.7 us -> 41.9 us
  starting transfers between devices: 23 us -> 21.6 us
  waiting for transfers between devices: 18.7 us -> 17.6 us
    pallas_call x1, Pallas kernels: 11.5 us -> 5.33 us  [fold(): pl.pallas_call(fold_kernel, in_specs=[SCALARS, SCALARS] + [ON_CHIP] * 4 +...]
    ppermute x3, waiting for transfers between devices: 3.76 us -> 0.01 us  [over_chips(): lax.ppermute(x, 'tile', [(t, (t + 2 * shift) % owners) for t in range(own...]
    pallas_call x1, Pallas kernels: 13.1 us -> 10.5 us  [prepare(): pl.pallas_call(prepare_kernel, in_specs=[SCALARS, SCALARS, ON_CHIP, ON_CH...]
    all_to_all x1, waiting for transfers between devices: 0.38 us -> 2.94 us  [shards(): lax.all_to_all(cores.reshape(owners, CAP, rank, rank), 'tile', split_axis...]
    pallas_call x1, Pallas kernels: 11.8 us -> 9.4 us  [encode(): pl.pallas_call(body, in_specs=[SCALARS, IN_HBM] + [ANYWHERE] * len(parts)...]
    ppermute x3, starting transfers between devices: 5.34 us -> 3.87 us  [over_chips(): lax.ppermute(x, 'tile', [(t, (t + 2 * shift) % owners) for t in range(own...]
    pallas_call x1 -> x2, Pallas kernels: 14.3 us -> 14.6 us  [update(): pl.pallas_call(body, in_specs=[SCALARS, IN_HBM] + [IN_HBM] * len(given) +...]
  transfers between devices with their start and end apart: 17 -> 17, of which waited for: 9 -> 7; matrix products, arithmetic and copies ran while one was open for 5% -> 6% of each run, Pallas kernels for 26% -> 28%
where the time goes in v3:
time: 91.7 us; the launch traced here: 91.1 us
  Pallas kernels  41.9 us (46%)
  starting transfers between devices  21.6 us (24%)
  waiting for transfers between devices  17.6 us (19%)
  local copies, waits for them, and re-layouts  4.58 us (5%)
  other arithmetic  4.46 us (5%)
  between operations  1.03 us (1%)
    pallas_call x2, Pallas kernels, update(): pl.pallas_call(body, in_specs=[SCALARS, IN_HBM] + [IN_HBM] * len(given) +...  14.6 us
    ppermute x4, waiting for transfers between devices, along_chips(): lax.ppermute(x, 'tile', [(t, (t + 2 * shift) % owners) for t in range(own...  11.9 us
    pallas_call x1, Pallas kernels, prepare(): pl.pallas_call(prepare_kernel, in_specs=[SCALARS, SCALARS, ON_CHIP, ON_CH...  10.5 us
    pallas_call x1, Pallas kernels, encode(): pl.pallas_call(body, in_specs=[SCALARS, IN_HBM] + [ANYWHERE] * len(parts)...  9.4 us
    ppermute x4, starting transfers between devices, along_chips(): lax.ppermute(x, 'tile', [(t, (t + 2 * shift) % owners) for t in range(own...  8.21 us
    pallas_call x1, Pallas kernels, fold(): pl.pallas_call(fold_kernel, in_specs=[SCALARS, SCALARS] + [ON_CHIP] * 4 +...  5.33 us
    ppermute x3, starting transfers between devices, over_child(): lax.ppermute(x, 'child', [(i, (i + shift) % children) for i in range(chil...  4.48 us
    all_to_all x1, starting transfers between devices, shards(): lax.all_to_all(cores.reshape(owners, CAP, rank, rank), 'tile', split_axis...  4.41 us
  transfers between devices with their start and end apart: 17, of which 7 were waited for; matrix products, arithmetic and copies ran while one was open for 6% of the time, Pallas kernels for 28%

profile of v3, /device:TPU:0, one launch (start us, length us, event | category | flops | bytes accessed | tf_op | source)
XLA Modules:
  0.0 91.1 jit_solution(3809324364781659593)
XLA Ops:
  0.6 2.0 %project.1.refs_0_ = bf16[1,256,512]{2,1,0:T(8,128)(2,1)} custom-call(bf16[1,512,512]{2,1,0:T(8,128)(2,1)} %panel_ref.1, bf16[1,512,128]{2,1,0:T(8,128)(2,1)} %basis_ref.1), custom_call_target="tpu_custom_call" | custom-call | tf_op jit(solution)/shard_map/project/pallas_call | solution.py:34
  2.7 3.1 %collective-permute-start = (bf16[1,256,512]{2,1,0:T(8,128)(2,1)}, bf16[1,256,512]{2,1,0:T(8,128)(2,1)S(1)}, u32[]{:S(2)}, u32[]{:S(2)}) collective-permute-start(bf16[1,256,512]{2,1,0:T(8,128)(2,1)} %project.1.refs_0_), channel_id=1, source_target_pairs={{0,2},{1,3},{2,4},{3,5},{4,6},{5,7},{6,0},{7,1},{8,10},{9,11},{10,... | collective-permute-start | bytes 786440 | tf_op jit(solution)/shard_map/ppermute | solution.py:49
  5.7 2.0 %collective-permute-start.1 = (bf16[1,256,512]{2,1,0:T(8,128)(2,1)}, bf16[1,256,512]{2,1,0:T(8,128)(2,1)S(1)}, u32[]{:S(2)}, u32[]{:S(2)}) collective-permute-start(bf16[1,256,512]{2,1,0:T(8,128)(2,1)} %project.1.refs_0_), channel_id=1, source_target_pairs={{0,6},{1,7},{2,0},{3,1},{4,2},{5,3},{6,4},{7,5},{8,14},{9,15},{10,... | collective-permute-start | bytes 786440 | tf_op jit(solution)/shard_map/ppermute | solution.py:49
  7.7 0.0 collective-permute-start.4
  7.7 0.5 broadcast.55
  8.2 1.3 %reduce.11 = s32[128]{0:T(128)S(1)} reduce(s32[1,128,1]{1,2,0:T(1,128)} %param.13, s32[]{:T(128)} %broadcast.55), dimensions={0,2}, to_apply=%param.13.reduce_sub_computation.3 | reduce | bytes 1028 | tf_op args[4]
  9.6 0.1 reshape_squeeze.7
  9.7 5.5 %collective-permute-done.refs_1_ = bf16[1,256,512]{2,1,0:T(8,128)(2,1)S(1)} collective-permute-done((bf16[1,256,512]{2,1,0:T(8,128)(2,1)}, bf16[1,256,512]{2,1,0:T(8,128)(2,1)S(1)}, u32[]{:S(2)}, u32[]{:S(2)}) %collective-permute-start) | collective-permute-done | bytes 262176 | tf_op jit(solution)/shard_map/ppermute | solution.py:49
  15.2 0.1 collective-permute-start.2
  15.2 4.3 %collective-permute-done.1.refs_2_ = bf16[1,256,512]{2,1,0:T(8,128)(2,1)S(1)} collective-permute-done((bf16[1,256,512]{2,1,0:T(8,128)(2,1)}, bf16[1,256,512]{2,1,0:T(8,128)(2,1)S(1)}, u32[]{:S(2)}, u32[]{:S(2)}) %collective-permute-start.1) | collective-permute-done | bytes 262176 | tf_op jit(solution)/shard_map/ppermute | solution.py:49
  19.6 3.1 %collective-permute-start.3 = (bf16[1,128,512]{2,1,0:T(8,128)(2,1)S(1)}, bf16[1,128,512]{2,1,0:T(8,128)(2,1)S(1)}, u32[]{:S(2)}, u32[]{:S(2)}) collective-permute-start(bf16[1,128,512]{2,1,0:T(8,128)(2,1)S(1)} %slice.17), channel_id=1, source_target_pairs={{0,6},{1,7},{2,0},{3,1},{4,2},{5,3},{6,4},{7,5},{8,14},{9,15},{10,... | collective-permute-start | bytes 393224 | tf_op jit(solution)/shard_map/ppermute | solution.py:49
  22.6 0.2 convert_reduce_fusion.1
  22.8 0.1 collective-permute-start.5
  22.9 0.5 collective-permute-start.6
  23.4 0.8 add_reduce_fusion
  24.1 0.1 add.126
  24.2 0.5 collective-permute-done.2.refs_3_
  24.7 0.0 collective-permute-start.7
  24.8 1.5 %collective-permute-done.3.refs_4_ = bf16[1,128,512]{2,1,0:T(8,128)(2,1)S(1)} collective-permute-done((bf16[1,128,512]{2,1,0:T(8,128)(2,1)S(1)}, bf16[1,128,512]{2,1,0:T(8,128)(2,1)S(1)}, u32[]{:S(2)}, u32[]{:S(2)}) %collective-permute-start.3) | collective-permute-done | bytes 131104 | tf_op jit(solution)/shard_map/ppermute | solution.py:49
  26.3 0.0 collective-permute-start.8
  26.3 0.5 fusion.3.words
  26.8 0.0 collective-permute-done.4.refs_5_
  26.8 0.0 collective-permute-done.7.refs_8_
  26.9 0.8 collective-permute-done.8.refs_9_
  27.6 0.0 collective-permute-done.5.refs_6_
  27.6 0.0 collective-permute-done.6.refs_7_
  27.7 0.6 copy-done.9
  28.3 0.1 copy-done.4
  28.4 0.1 copy-done.5
  28.5 9.4 %encode.1 = (bf16[16,128,128]{2,1,0:T(8,128)(2,1)}, bf16[8,128,512]{2,1,0:T(8,128)(2,1)}) custom-call(s32[16]{0:T(128)} %fusion.3.words, bf16[16,512,512]{2,1,0:T(8,128)(2,1)} %bitcast.26, bf16[1,256,512]{2,1,0:T(8,128)(2,1)} %project.1.refs_0_, bf16[1,256,512]{2,1,0:T(8,128)(2,1)} %copy-done.1, bf16[1,256,512]{2,1,0:T(8,128)(2,1)} %copy-done.2, ...), custom_call_target="tpu_custom_call" | custom-call | tf_op jit(solution)/shard_map/encode/pallas_call | solution.py:176
  37.9 4.4 %all-to-all-start = ((bf16[8,2,128,128]{3,2,1,0:T(8,128)(2,1)}), bf16[8,2,128,128]{3,2,1,0:T(8,128)(2,1)S(1)}, u32[]{:S(2)}, u32[]{:S(2)}) async-start(bf16[8,2,128,128]{3,2,1,0:T(8,128)(2,1)} %bitcast.28), calls=%async_computation | async-start | bytes 1048576 | tf_op jit(solution)/shard_map/all_to_all | solution.py:468
  42.3 0.0 copy-done.11
  42.3 0.1 mul.45
  42.4 0.2 convert_reduce_fusion
  42.7 0.1 select_reduce_fusion
  42.8 0.1 copy.16
  42.9 0.6 reshape.63.words
  43.5 0.0 copy-done.10
  43.5 0.1 copy.17
  43.6 0.6 reshape_squeeze.8.pwords
  44.2 10.5 %prepare.1 = (bf16[8,512,128]{2,1,0:T(8,128)(2,1)}, bf16[16,128,128]{2,1,0:T(8,128)(2,1)}, bf16[16,128,128]{2,1,0:T(8,128)(2,1)}, f32[32,128,128]{2,1,0:T(8,128)}) custom-call(s32[16]{0:T(128)} %reshape.63.words, s32[16]{0:T(128)} %reshape_squeeze.8.pwords, bf16[8,128,512]{2,1,0:T(8,128)(2,1)} %get-tuple-element.14.flip_ref.refs_2_.refs_3_, ...), custom_call_target="tpu_custom_call" | custom-call | flops 1073741824 | bytes 4194304 | tf_op jit(solution)/shard_map/prepare/pallas_call | solution.py:252
  54.7 2.9 %all-to-all-done = bf16[8,2,128,128]{3,2,1,0:T(8,128)(2,1)S(1)} async-done(((bf16[8,2,128,128]{3,2,1,0:T(8,128)(2,1)}), bf16[8,2,128,128]{3,2,1,0:T(8,128)(2,1)S(1)}, u32[]{:S(2)}, u32[]{:S(2)}) %all-to-all-start) | async-done | bytes 524320 | tf_op jit(solution)/shard_map/all_to_all | solution.py:468
  57.6 0.8 copy-done
  58.4 5.3 %fold.1 = (bf16[16,128,128]{2,1,0:T(8,128)(2,1)}, bf16[16,128,128]{2,1,0:T(8,128)(2,1)}) custom-call(s32[16]{0:T(128)} %reshape.63.words, s32[16]{0:T(128)} %reshape_squeeze.8.pwords, bf16[16,128,128]{2,1,0:T(8,128)(2,1)} %bitcast.23, bf16[16,128,128]{2,1,0:T(8,128)(2,1)} %get-tuple-element.15.west, bf16[16,128,128]{2,1,0:T(8,128)(2,1)} %get-tuple-element.16.vest, ...), custom_call_target="tpu_custom_call" | custom-call | tf_op jit(solution)/shard_map/fold/pallas_call | solution.py:309
  63.8 0.1 collective-permute-start.9
  64.0 2.0 %collective-permute-done.9 = bf16[16,128,128]{2,1,0:T(8,128)(2,1)S(1)} collective-permute-done((bf16[16,128,128]{2,1,0:T(8,128)(2,1)}, bf16[16,128,128]{2,1,0:T(8,128)(2,1)S(1)}, u32[]{:S(2)}, u32[]{:S(2)}) %collective-permute-start.9) | collective-permute-done | bytes 524320 | tf_op jit(solution)/shard_map/ppermute | solution.py:53
  66.0 1.2 %convert_add_fusion = f32[16,128,128]{2,1,0:T(8,128)S(1)} fusion(bf16[16,128,128]{2,1,0:T(8,128)(2,1)S(1)} %collective-permute-done.9, bf16[16,128,128]{2,1,0:T(8,128)(2,1)} %get-tuple-element.18), kind=kLoop, calls=%fused_computation | loop fusion | flops 786432 | bytes 2097152 | tf_op jit(solution)/shard_map/add | solution.py:412
  67.1 0.1 dynamic-slice_convert_fusion.2
  67.2 1.5 %collective-permute-start.10 = (bf16[4,128,128]{2,1,0:T(8,128)(2,1)S(1)}, bf16[4,128,128]{2,1,0:T(8,128)(2,1)S(1)}, u32[]{:S(2)}, u32[]{:S(2)}) collective-permute-start(bf16[4,128,128]{2,1,0:T(8,128)(2,1)S(1)} %get-tuple-element.30), channel_id=1, source_target_pairs={{0,8},{8,16},{16,24},{24,0},{1,9},{9,17},{17,25},{25,1},{2,10},{10... | collective-permute-start | bytes 393224 | tf_op jit(solution)/shard_map/ppermute | solution.py:415
  68.8 1.5 %collective-permute-start.11 = (bf16[4,128,128]{2,1,0:T(8,128)(2,1)S(1)}, bf16[4,128,128]{2,1,0:T(8,128)(2,1)S(1)}, u32[]{:S(2)}, u32[]{:S(2)}) collective-permute-start(bf16[4,128,128]{2,1,0:T(8,128)(2,1)S(1)} %get-tuple-element.32), channel_id=1, source_target_pairs={{0,16},{8,24},{16,0},{24,8},{1,17},{9,25},{17,1},{25,9},{2,18},{10... | collective-permute-start | bytes 393224 | tf_op jit(solution)/shard_map/ppermute | solution.py:415
  70.3 1.4 %collective-permute-start.12 = (bf16[4,128,128]{2,1,0:T(8,128)(2,1)S(1)}, bf16[4,128,128]{2,1,0:T(8,128)(2,1)S(1)}, u32[]{:S(2)}, u32[]{:S(2)}) collective-permute-start(bf16[4,128,128]{2,1,0:T(8,128)(2,1)S(1)} %get-tuple-element.31), channel_id=1, source_target_pairs={{0,24},{8,0},{16,8},{24,16},{1,25},{9,1},{17,9},{25,17},{2,26},{10... | collective-permute-start | bytes 393224 | tf_op jit(solution)/shard_map/ppermute | solution.py:415
  71.7 7.3 %update.2.refs_0_ = bf16[8,512,512]{2,1,0:T(8,128)(2,1)} custom-call(s32[16]{0:T(128)} %reshape.63.words, bf16[8,512,512]{2,1,0:T(8,128)(2,1)} %bitcast.20, bf16[16,128,128]{2,1,0:T(8,128)(2,1)} %bitcast.24, bf16[8,512,128]{2,1,0:T(8,128)(2,1)} %get-tuple-element.20.refs_1_.refs_2_, bf16[8,128,512]{2,1,0:T(8,128)(2,1)} %get-tuple-element.14.flip_ref.refs_2_.refs_3_), custom_call_target="tpu_custom_call" | custom-call | flops 2147483648 | bytes 8388608 | tf_op jit(solution)/shard_map/update/pallas_call | solution.py:378
  79.0 0.0 collective-permute-done.10
  79.0 0.0 collective-permute-done.11
  79.0 0.0 collective-permute-done.12
  79.1 0.1 convert_add_fusion.1
  79.2 0.1 collective-permute-start.13
  79.2 1.8 %collective-permute-start.14 = (bf16[1,128,128]{2,1,0:T(8,128)(2,1)S(1)}, bf16[1,128,128]{2,1,0:T(8,128)(2,1)S(1)}, u32[]{:S(2)}, u32[]{:S(2)}) collective-permute-start(bf16[1,128,128]{2,1,0:T(8,128)(2,1)S(1)} %get-tuple-element.35), channel_id=1, source_target_pairs={{0,4},{1,5},{2,6},{3,7},{4,0},{5,1},{6,2},{7,3},{8,12},{9,13},{10,... | collective-permute-start | bytes 98312 | tf_op jit(solution)/shard_map/ppermute | solution.py:420
  81.1 2.0 %collective-permute-start.15 = (bf16[1,128,128]{2,1,0:T(8,128)(2,1)S(1)}, bf16[1,128,128]{2,1,0:T(8,128)(2,1)S(1)}, u32[]{:S(2)}, u32[]{:S(2)}) collective-permute-start(bf16[1,128,128]{2,1,0:T(8,128)(2,1)S(1)} %get-tuple-element.34), channel_id=1, source_target_pairs={{0,6},{1,7},{2,0},{3,1},{4,2},{5,3},{6,4},{7,5},{8,14},{9,15},{10,... | collective-permute-start | bytes 98312 | tf_op jit(solution)/shard_map/ppermute | solution.py:420
  83.0 7.3 %update.3 = bf16[8,512,512]{2,1,0:T(8,128)(2,1)} custom-call(s32[16]{0:T(128)} %reshape.63.words, bf16[8,512,512]{2,1,0:T(8,128)(2,1)} %bitcast.21, bf16[8,512,512]{2,1,0:T(8,128)(2,1)} %update.2.refs_0_, bf16[16,128,128]{2,1,0:T(8,128)(2,1)} %bitcast.25, bf16[8,512,128]{2,1,0:T(8,128)(2,1)} %get-tuple-element.20.refs_1_.refs_2_, ...), custom_call_target="tpu_custom_call", output_to_operand_aliasing={{}: (2, {})} | custom-call | flops 2147483648 | bytes 8388608 | tf_op jit(solution)/shard_map/update/pallas_call | solution.py:378
  90.4 0.0 collective-permute-done.13
  90.4 0.0 collective-permute-done.14
  90.4 0.0 collective-permute-done.15
  90.4 0.7 copy.18
  (27 shorter events, 0.1 us)
Async XLA Ops:
  2.7 12.5 %collective-permute-start = (bf16[1,256,512]{2,1,0:T(8,128)(2,1)}, bf16[1,256,512]{2,1,0:T(8,128)(2,1)S(1)}, u32[]{:S(2)}, u32[]{:S(2)}) collective-permute-start(bf16[1,256,512]{2,1,0:T(8,128)(2,1)} %project.1.refs_0_), channel_id=1, source_target_pairs={{0,2},{1,3},{2,4},{3,5},{4,6},{5,7},{6,0},{7,1},{8,10},{9,11},{10,... | collective-permute-start | bytes 786440 | tf_op jit(solution)/shard_map/ppermute | solution.py:49
  5.7 13.8 %collective-permute-start.1 = (bf16[1,256,512]{2,1,0:T(8,128)(2,1)}, bf16[1,256,512]{2,1,0:T(8,128)(2,1)S(1)}, u32[]{:S(2)}, u32[]{:S(2)}) collective-permute-start(bf16[1,256,512]{2,1,0:T(8,128)(2,1)} %project.1.refs_0_), channel_id=1, source_target_pairs={{0,6},{1,7},{2,0},{3,1},{4,2},{5,3},{6,4},{7,5},{8,14},{9,15},{10,... | collective-permute-start | bytes 786440 | tf_op jit(solution)/shard_map/ppermute | solution.py:49
  7.7 19.1 %collective-permute-start.4 = (bf16[1,256,512]{2,1,0:T(8,128)(2,1)}, bf16[1,256,512]{2,1,0:T(8,128)(2,1)S(1)}, u32[]{:S(2)}, u32[]{:S(2)}) collective-permute-start(bf16[1,256,512]{2,1,0:T(8,128)(2,1)} %project.1.refs_0_), channel_id=1, source_target_pairs={{0,1},{1,0},{2,3},{3,2},{4,5},{5,4},{6,7},{7,6},{8,9},{9,8},{10,11... | collective-permute-start | bytes 786440 | tf_op jit(solution)/shard_map/ppermute | solution.py:53
  15.1 12.5 %copy-start.1 = (bf16[1,256,512]{2,1,0:T(8,128)(2,1)}, bf16[1,256,512]{2,1,0:T(8,128)(2,1)S(1)}, u32[]{:S(2)}) copy-start(bf16[1,256,512]{2,1,0:T(8,128)(2,1)S(1)} %collective-permute-done.refs_1_) | copy-start | bytes 786436
  15.2 9.6 %collective-permute-start.2 = (bf16[1,128,512]{2,1,0:T(8,128)(2,1)S(1)}, bf16[1,128,512]{2,1,0:T(8,128)(2,1)S(1)}, u32[]{:S(2)}, u32[]{:S(2)}) collective-permute-start(bf16[1,128,512]{2,1,0:T(8,128)(2,1)S(1)} %slice.16), channel_id=1, source_target_pairs={{0,2},{1,3},{2,4},{3,5},{4,6},{5,7},{6,0},{7,1},{8,10},{9,11},{10,... | collective-permute-start | bytes 393224 | tf_op jit(solution)/shard_map/ppermute | solution.py:49
  19.5 8.1 %copy-start.2 = (bf16[1,256,512]{2,1,0:T(8,128)(2,1)}, bf16[1,256,512]{2,1,0:T(8,128)(2,1)S(1)}, u32[]{:S(2)}) copy-start(bf16[1,256,512]{2,1,0:T(8,128)(2,1)S(1)} %collective-permute-done.1.refs_2_) | copy-start | bytes 786436
  19.6 6.7 %collective-permute-start.3 = (bf16[1,128,512]{2,1,0:T(8,128)(2,1)S(1)}, bf16[1,128,512]{2,1,0:T(8,128)(2,1)S(1)}, u32[]{:S(2)}, u32[]{:S(2)}) collective-permute-start(bf16[1,128,512]{2,1,0:T(8,128)(2,1)S(1)} %slice.17), channel_id=1, source_target_pairs={{0,6},{1,7},{2,0},{3,1},{4,2},{5,3},{6,4},{7,5},{8,14},{9,15},{10,... | collective-permute-start | bytes 393224 | tf_op jit(solution)/shard_map/ppermute | solution.py:49
  22.8 4.8 %collective-permute-start.5 = (bf16[1,256,512]{2,1,0:T(8,128)(2,1)S(1)}, bf16[1,256,512]{2,1,0:T(8,128)(2,1)S(1)}, u32[]{:S(2)}, u32[]{:S(2)}) collective-permute-start(bf16[1,256,512]{2,1,0:T(8,128)(2,1)S(1)} %collective-permute-done.refs_1_), channel_id=1, source_target_pairs={{0,1},{1,0},{2,3},{3,2},{4,5},{5,4},{6,7},{7,6},{8,9},{9,8},{10,11... | collective-permute-start | bytes 786440 | tf_op jit(solution)/shard_map/ppermute | solution.py:53
  22.9 4.8 %collective-permute-start.6 = (bf16[1,256,512]{2,1,0:T(8,128)(2,1)S(1)}, bf16[1,256,512]{2,1,0:T(8,128)(2,1)S(1)}, u32[]{:S(2)}, u32[]{:S(2)}) collective-permute-start(bf16[1,256,512]{2,1,0:T(8,128)(2,1)S(1)} %collective-permute-done.1.refs_2_), channel_id=1, source_target_pairs={{0,1},{1,0},{2,3},{3,2},{4,5},{5,4},{6,7},{7,6},{8,9},{9,8},{10,11... | collective-permute-start | bytes 786440 | tf_op jit(solution)/shard_map/ppermute | solution.py:53
  24.7 2.9 %copy-start.6 = (bf16[1,128,512]{2,1,0:T(8,128)(2,1)}, bf16[1,128,512]{2,1,0:T(8,128)(2,1)S(1)}, u32[]{:S(2)}) copy-start(bf16[1,128,512]{2,1,0:T(8,128)(2,1)S(1)} %collective-permute-done.2.refs_3_) | copy-start | bytes 393220
  24.7 2.1 %collective-permute-start.7 = (bf16[1,128,512]{2,1,0:T(8,128)(2,1)S(1)}, bf16[1,128,512]{2,1,0:T(8,128)(2,1)S(1)}, u32[]{:S(2)}, u32[]{:S(2)}) collective-permute-start(bf16[1,128,512]{2,1,0:T(8,128)(2,1)S(1)} %collective-permute-done.2.refs_3_), channel_id=1, source_target_pairs={{0,1},{1,0},{2,3},{3,2},{4,5},{5,4},{6,7},{7,6},{8,9},{9,8},{10,11... | collective-permute-start | bytes 393224 | tf_op jit(solution)/shard_map/ppermute | solution.py:53
  26.3 1.4 %copy-start.7 = (bf16[1,128,512]{2,1,0:T(8,128)(2,1)}, bf16[1,128,512]{2,1,0:T(8,128)(2,1)S(1)}, u32[]{:S(2)}) copy-start(bf16[1,128,512]{2,1,0:T(8,128)(2,1)S(1)} %collective-permute-done.3.refs_4_) | copy-start | bytes 393220
  26.3 1.3 %collective-permute-start.8 = (bf16[1,128,512]{2,1,0:T(8,128)(2,1)S(1)}, bf16[1,128,512]{2,1,0:T(8,128)(2,1)S(1)}, u32[]{:S(2)}, u32[]{:S(2)}) collective-permute-start(bf16[1,128,512]{2,1,0:T(8,128)(2,1)S(1)} %collective-permute-done.3.refs_4_), channel_id=1, source_target_pairs={{0,1},{1,0},{2,3},{3,2},{4,5},{5,4},{6,7},{7,6},{8,9},{9,8},{10,11... | collective-permute-start | bytes 393224 | tf_op jit(solution)/shard_map/ppermute | solution.py:53
  26.8 0.9 copy-start.3
  26.8 0.9 copy-start.8
  27.6 0.6 copy-start.9
  27.6 0.8 copy-start.4
  27.6 0.8 copy-start.5
  28.5 13.8 %copy-start.11 = (s32[1,128]{1,0:T(1,128)S(1)}, s32[1,128]{1,0:T(1,128)}, u32[]{:S(2)}) copy-start(s32[1,128]{1,0:T(1,128)} %param.14) | copy-start | bytes 1540
  28.5 15.0 %copy-start.10 = (s32[1,8,2]{1,2,0:T(2,128)S(1)}, s32[1,8,2]{1,2,0:T(2,128)}, u32[]{:S(2)}) copy-start(s32[1,8,2]{1,2,0:T(2,128)} %param.16) | copy-start | bytes 196
  37.9 19.7 %all-to-all-start = ((bf16[8,2,128,128]{3,2,1,0:T(8,128)(2,1)}), bf16[8,2,128,128]{3,2,1,0:T(8,128)(2,1)S(1)}, u32[]{:S(2)}, u32[]{:S(2)}) async-start(bf16[8,2,128,128]{3,2,1,0:T(8,128)(2,1)} %bitcast.28), calls=%async_computation | async-start | bytes 1048576 | tf_op jit(solution)/shard_map/all_to_all | solution.py:468
  57.6 0.8 copy-start
  63.8 2.2 %collective-permute-start.9 = (bf16[16,128,128]{2,1,0:T(8,128)(2,1)}, bf16[16,128,128]{2,1,0:T(8,128)(2,1)S(1)}, u32[]{:S(2)}, u32[]{:S(2)}) collective-permute-start(bf16[16,128,128]{2,1,0:T(8,128)(2,1)} %get-tuple-element.19), channel_id=1, source_target_pairs={{0,1},{1,0},{2,3},{3,2},{4,5},{5,4},{6,7},{7,6},{8,9},{9,8},{10,11... | collective-permute-start | bytes 1572872 | tf_op jit(solution)/shard_map/ppermute | solution.py:53
  67.2 11.8 %collective-permute-start.10 = (bf16[4,128,128]{2,1,0:T(8,128)(2,1)S(1)}, bf16[4,128,128]{2,1,0:T(8,128)(2,1)S(1)}, u32[]{:S(2)}, u32[]{:S(2)}) collective-permute-start(bf16[4,128,128]{2,1,0:T(8,128)(2,1)S(1)} %get-tuple-element.30), channel_id=1, source_target_pairs={{0,8},{8,16},{16,24},{24,0},{1,9},{9,17},{17,25},{25,1},{2,10},{10... | collective-permute-start | bytes 393224 | tf_op jit(solution)/shard_map/ppermute | solution.py:415
  68.8 10.3 %collective-permute-start.11 = (bf16[4,128,128]{2,1,0:T(8,128)(2,1)S(1)}, bf16[4,128,128]{2,1,0:T(8,128)(2,1)S(1)}, u32[]{:S(2)}, u32[]{:S(2)}) collective-permute-start(bf16[4,128,128]{2,1,0:T(8,128)(2,1)S(1)} %get-tuple-element.32), channel_id=1, source_target_pairs={{0,16},{8,24},{16,0},{24,8},{1,17},{9,25},{17,1},{25,9},{2,18},{10... | collective-permute-start | bytes 393224 | tf_op jit(solution)/shard_map/ppermute | solution.py:415
  70.3 8.8 %collective-permute-start.12 = (bf16[4,128,128]{2,1,0:T(8,128)(2,1)S(1)}, bf16[4,128,128]{2,1,0:T(8,128)(2,1)S(1)}, u32[]{:S(2)}, u32[]{:S(2)}) collective-permute-start(bf16[4,128,128]{2,1,0:T(8,128)(2,1)S(1)} %get-tuple-element.31), channel_id=1, source_target_pairs={{0,24},{8,0},{16,8},{24,16},{1,25},{9,1},{17,9},{25,17},{2,26},{10... | collective-permute-start | bytes 393224 | tf_op jit(solution)/shard_map/ppermute | solution.py:415
  79.2 11.2 %collective-permute-start.13 = (bf16[1,128,128]{2,1,0:T(8,128)(2,1)S(1)}, bf16[1,128,128]{2,1,0:T(8,128)(2,1)S(1)}, u32[]{:S(2)}, u32[]{:S(2)}) collective-permute-start(bf16[1,128,128]{2,1,0:T(8,128)(2,1)S(1)} %get-tuple-element.33), channel_id=1, source_target_pairs={{0,2},{1,3},{2,4},{3,5},{4,6},{5,7},{6,0},{7,1},{8,10},{9,11},{10,... | collective-permute-start | bytes 98312 | tf_op jit(solution)/shard_map/ppermute | solution.py:420
  79.2 11.1 %collective-permute-start.14 = (bf16[1,128,128]{2,1,0:T(8,128)(2,1)S(1)}, bf16[1,128,128]{2,1,0:T(8,128)(2,1)S(1)}, u32[]{:S(2)}, u32[]{:S(2)}) collective-permute-start(bf16[1,128,128]{2,1,0:T(8,128)(2,1)S(1)} %get-tuple-element.35), channel_id=1, source_target_pairs={{0,4},{1,5},{2,6},{3,7},{4,0},{5,1},{6,2},{7,3},{8,12},{9,13},{10,... | collective-permute-start | bytes 98312 | tf_op jit(solution)/shard_map/ppermute | solution.py:420
  81.1 9.3 %collective-permute-start.15 = (bf16[1,128,128]{2,1,0:T(8,128)(2,1)S(1)}, bf16[1,128,128]{2,1,0:T(8,128)(2,1)S(1)}, u32[]{:S(2)}, u32[]{:S(2)}) collective-permute-start(bf16[1,128,128]{2,1,0:T(8,128)(2,1)S(1)} %get-tuple-element.34), channel_id=1, source_target_pairs={{0,6},{1,7},{2,0},{3,1},{4,2},{5,3},{6,4},{7,5},{8,14},{9,15},{10,... | collective-permute-start | bytes 98312 | tf_op jit(solution)/shard_map/ppermute | solution.py:420

commit v4 on v3

--- a/solution.py
+++ b/solution.py
@@ -8,6 +8,7 @@
 CAP = 2
 RING_OWNERS = 8
 VMEM_BYTES = 58 * 1024 * 1024
+STAGE_BYTES = 48 * 1024 * 1024
 F32 = jnp.float32
 BF16 = jnp.bfloat16
 NT = (((1,), (1,)), ((), ()))
@@ -17,8 +18,8 @@
     return jnp.dot(x, y, preferred_element_type=F32)
 
 
-def params():
-    return pltpu.CompilerParams(vmem_limit_bytes=VMEM_BYTES)
+def params(size=VMEM_BYTES):
+    return pltpu.CompilerParams(vmem_limit_bytes=size)
 
 
 def project_kernel(panel_ref, basis_ref, out_ref):
@@ -53,9 +54,9 @@
     return lax.ppermute(x, "tile", [(t, t ^ 1) for t in range(owners)])
 
 
-def spread(block, owners):
+def spread(block, tiles, owners):
     if owners > RING_OWNERS or owners % 4:
-        return [lax.all_gather(block, "tile", axis=0, tiled=True)], None
+        return [lax.all_gather(block, "tile", axis=0, tiled=True)], None, stage(tiles)
     far, half = owners // 4, block.shape[1] // 2
     arrays, places = [block], [(0, 0)]
     up, down = block, block
@@ -65,7 +66,7 @@
         up, down = along_chips(up, owners, 1), along_chips(down, owners, -1)
         arrays += [up, down]
         places += [(-step, 0), (step, half if step == far else 0)]
-    return arrays + [to_partner(x, owners) for x in arrays], places
+    return arrays + [to_partner(x, owners) for x in arrays], places, stage(tiles)
 
 
 def grouped(count):
@@ -83,10 +84,36 @@
 ON_CHIP = pl.BlockSpec(memory_space=pltpu.VMEM)
 
 
-def encode_kernel(places, count, words, tiles, *refs):
-    parts = refs[:-11]
-    core_out, flip_out = refs[-11:-9]
-    held, staged, crossed, tile_sems, part_sems, core_sems, flip_sem = refs[-9:-2]
+def stage_kernel(tiles, staged, sems):
+    copies = [
+        pltpu.make_async_copy(tiles.at[q], staged.at[q], sems.at[q])
+        for q in range(tiles.shape[0])
+    ]
+    for copy in copies:
+        copy.start()
+    for copy in copies:
+        copy.wait()
+
+
+def stage(tiles):
+    return pl.pallas_call(
+        stage_kernel,
+        in_specs=[IN_HBM],
+        out_specs=ON_CHIP,
+        scratch_shapes=[pltpu.SemaphoreType.DMA((tiles.shape[0],))],
+        out_shape=pltpu.VMEM(tiles.shape, BF16),
+        compiler_params=params(STAGE_BYTES),
+        cost_estimate=pl.CostEstimate(
+            flops=64 * tiles.size, bytes_accessed=4 * tiles.size, transcendentals=0
+        ),
+        name="stage",
+    )(tiles)
+
+
+def encode_kernel(places, count, words, staged, *refs):
+    parts = refs[:-9]
+    core_out, flip_out = refs[-9:-7]
+    held, crossed, part_sems, core_sems, flip_sem = refs[-7:-2]
     coded = refs[-2]
     blocks = held.shape[0]
     rank = core_out.shape[1]
@@ -113,17 +140,12 @@
             )
         return copies
 
-    def tile_copy(q):
-        return pltpu.make_async_copy(tiles.at[q], staged.at[q], tile_sems.at[q])
-
     def core_copy(q, place):
         return pltpu.make_async_copy(coded.at[q], core_out.at[place], core_sems.at[q])
 
     copies = part_copies()
     for copy in copies:
         copy.start()
-    for q in range(count):
-        tile_copy(q).start()
     for copy in copies:
         copy.wait()
     flip_copy.start()
@@ -141,8 +163,6 @@
     def one(g, carry):
         tiles_now = [g * group + n for n in range(group)]
         keys = [unpack(words[q], blocks) for q in tiles_now]
-        for q in tiles_now:
-            tile_copy(q).wait()
         halves = [
             dot(held[row, :rank], staged[q]).astype(BF16)
             for q, (_, row, _) in zip(tiles_now, keys)
@@ -170,18 +190,16 @@
     blocks = parts[0].shape[0] * (1 if places is None else owners)
     slots = owners * CAP
 
-    def body(words, tiles, *refs):
-        encode_kernel(places, count, words, tiles, *refs, None)
+    def body(words, staged, *refs):
+        encode_kernel(places, count, words, staged, *refs, None)
 
     return pl.pallas_call(
         body,
-        in_specs=[SCALARS, IN_HBM] + [ANYWHERE] * len(parts),
+        in_specs=[SCALARS, ON_CHIP] + [ANYWHERE] * len(parts),
         out_specs=[ANYWHERE, ANYWHERE],
         scratch_shapes=[
             pltpu.VMEM((blocks, 2 * rank, order), BF16),
-            pltpu.VMEM(tiles.shape, BF16),
             pltpu.VMEM((count, rank, rank), F32),
-            pltpu.SemaphoreType.DMA((count,)),
             pltpu.SemaphoreType.DMA((len(parts),)),
             pltpu.SemaphoreType.DMA((count,)),
             pltpu.SemaphoreType.DMA,
@@ -191,7 +209,7 @@
             jax.ShapeDtypeStruct((slots, rank, rank), BF16),
             jax.ShapeDtypeStruct((blocks, rank, order), BF16),
         ],
-        compiler_params=params(),
+        compiler_params=params(VMEM_BYTES // 2),
         name="encode",
     )(words, tiles, *parts)
 
@@ -260,7 +278,7 @@
             jax.ShapeDtypeStruct((items, width, rank), BF16),
             jax.ShapeDtypeStruct((tests * order // lanes, width, lanes), F32),
         ],
-        compiler_params=params(),
+        compiler_params=params(VMEM_BYTES),
         cost_estimate=pl.CostEstimate(
             flops=4 * parents.size * width, bytes_accessed=2 * parents.size, transcendentals=0
         ),
@@ -316,114 +334,127 @@
             pltpu.SemaphoreType.DMA,
         ],
         out_shape=[half, half],
-        compiler_params=params(),
+        compiler_params=params(VMEM_BYTES),
         name="fold",
     )(words, pwords, cores, west, vest, flipped, start)
 
 
 def update_kernel(
-    low, words, parents, partial, core_ref, basis_ref, flip_ref, updated,
-    held, total, mixed, made, in_sems, out_sems,
+    words, parents, core_in, flip_in, basis_in, updated,
+    cores, flips, basis, held, total, mixed, sems, in_sems, out_sems,
 ):
-    count, blocks, items = held.shape[0], basis_ref.shape[0], core_ref.shape[0]
+    count, blocks, items = held.shape[0], basis.shape[0], cores.shape[0]
     group = grouped(items)
+    loads = [
+        pltpu.make_async_copy(source, target, sems.at[n])
+        for n, (source, target) in enumerate(
+            ((core_in, cores), (flip_in, flips), (basis_in, basis))
+        )
+    ]
 
     def in_copy(p):
-        return pltpu.make_async_copy(parents.at[low + p], held.at[p], in_sems.at[p])
+        return pltpu.make_async_copy(parents.at[p], held.at[p], in_sems.at[p])
 
     def out_copy(p):
-        return pltpu.make_async_copy(made.at[p], updated.at[low + p], out_sems.at[p])
-
+        return pltpu.make_async_copy(held.at[p], updated.at[p], out_sems.at[p])
+
+    for load in loads:
+        load.start()
     for p in range(count):
         in_copy(p).start()
+    loads[0].wait()
+    loads[1].wait()
 
     def mix(g, carry):
         for s in [g * group + n for n in range(group)]:
             _, _, col = unpack(words[s], blocks)
-            mixed[s] = dot(core_ref[s], flip_ref[col]).astype(BF16)
+            mixed[s] = dot(cores[s], flips[col]).astype(BF16)
         return carry
 
     lax.fori_loop(0, items // group, mix, 0)
-    for p in range(count):
+    loads[2].wait()
+
+    def one(p, carry):
         in_copy(p).wait()
-        total[p] = held[p].astype(F32)
-
-    def item(s, carry):
-        slot, row, _ = unpack(words[s], blocks)
-
-        @pl.when((slot > low) & (slot <= low + count))
-        def _():
-            total[slot - 1 - low] += dot(basis_ref[row], mixed[s])
-
-        return carry
-
-    lax.fori_loop(0, items, item, 0)
-    for p in range(count):
-        made[p] = total[p].astype(BF16)
+        total[...] = held[p].astype(F32)
+
+        def item(s, carry):
+            slot, row, _ = unpack(words[s], blocks)
+
+            @pl.when(slot == p + 1)
+            def _():
+                total[...] += dot(basis[row], mixed[s])
+
+            return carry
+
+        lax.fori_loop(0, items, item, 0)
+        held[p] = total[...].astype(BF16)
         out_copy(p).start()
+        return carry
+
+    lax.fori_loop(0, count, one, 0)
     for p in range(count):
         out_copy(p).wait()
 
 
-def update(low, count, words, parents, partial, cores, basis, flipped):
-    order = parents.shape[1]
+def update(words, parents, cores, basis, flipped):
+    count, order, _ = parents.shape
     rank = basis.shape[2]
-    items = cores.shape[0]
-    first = partial is None
-    given = [] if first else [partial]
-
-    def body(words, parents, *refs):
-        update_kernel(low, words, parents, *([None] if first else []), *refs)
-
     return pl.pallas_call(
-        body,
-        in_specs=[SCALARS, IN_HBM] + [IN_HBM] * len(given) + [ON_CHIP] * 3,
+        update_kernel,
+        in_specs=[SCALARS, IN_HBM] + [ANYWHERE] * 3,
         out_specs=IN_HBM,
         scratch_shapes=[
-            pltpu.VMEM((count, order, order), BF16),
-            pltpu.VMEM((count, order, order), F32),
-            pltpu.VMEM((items, rank, order), BF16),
-            pltpu.VMEM((count, order, order), BF16),
+            pltpu.VMEM(cores.shape, BF16),
+            pltpu.VMEM(flipped.shape, BF16),
+            pltpu.VMEM(basis.shape, BF16),
+            pltpu.VMEM(parents.shape, BF16),
+            pltpu.VMEM((order, order), F32),
+            pltpu.VMEM((cores.shape[0], rank, order), BF16),
+            pltpu.SemaphoreType.DMA((3,)),
             pltpu.SemaphoreType.DMA((count,)),
             pltpu.SemaphoreType.DMA((count,)),
         ],
         out_shape=jax.ShapeDtypeStruct(parents.shape, BF16),
-        input_output_aliases={} if first else {2: 0},
         compiler_params=params(),
         cost_estimate=pl.CostEstimate(
             flops=8 * parents.size * rank, bytes_accessed=4 * parents.size, transcendentals=0
         ),
         name="update",
-    )(words, parents, *given, cores, basis, flipped)
+    )(words, parents, cores, flipped, basis)
+
+
+def partner(i, step, size):
+    return i ^ step if size & (size - 1) == 0 else (i + step) % size
 
 
 def exchange_sum(pieces, size, me, send, group):
     mine = lax.dynamic_slice_in_dim(pieces, me * group, group, 0)
     for shift in range(1, size):
-        peer = (me + shift) % size
+        peer = partner(me, shift, size)
         out = lax.dynamic_slice_in_dim(pieces, peer * group, group, 0).astype(BF16)
         mine = mine + send(out, shift).astype(F32)
     return mine
 
 
-def reduce_sketch(keep, sent, decode, cores, owners, children):
+def reduce_sketch(keep, sent, updated, owners, children):
     child, tile = lax.axis_index("child"), lax.axis_index("tile")
     chips = owners // 2
     pieces = keep.astype(F32) + to_partner(sent, owners).astype(F32)
 
     def over_child(x, shift):
         return lax.ppermute(
-            x, "child", [(i, (i + shift) % children) for i in range(children)]
+            x, "child", [(i, partner(i, shift, children)) for i in range(children)]
         )
 
     def over_chips(x, shift):
         return lax.ppermute(
-            x, "tile", [(t, (t + 2 * shift) % owners) for t in range(owners)]
+            x, "tile", [(t, 2 * partner(t // 2, shift, chips) + t % 2) for t in range(owners)]
         )
 
     pieces = exchange_sum(pieces, children, child, over_child, chips)
-    pieces, updated, cores = lax.optimization_barrier((pieces, decode(None, cores), cores))
-    return exchange_sum(pieces, chips, tile // 2, over_chips, 1)[0], decode(updated, cores)
+    pieces, updated = lax.optimization_barrier((pieces, updated))
+    return exchange_sum(pieces, chips, tile // 2, over_chips, 1)[0], updated
 
 
 def shards(
@@ -442,7 +473,7 @@
     tile_count, order = child_tiles.shape[1], child_tiles.shape[2]
 
     block = project(panel[0], bases[0], order)
-    parts, places = spread(block, owners)
+    parts, places, staged = spread(block, child_tiles[0], owners)
 
     blocks = owners * panel.shape[1] // order
     pair_all = (tile_blocks[0, :, 0] * blocks + tile_blocks[0, :, 1]).reshape(owners, tile_count)
@@ -463,7 +494,7 @@
     words = jnp.sum(jnp.where(matched, word_all[:, None, :], 0), axis=2).reshape(-1)
     pwords = parent_blocks[0].reshape(-1)
 
-    cores, flipped = encode(child_tiles[0], parts, places, own_words, owners)
+    cores, flipped = encode(staged, parts, places, own_words, owners)
     rank = cores.shape[1]
     incoming = lax.all_to_all(
         cores.reshape(owners, CAP, rank, rank), "tile", split_axis=0, concat_axis=0, tiled=True
@@ -474,14 +505,8 @@
         words, pwords, flipped, sketch_test.reshape(-1, order, width), parent_tiles[0], lanes
     )
     keep, sent = fold(words, pwords, incoming, west, vest, flipped, start)
-
-    def decode(partial, cores):
-        count = parent_tiles.shape[1]
-        early = count - count // 2
-        low, size = (0, early) if partial is None else (early, count - early)
-        return update(low, size, words, parent_tiles[0], partial, cores, basis, flipped)
-
-    sketch, updated = reduce_sketch(keep, sent, decode, incoming, owners, children)
+    updated = update(words, parent_tiles[0], incoming, basis, flipped)
+    sketch, updated = reduce_sketch(keep, sent, updated, owners, children)
     return updated[None], sketch.T
 
 

time: 91.7 us -> 89.8 us (0.979)
    ppermute x6, waiting for transfers between devices: 0.02 us -> 2.29 us  [the longest x3 2.28 us: over_chips(): lax.ppermute(x, 'tile', [(t, 2 * partner(t // 2, shift, chips) + t % 2) f...]
    ppermute x4, waiting for transfers between devices: 11.9 us -> 9.63 us  [along_chips(): lax.ppermute(x, 'tile', [(t, (t + 2 * shift) % owners) for t in range(own...]
    all_to_all x1, starting transfers between devices: 4.41 us -> 3.49 us  [shards(): lax.all_to_all(cores.reshape(owners, CAP, rank, rank), 'tile', split_axis...]
    unnamed x27 -> x13, local copies, waits for them, and re-layouts: 2.93 us -> 3.11 us
  transfers between devices with their start and end apart: 17 -> 17, of which waited for: 7 -> 8; matrix products, arithmetic and copies ran while one was open for 6% -> 5% of each run, Pallas kernels for 28% -> 31%
where the time goes in v4:
time: 89.8 us; the launch traced here: 89.4 us
  Pallas kernels  41 us (46%)
  starting transfers between devices  20.9 us (23%)
  waiting for transfers between devices  18 us (20%)
  local copies, waits for them, and re-layouts  4.82 us (5%)
  other arithmetic  3.92 us (4%)
  between operations  0.92 us (1%)
    pallas_call x1, Pallas kernels, update(): pl.pallas_call(update_kernel, in_specs=[SCALARS, IN_HBM] + [ANYWHERE] * 3...  13.7 us
    pallas_call x1, Pallas kernels, prepare(): pl.pallas_call(prepare_kernel, in_specs=[SCALARS, SCALARS, ON_CHIP, ON_CH...  10.3 us
    ppermute x4, waiting for transfers between devices, along_chips(): lax.ppermute(x, 'tile', [(t, (t + 2 * shift) % owners) for t in range(own...  9.63 us
    ppermute x4, starting transfers between devices, along_chips(): lax.ppermute(x, 'tile', [(t, (t + 2 * shift) % owners) for t in range(own...  8.21 us
    pallas_call x1, Pallas kernels, encode(): pl.pallas_call(body, in_specs=[SCALARS, ON_CHIP] + [ANYWHERE] * len(parts...  6.03 us
    pallas_call x1, Pallas kernels, fold(): pl.pallas_call(fold_kernel, in_specs=[SCALARS, SCALARS] + [ON_CHIP] * 4 +...  5.36 us
    ppermute x3, starting transfers between devices, over_chips(): lax.ppermute(x, 'tile', [(t, 2 * partner(t // 2, shift, chips) + t % 2) f...  4.45 us
    pallas_call x1, Pallas kernels, stage(): pl.pallas_call(stage_kernel, in_specs=[IN_HBM], out_specs=ON_CHIP, scratc...  3.55 us
  transfers between devices with their start and end apart: 17, of which 8 were waited for; matrix products, arithmetic and copies ran while one was open for 5% of the time, Pallas kernels for 31%

profile of v4, /device:TPU:0, one launch (start us, length us, event | category | flops | bytes accessed | tf_op | source)
XLA Modules:
  0.0 89.4 jit_solution(10304185214142672748)
XLA Ops:
  0.6 2.0 %project.1.refs_0_ = bf16[1,256,512]{2,1,0:T(8,128)(2,1)} custom-call(bf16[1,512,512]{2,1,0:T(8,128)(2,1)} %panel_ref.1, bf16[1,512,128]{2,1,0:T(8,128)(2,1)} %basis_ref.1), custom_call_target="tpu_custom_call" | custom-call | tf_op jit(solution)/shard_map/project/pallas_call | solution.py:35
  2.7 3.1 %collective-permute-start = (bf16[1,256,512]{2,1,0:T(8,128)(2,1)}, bf16[1,256,512]{2,1,0:T(8,128)(2,1)S(1)}, u32[]{:S(2)}, u32[]{:S(2)}) collective-permute-start(bf16[1,256,512]{2,1,0:T(8,128)(2,1)} %project.1.refs_0_), channel_id=1, source_target_pairs={{0,2},{1,3},{2,4},{3,5},{4,6},{5,7},{6,0},{7,1},{8,10},{9,11},{10,... | collective-permute-start | bytes 786440 | tf_op jit(solution)/shard_map/ppermute | solution.py:50
  5.7 2.0 %collective-permute-start.1 = (bf16[1,256,512]{2,1,0:T(8,128)(2,1)}, bf16[1,256,512]{2,1,0:T(8,128)(2,1)S(1)}, u32[]{:S(2)}, u32[]{:S(2)}) collective-permute-start(bf16[1,256,512]{2,1,0:T(8,128)(2,1)} %project.1.refs_0_), channel_id=1, source_target_pairs={{0,6},{1,7},{2,0},{3,1},{4,2},{5,3},{6,4},{7,5},{8,14},{9,15},{10,... | collective-permute-start | bytes 786440 | tf_op jit(solution)/shard_map/ppermute | solution.py:50
  7.7 0.0 collective-permute-start.4
  7.7 0.5 broadcast.49
  8.2 1.3 %reduce.11 = s32[128]{0:T(128)S(1)} reduce(s32[1,128,1]{1,2,0:T(1,128)} %param.13, s32[]{:T(128)} %broadcast.49), dimensions={0,2}, to_apply=%param.13.reduce_sub_computation.3 | reduce | bytes 1028 | tf_op args[4]
  9.6 0.1 reshape_squeeze.7
  9.7 0.2 convert_reduce_fusion.1
  9.8 5.3 %collective-permute-done.refs_1_ = bf16[1,256,512]{2,1,0:T(8,128)(2,1)S(1)} collective-permute-done((bf16[1,256,512]{2,1,0:T(8,128)(2,1)}, bf16[1,256,512]{2,1,0:T(8,128)(2,1)S(1)}, u32[]{:S(2)}, u32[]{:S(2)}) %collective-permute-start) | collective-permute-done | bytes 262176 | tf_op jit(solution)/shard_map/ppermute | solution.py:50
  15.2 0.1 collective-permute-start.2
  15.2 4.3 %collective-permute-done.1.refs_2_ = bf16[1,256,512]{2,1,0:T(8,128)(2,1)S(1)} collective-permute-done((bf16[1,256,512]{2,1,0:T(8,128)(2,1)}, bf16[1,256,512]{2,1,0:T(8,128)(2,1)S(1)}, u32[]{:S(2)}, u32[]{:S(2)}) %collective-permute-start.1) | collective-permute-done | bytes 262176 | tf_op jit(solution)/shard_map/ppermute | solution.py:50
  19.6 3.1 %collective-permute-start.3 = (bf16[1,128,512]{2,1,0:T(8,128)(2,1)S(1)}, bf16[1,128,512]{2,1,0:T(8,128)(2,1)S(1)}, u32[]{:S(2)}, u32[]{:S(2)}) collective-permute-start(bf16[1,128,512]{2,1,0:T(8,128)(2,1)S(1)} %slice.17), channel_id=1, source_target_pairs={{0,6},{1,7},{2,0},{3,1},{4,2},{5,3},{6,4},{7,5},{8,14},{9,15},{10,... | collective-permute-start | bytes 393224 | tf_op jit(solution)/shard_map/ppermute | solution.py:50
  22.6 0.0 collective-permute-start.5
  22.6 0.5 collective-permute-start.6
  23.1 0.8 add_reduce_fusion
  23.9 0.1 add.89
  24.0 3.6 %stage.1.staged = bf16[16,512,512]{2,1,0:T(8,128)(2,1)S(1)} custom-call(bf16[16,512,512]{2,1,0:T(8,128)(2,1)} %bitcast.21), custom_call_target="tpu_custom_call" | custom-call | flops 268435456 | bytes 16777216 | tf_op jit(solution)/shard_map/stage/pallas_call | solution.py:99
  27.6 0.0 collective-permute-done.2.refs_3_
  27.6 0.1 collective-permute-start.7
  27.6 0.0 collective-permute-done.3.refs_4_
  27.7 0.5 collective-permute-start.8
  28.2 0.0 copy-start.3
  28.2 0.0 collective-permute-done.4.refs_5_
  28.2 0.0 collective-permute-done.5.refs_6_
  28.2 0.0 collective-permute-done.6.refs_7_
  28.2 0.8 collective-permute-done.7.refs_8_
  29.0 0.2 collective-permute-done.8.refs_9_
  29.2 0.0 copy-done.1
  29.2 6.0 %encode.1 = (bf16[16,128,128]{2,1,0:T(8,128)(2,1)}, bf16[8,128,512]{2,1,0:T(8,128)(2,1)S(1)}) custom-call(s32[16]{0:T(128)S(1)} %fusion.3.words, bf16[16,512,512]{2,1,0:T(8,128)(2,1)S(1)} %stage.1.staged, bf16[1,256,512]{2,1,0:T(8,128)(2,1)S(1)} %copy-done.1, bf16[1,256,512]{2,1,0:T(8,128)(2,1)S(1)} %collective-permute-done.refs_1_, ...), custom_call_target="tpu_custom_call" | custom-call | tf_op jit(solution)/shard_map/encode/pallas_call | solution.py:196
  35.2 0.0 copy-start
  35.2 1.0 %copy-done = bf16[8,128,512]{2,1,0:T(8,128)(2,1)} copy-done((bf16[8,128,512]{2,1,0:T(8,128)(2,1)}, bf16[8,128,512]{2,1,0:T(8,128)(2,1)S(1)}, u32[]{:S(2)}) %copy-start) | copy-done | bytes 1048600
  36.2 3.5 %all-to-all-start = ((bf16[8,2,128,128]{3,2,1,0:T(8,128)(2,1)}), bf16[8,2,128,128]{3,2,1,0:T(8,128)(2,1)S(1)}, u32[]{:S(2)}, u32[]{:S(2)}) async-start(bf16[8,2,128,128]{3,2,1,0:T(8,128)(2,1)} %bitcast.3), calls=%async_computation | async-start | bytes 1048576 | tf_op jit(solution)/shard_map/all_to_all | solution.py:499
  39.7 0.0 copy-done.4
  39.7 0.1 mul.45
  39.8 0.2 convert_reduce_fusion
  40.0 0.1 select_reduce_fusion
  40.2 0.1 copy.15
  40.3 0.6 reshape.63.words
  40.9 0.0 copy-done.3
  40.9 0.1 copy.16
  41.0 0.7 reshape_squeeze.8.pwords
  41.6 10.3 %prepare.1 = (bf16[8,512,128]{2,1,0:T(8,128)(2,1)}, bf16[16,128,128]{2,1,0:T(8,128)(2,1)}, bf16[16,128,128]{2,1,0:T(8,128)(2,1)}, f32[32,128,128]{2,1,0:T(8,128)}) custom-call(s32[16]{0:T(128)} %reshape.63.words, s32[16]{0:T(128)} %reshape_squeeze.8.pwords, bf16[8,128,512]{2,1,0:T(8,128)(2,1)} %copy-done, bf16[8,512,128]{2,1,0:T(8,128)(2,1)} %bitcast.25, ...), custom_call_target="tpu_custom_call" | custom-call | flops 1073741824 | bytes 4194304 | tf_op jit(solution)/shard_map/prepare/pallas_call | solution.py:270
  51.9 3.0 %all-to-all-done = bf16[8,2,128,128]{3,2,1,0:T(8,128)(2,1)S(1)} async-done(((bf16[8,2,128,128]{3,2,1,0:T(8,128)(2,1)}), bf16[8,2,128,128]{3,2,1,0:T(8,128)(2,1)S(1)}, u32[]{:S(2)}, u32[]{:S(2)}) %all-to-all-start) | async-done | bytes 524320 | tf_op jit(solution)/shard_map/all_to_all | solution.py:499
  54.9 0.8 copy-done.2
  55.7 5.4 %fold.1 = (bf16[16,128,128]{2,1,0:T(8,128)(2,1)}, bf16[16,128,128]{2,1,0:T(8,128)(2,1)}) custom-call(s32[16]{0:T(128)} %reshape.63.words, s32[16]{0:T(128)} %reshape_squeeze.8.pwords, bf16[16,128,128]{2,1,0:T(8,128)(2,1)} %bitcast.22, bf16[16,128,128]{2,1,0:T(8,128)(2,1)} %get-tuple-element.14.west, bf16[16,128,128]{2,1,0:T(8,128)(2,1)} %get-tuple-element.15.vest, ...), custom_call_target="tpu_custom_call" | custom-call | tf_op jit(solution)/shard_map/fold/pallas_call | solution.py:327
  61.1 0.1 collective-permute-start.9
  61.2 2.1 %collective-permute-done.9 = bf16[16,128,128]{2,1,0:T(8,128)(2,1)S(1)} collective-permute-done((bf16[16,128,128]{2,1,0:T(8,128)(2,1)}, bf16[16,128,128]{2,1,0:T(8,128)(2,1)S(1)}, u32[]{:S(2)}, u32[]{:S(2)}) %collective-permute-start.9) | collective-permute-done | bytes 524320 | tf_op jit(solution)/shard_map/ppermute | solution.py:54
  63.3 1.2 %convert_add_fusion = f32[16,128,128]{2,1,0:T(8,128)S(1)} fusion(bf16[16,128,128]{2,1,0:T(8,128)(2,1)S(1)} %collective-permute-done.9, bf16[16,128,128]{2,1,0:T(8,128)(2,1)} %get-tuple-element.17), kind=kLoop, calls=%fused_computation | loop fusion | flops 786432 | bytes 2097152 | tf_op jit(solution)/shard_map/add | solution.py:443
  64.5 0.1 dynamic-slice_convert_fusion.2
  64.5 2.5 %collective-permute-start.12 = (bf16[4,128,128]{2,1,0:T(8,128)(2,1)S(1)}, bf16[4,128,128]{2,1,0:T(8,128)(2,1)S(1)}, u32[]{:S(2)}, u32[]{:S(2)}) collective-permute-start(bf16[4,128,128]{2,1,0:T(8,128)(2,1)S(1)} %get-tuple-element.29), channel_id=1, source_target_pairs={{0,24},{8,16},{16,8},{24,0},{1,25},{9,17},{17,9},{25,1},{2,26},{10... | collective-permute-start | bytes 393224 | tf_op jit(solution)/shard_map/ppermute | solution.py:446
  67.0 0.5 collective-permute-start.11
  67.6 0.5 collective-permute-start.10
  68.1 13.7 %update.1 = bf16[8,512,512]{2,1,0:T(8,128)(2,1)} custom-call(s32[16]{0:T(128)} %reshape.63.words, bf16[8,512,512]{2,1,0:T(8,128)(2,1)} %bitcast.20, bf16[16,128,128]{2,1,0:T(8,128)(2,1)} %bitcast.23, bf16[8,128,512]{2,1,0:T(8,128)(2,1)} %copy-done, bf16[8,512,128]{2,1,0:T(8,128)(2,1)} %get-tuple-element.19.basis_in), custom_call_target="tpu_custom_call" | custom-call | flops 2147483648 | bytes 8388608 | tf_op jit(solution)/shard_map/update/pallas_call | solution.py:403
  81.8 0.0 collective-permute-done.12
  81.8 0.0 collective-permute-done.11
  81.8 0.0 collective-permute-done.10
  81.8 0.1 convert_add_fusion.1
  82.0 1.5 %collective-permute-start.15 = (bf16[1,128,128]{2,1,0:T(8,128)(2,1)S(1)}, bf16[1,128,128]{2,1,0:T(8,128)(2,1)S(1)}, u32[]{:S(2)}, u32[]{:S(2)}) collective-permute-start(bf16[1,128,128]{2,1,0:T(8,128)(2,1)S(1)} %get-tuple-element.32), channel_id=1, source_target_pairs={{0,6},{1,7},{2,4},{3,5},{4,2},{5,3},{6,0},{7,1},{8,14},{9,15},{10,... | collective-permute-start | bytes 98312 | tf_op jit(solution)/shard_map/ppermute | solution.py:451
  83.4 0.0 collective-permute-start.14
  83.4 3.0 %collective-permute-start.13 = (bf16[1,128,128]{2,1,0:T(8,128)(2,1)S(1)}, bf16[1,128,128]{2,1,0:T(8,128)(2,1)S(1)}, u32[]{:S(2)}, u32[]{:S(2)}) collective-permute-start(bf16[1,128,128]{2,1,0:T(8,128)(2,1)S(1)} %get-tuple-element.31), channel_id=1, source_target_pairs={{0,2},{1,3},{2,0},{3,1},{4,6},{5,7},{6,4},{7,5},{8,10},{9,11},{10,... | collective-permute-start | bytes 98312 | tf_op jit(solution)/shard_map/ppermute | solution.py:451
  86.4 1.8 %collective-permute-done.15 = bf16[1,128,128]{2,1,0:T(8,128)(2,1)S(1)} collective-permute-done((bf16[1,128,128]{2,1,0:T(8,128)(2,1)S(1)}, bf16[1,128,128]{2,1,0:T(8,128)(2,1)S(1)}, u32[]{:S(2)}, u32[]{:S(2)}) %collective-permute-start.15) | collective-permute-done | bytes 32800 | tf_op jit(solution)/shard_map/ppermute | solution.py:451
  88.2 0.5 collective-permute-done.14
  88.7 0.0 collective-permute-done.13
  88.7 0.7 copy.17
  (13 shorter events, 0.1 us)
Async XLA Ops:
  2.7 12.5 %collective-permute-start = (bf16[1,256,512]{2,1,0:T(8,128)(2,1)}, bf16[1,256,512]{2,1,0:T(8,128)(2,1)S(1)}, u32[]{:S(2)}, u32[]{:S(2)}) collective-permute-start(bf16[1,256,512]{2,1,0:T(8,128)(2,1)} %project.1.refs_0_), channel_id=1, source_target_pairs={{0,2},{1,3},{2,4},{3,5},{4,6},{5,7},{6,0},{7,1},{8,10},{9,11},{10,... | collective-permute-start | bytes 786440 | tf_op jit(solution)/shard_map/ppermute | solution.py:50
  5.7 13.8 %collective-permute-start.1 = (bf16[1,256,512]{2,1,0:T(8,128)(2,1)}, bf16[1,256,512]{2,1,0:T(8,128)(2,1)S(1)}, u32[]{:S(2)}, u32[]{:S(2)}) collective-permute-start(bf16[1,256,512]{2,1,0:T(8,128)(2,1)} %project.1.refs_0_), channel_id=1, source_target_pairs={{0,6},{1,7},{2,0},{3,1},{4,2},{5,3},{6,4},{7,5},{8,14},{9,15},{10,... | collective-permute-start | bytes 786440 | tf_op jit(solution)/shard_map/ppermute | solution.py:50
  7.7 20.4 %collective-permute-start.4 = (bf16[1,256,512]{2,1,0:T(8,128)(2,1)}, bf16[1,256,512]{2,1,0:T(8,128)(2,1)S(1)}, u32[]{:S(2)}, u32[]{:S(2)}) collective-permute-start(bf16[1,256,512]{2,1,0:T(8,128)(2,1)} %project.1.refs_0_), channel_id=1, source_target_pairs={{0,1},{1,0},{2,3},{3,2},{4,5},{5,4},{6,7},{7,6},{8,9},{9,8},{10,11... | collective-permute-start | bytes 786440 | tf_op jit(solution)/shard_map/ppermute | solution.py:54
  15.2 12.4 %collective-permute-start.2 = (bf16[1,128,512]{2,1,0:T(8,128)(2,1)S(1)}, bf16[1,128,512]{2,1,0:T(8,128)(2,1)S(1)}, u32[]{:S(2)}, u32[]{:S(2)}) collective-permute-start(bf16[1,128,512]{2,1,0:T(8,128)(2,1)S(1)} %slice.16), channel_id=1, source_target_pairs={{0,2},{1,3},{2,4},{3,5},{4,6},{5,7},{6,0},{7,1},{8,10},{9,11},{10,... | collective-permute-start | bytes 393224 | tf_op jit(solution)/shard_map/ppermute | solution.py:50
  19.6 8.1 %collective-permute-start.3 = (bf16[1,128,512]{2,1,0:T(8,128)(2,1)S(1)}, bf16[1,128,512]{2,1,0:T(8,128)(2,1)S(1)}, u32[]{:S(2)}, u32[]{:S(2)}) collective-permute-start(bf16[1,128,512]{2,1,0:T(8,128)(2,1)S(1)} %slice.17), channel_id=1, source_target_pairs={{0,6},{1,7},{2,0},{3,1},{4,2},{5,3},{6,4},{7,5},{8,14},{9,15},{10,... | collective-permute-start | bytes 393224 | tf_op jit(solution)/shard_map/ppermute | solution.py:50
  22.6 5.6 %collective-permute-start.5 = (bf16[1,256,512]{2,1,0:T(8,128)(2,1)S(1)}, bf16[1,256,512]{2,1,0:T(8,128)(2,1)S(1)}, u32[]{:S(2)}, u32[]{:S(2)}) collective-permute-start(bf16[1,256,512]{2,1,0:T(8,128)(2,1)S(1)} %collective-permute-done.refs_1_), channel_id=1, source_target_pairs={{0,1},{1,0},{2,3},{3,2},{4,5},{5,4},{6,7},{7,6},{8,9},{9,8},{10,11... | collective-permute-start | bytes 786440 | tf_op jit(solution)/shard_map/ppermute | solution.py:54
  22.6 5.6 %collective-permute-start.6 = (bf16[1,256,512]{2,1,0:T(8,128)(2,1)S(1)}, bf16[1,256,512]{2,1,0:T(8,128)(2,1)S(1)}, u32[]{:S(2)}, u32[]{:S(2)}) collective-permute-start(bf16[1,256,512]{2,1,0:T(8,128)(2,1)S(1)} %collective-permute-done.1.refs_2_), channel_id=1, source_target_pairs={{0,1},{1,0},{2,3},{3,2},{4,5},{5,4},{6,7},{7,6},{8,9},{9,8},{10,11... | collective-permute-start | bytes 786440 | tf_op jit(solution)/shard_map/ppermute | solution.py:54
  24.0 5.2 %copy-start.1 = (bf16[1,256,512]{2,1,0:T(8,128)(2,1)S(1)}, bf16[1,256,512]{2,1,0:T(8,128)(2,1)}, u32[]{:S(2)}) copy-start(bf16[1,256,512]{2,1,0:T(8,128)(2,1)} %project.1.refs_0_) | copy-start | bytes 786436
  27.6 1.4 %collective-permute-start.7 = (bf16[1,128,512]{2,1,0:T(8,128)(2,1)S(1)}, bf16[1,128,512]{2,1,0:T(8,128)(2,1)S(1)}, u32[]{:S(2)}, u32[]{:S(2)}) collective-permute-start(bf16[1,128,512]{2,1,0:T(8,128)(2,1)S(1)} %collective-permute-done.2.refs_3_), channel_id=1, source_target_pairs={{0,1},{1,0},{2,3},{3,2},{4,5},{5,4},{6,7},{7,6},{8,9},{9,8},{10,11... | collective-permute-start | bytes 393224 | tf_op jit(solution)/shard_map/ppermute | solution.py:54
  27.7 1.5 %collective-permute-start.8 = (bf16[1,128,512]{2,1,0:T(8,128)(2,1)S(1)}, bf16[1,128,512]{2,1,0:T(8,128)(2,1)S(1)}, u32[]{:S(2)}, u32[]{:S(2)}) collective-permute-start(bf16[1,128,512]{2,1,0:T(8,128)(2,1)S(1)} %collective-permute-done.3.refs_4_), channel_id=1, source_target_pairs={{0,1},{1,0},{2,3},{3,2},{4,5},{5,4},{6,7},{7,6},{8,9},{9,8},{10,11... | collective-permute-start | bytes 393224 | tf_op jit(solution)/shard_map/ppermute | solution.py:54
  28.2 11.5 %copy-start.4 = (s32[1,128]{1,0:T(1,128)S(1)}, s32[1,128]{1,0:T(1,128)}, u32[]{:S(2)}) copy-start(s32[1,128]{1,0:T(1,128)} %param.14) | copy-start | bytes 1540
  28.2 12.7 %copy-start.3 = (s32[1,8,2]{1,2,0:T(2,128)S(1)}, s32[1,8,2]{1,2,0:T(2,128)}, u32[]{:S(2)}) copy-start(s32[1,8,2]{1,2,0:T(2,128)} %param.16) | copy-start | bytes 196
  35.2 1.0 %copy-start = (bf16[8,128,512]{2,1,0:T(8,128)(2,1)}, bf16[8,128,512]{2,1,0:T(8,128)(2,1)S(1)}, u32[]{:S(2)}) copy-start(bf16[8,128,512]{2,1,0:T(8,128)(2,1)S(1)} %get-tuple-element.13.flip_ref.flip_in) | copy-start | bytes 3145732
  36.2 18.8 %all-to-all-start = ((bf16[8,2,128,128]{3,2,1,0:T(8,128)(2,1)}), bf16[8,2,128,128]{3,2,1,0:T(8,128)(2,1)S(1)}, u32[]{:S(2)}, u32[]{:S(2)}) async-start(bf16[8,2,128,128]{3,2,1,0:T(8,128)(2,1)} %bitcast.3), calls=%async_computation | async-start | bytes 1048576 | tf_op jit(solution)/shard_map/all_to_all | solution.py:499
  54.9 0.8 copy-start.2
  61.1 2.2 %collective-permute-start.9 = (bf16[16,128,128]{2,1,0:T(8,128)(2,1)}, bf16[16,128,128]{2,1,0:T(8,128)(2,1)S(1)}, u32[]{:S(2)}, u32[]{:S(2)}) collective-permute-start(bf16[16,128,128]{2,1,0:T(8,128)(2,1)} %get-tuple-element.18), channel_id=1, source_target_pairs={{0,1},{1,0},{2,3},{3,2},{4,5},{5,4},{6,7},{7,6},{8,9},{9,8},{10,11... | collective-permute-start | bytes 1572872 | tf_op jit(solution)/shard_map/ppermute | solution.py:54
  64.5 17.3 %collective-permute-start.12 = (bf16[4,128,128]{2,1,0:T(8,128)(2,1)S(1)}, bf16[4,128,128]{2,1,0:T(8,128)(2,1)S(1)}, u32[]{:S(2)}, u32[]{:S(2)}) collective-permute-start(bf16[4,128,128]{2,1,0:T(8,128)(2,1)S(1)} %get-tuple-element.29), channel_id=1, source_target_pairs={{0,24},{8,16},{16,8},{24,0},{1,25},{9,17},{17,9},{25,1},{2,26},{10... | collective-permute-start | bytes 393224 | tf_op jit(solution)/shard_map/ppermute | solution.py:446
  67.0 14.8 %collective-permute-start.11 = (bf16[4,128,128]{2,1,0:T(8,128)(2,1)S(1)}, bf16[4,128,128]{2,1,0:T(8,128)(2,1)S(1)}, u32[]{:S(2)}, u32[]{:S(2)}) collective-permute-start(bf16[4,128,128]{2,1,0:T(8,128)(2,1)S(1)} %get-tuple-element.30), channel_id=1, source_target_pairs={{0,16},{8,24},{16,0},{24,8},{1,17},{9,25},{17,1},{25,9},{2,18},{10... | collective-permute-start | bytes 393224 | tf_op jit(solution)/shard_map/ppermute | solution.py:446
  67.6 14.3 %collective-permute-start.10 = (bf16[4,128,128]{2,1,0:T(8,128)(2,1)S(1)}, bf16[4,128,128]{2,1,0:T(8,128)(2,1)S(1)}, u32[]{:S(2)}, u32[]{:S(2)}) collective-permute-start(bf16[4,128,128]{2,1,0:T(8,128)(2,1)S(1)} %get-tuple-element.28), channel_id=1, source_target_pairs={{0,8},{8,0},{16,24},{24,16},{1,9},{9,1},{17,25},{25,17},{2,10},{10... | collective-permute-start | bytes 393224 | tf_op jit(solution)/shard_map/ppermute | solution.py:446
  82.0 6.2 %collective-permute-start.15 = (bf16[1,128,128]{2,1,0:T(8,128)(2,1)S(1)}, bf16[1,128,128]{2,1,0:T(8,128)(2,1)S(1)}, u32[]{:S(2)}, u32[]{:S(2)}) collective-permute-start(bf16[1,128,128]{2,1,0:T(8,128)(2,1)S(1)} %get-tuple-element.32), channel_id=1, source_target_pairs={{0,6},{1,7},{2,4},{3,5},{4,2},{5,3},{6,0},{7,1},{8,14},{9,15},{10,... | collective-permute-start | bytes 98312 | tf_op jit(solution)/shard_map/ppermute | solution.py:451
  83.4 5.3 %collective-permute-start.14 = (bf16[1,128,128]{2,1,0:T(8,128)(2,1)S(1)}, bf16[1,128,128]{2,1,0:T(8,128)(2,1)S(1)}, u32[]{:S(2)}, u32[]{:S(2)}) collective-permute-start(bf16[1,128,128]{2,1,0:T(8,128)(2,1)S(1)} %get-tuple-element.33), channel_id=1, source_target_pairs={{0,4},{1,5},{2,6},{3,7},{4,0},{5,1},{6,2},{7,3},{8,12},{9,13},{10,... | collective-permute-start | bytes 98312 | tf_op jit(solution)/shard_map/ppermute | solution.py:451
  83.4 5.3 %collective-permute-start.13 = (bf16[1,128,128]{2,1,0:T(8,128)(2,1)S(1)}, bf16[1,128,128]{2,1,0:T(8,128)(2,1)S(1)}, u32[]{:S(2)}, u32[]{:S(2)}) collective-permute-start(bf16[1,128,128]{2,1,0:T(8,128)(2,1)S(1)} %get-tuple-element.31), channel_id=1, source_target_pairs={{0,2},{1,3},{2,0},{3,1},{4,6},{5,7},{6,4},{7,5},{8,10},{9,11},{10,... | collective-permute-start | bytes 98312 | tf_op jit(solution)/shard_map/ppermute | solution.py:451

commit v5 on v4

--- a/solution.py
+++ b/solution.py
@@ -6,6 +6,7 @@
 from jax.sharding import PartitionSpec as P
 
 CAP = 2
+BITS = 10
 RING_OWNERS = 8
 VMEM_BYTES = 58 * 1024 * 1024
 STAGE_BYTES = 48 * 1024 * 1024
@@ -73,9 +74,13 @@
     return 4 if count % 4 == 0 else 1
 
 
-def unpack(word, blocks):
-    rest = word // blocks
-    return rest // blocks, rest % blocks, word % blocks
+def pack(place, row, col):
+    return (place << (2 * BITS)) | (row << BITS) | col
+
+
+def unpack(word):
+    low = (1 << BITS) - 1
+    return word >> (2 * BITS), (word >> BITS) & low, word & low
 
 
 SCALARS = pl.BlockSpec(memory_space=pltpu.SMEM)
@@ -115,7 +120,6 @@
     core_out, flip_out = refs[-9:-7]
     held, crossed, part_sems, core_sems, flip_sem = refs[-7:-2]
     coded = refs[-2]
-    blocks = held.shape[0]
     rank = core_out.shape[1]
     flip_copy = pltpu.make_async_copy(held.at[:, :rank], flip_out, flip_sem)
 
@@ -154,7 +158,7 @@
 
     def cross(g, carry):
         for q in [g * group + n for n in range(group)]:
-            _, row, col = unpack(words[q], blocks)
+            _, row, col = unpack(words[q])
             crossed[q] = lax.dot_general(
                 held[row, rank:], held[col, rank:], NT, preferred_element_type=F32
             )
@@ -162,7 +166,7 @@
 
     def one(g, carry):
         tiles_now = [g * group + n for n in range(group)]
-        keys = [unpack(words[q], blocks) for q in tiles_now]
+        keys = [unpack(words[q]) for q in tiles_now]
         halves = [
             dot(held[row, :rank], staged[q]).astype(BF16)
             for q, (_, row, _) in zip(tiles_now, keys)
@@ -207,7 +211,7 @@
         ],
         out_shape=[
             jax.ShapeDtypeStruct((slots, rank, rank), BF16),
-            jax.ShapeDtypeStruct((blocks, rank, order), BF16),
+            pltpu.HBM((blocks, rank, order), BF16),
         ],
         compiler_params=params(VMEM_BYTES // 2),
         name="encode",
@@ -250,7 +254,7 @@
 
     def item(g, carry):
         for s in [g * group + n for n in range(group)]:
-            slot, row, col = unpack(words[s], blocks)
+            slot, row, col = unpack(words[s])
             at = 2 * jnp.maximum(slot - 1, 0)
             west[s] = lax.dot_general(
                 turned[pwords[at + 1]], flip_ref[col], NT, preferred_element_type=F32
@@ -289,7 +293,6 @@
 def fold_kernel(
     words, pwords, core_ref, west, vest, flip_ref, start, keep_ref, send_ref, sketch, base, sem
 ):
-    blocks = flip_ref.shape[0]
     base_copy = pltpu.make_async_copy(start, base, sem)
     base_copy.start()
     sketch[...] = jnp.zeros_like(sketch)
@@ -299,7 +302,7 @@
     def item(g, carry):
         targets, values = [], []
         for s in [g * group + n for n in range(group)]:
-            slot, row, col = unpack(words[s], blocks)
+            slot, row, col = unpack(words[s])
             at = 2 * jnp.maximum(slot - 1, 0)
             prow, pcol = pwords[at], pwords[at + 1]
             core = jnp.where(slot > 0, core_ref[s], jnp.zeros_like(core_ref[s]))
@@ -340,10 +343,10 @@
 
 
 def update_kernel(
-    words, parents, core_in, flip_in, basis_in, updated,
+    low, words, parents, partial, core_in, flip_in, basis_in, updated,
     cores, flips, basis, held, total, mixed, sems, in_sems, out_sems,
 ):
-    count, blocks, items = held.shape[0], basis.shape[0], cores.shape[0]
+    count, items = held.shape[0], cores.shape[0]
     group = grouped(items)
     loads = [
         pltpu.make_async_copy(source, target, sems.at[n])
@@ -353,10 +356,10 @@
     ]
 
     def in_copy(p):
-        return pltpu.make_async_copy(parents.at[p], held.at[p], in_sems.at[p])
+        return pltpu.make_async_copy(parents.at[low + p], held.at[p], in_sems.at[p])
 
     def out_copy(p):
-        return pltpu.make_async_copy(held.at[p], updated.at[p], out_sems.at[p])
+        return pltpu.make_async_copy(held.at[p], updated.at[low + p], out_sems.at[p])
 
     for load in loads:
         load.start()
@@ -367,7 +370,7 @@
 
     def mix(g, carry):
         for s in [g * group + n for n in range(group)]:
-            _, _, col = unpack(words[s], blocks)
+            _, _, col = unpack(words[s])
             mixed[s] = dot(cores[s], flips[col]).astype(BF16)
         return carry
 
@@ -379,9 +382,9 @@
         total[...] = held[p].astype(F32)
 
         def item(s, carry):
-            slot, row, _ = unpack(words[s], blocks)
-
-            @pl.when(slot == p + 1)
+            slot, row, _ = unpack(words[s])
+
+            @pl.when(slot == low + p + 1)
             def _():
                 total[...] += dot(basis[row], mixed[s])
 
@@ -397,18 +400,24 @@
         out_copy(p).wait()
 
 
-def update(words, parents, cores, basis, flipped):
-    count, order, _ = parents.shape
+def update(low, count, words, parents, partial, cores, basis, flipped):
+    order = parents.shape[1]
     rank = basis.shape[2]
+    first = partial is None
+    given = [] if first else [partial]
+
+    def body(words, parents, *refs):
+        update_kernel(low, words, parents, *([None] if first else []), *refs)
+
     return pl.pallas_call(
-        update_kernel,
-        in_specs=[SCALARS, IN_HBM] + [ANYWHERE] * 3,
+        body,
+        in_specs=[SCALARS, IN_HBM] + [IN_HBM] * len(given) + [ANYWHERE] * 3,
         out_specs=IN_HBM,
         scratch_shapes=[
             pltpu.VMEM(cores.shape, BF16),
             pltpu.VMEM(flipped.shape, BF16),
             pltpu.VMEM(basis.shape, BF16),
-            pltpu.VMEM(parents.shape, BF16),
+            pltpu.VMEM((count, order, order), BF16),
             pltpu.VMEM((order, order), F32),
             pltpu.VMEM((cores.shape[0], rank, order), BF16),
             pltpu.SemaphoreType.DMA((3,)),
@@ -416,12 +425,13 @@
             pltpu.SemaphoreType.DMA((count,)),
         ],
         out_shape=jax.ShapeDtypeStruct(parents.shape, BF16),
+        input_output_aliases={} if first else {2: 0},
         compiler_params=params(),
         cost_estimate=pl.CostEstimate(
             flops=8 * parents.size * rank, bytes_accessed=4 * parents.size, transcendentals=0
         ),
         name="update",
-    )(words, parents, cores, flipped, basis)
+    )(words, parents, *given, cores, flipped, basis)
 
 
 def partner(i, step, size):
@@ -437,7 +447,7 @@
     return mine
 
 
-def reduce_sketch(keep, sent, updated, owners, children):
+def reduce_sketch(keep, sent, decode, cores, owners, children):
     child, tile = lax.axis_index("child"), lax.axis_index("tile")
     chips = owners // 2
     pieces = keep.astype(F32) + to_partner(sent, owners).astype(F32)
@@ -453,8 +463,8 @@
         )
 
     pieces = exchange_sum(pieces, children, child, over_child, chips)
-    pieces, updated = lax.optimization_barrier((pieces, updated))
-    return exchange_sum(pieces, chips, tile // 2, over_chips, 1)[0], updated
+    pieces, updated, cores = lax.optimization_barrier((pieces, decode(None, cores), cores))
+    return exchange_sum(pieces, chips, tile // 2, over_chips, 1)[0], decode(updated, cores)
 
 
 def shards(
@@ -475,8 +485,7 @@
     block = project(panel[0], bases[0], order)
     parts, places, staged = spread(block, child_tiles[0], owners)
 
-    blocks = owners * panel.shape[1] // order
-    pair_all = (tile_blocks[0, :, 0] * blocks + tile_blocks[0, :, 1]).reshape(owners, tile_count)
+    pair_all = pack(0, tile_blocks[0, :, 0], tile_blocks[0, :, 1]).reshape(owners, tile_count)
     dest_all = tile_dest[0, :, 0].reshape(owners, tile_count)
     own_pair = lax.dynamic_index_in_dim(pair_all, myself, 0, keepdims=False)
     own_dest = lax.dynamic_index_in_dim(dest_all, myself, 0, keepdims=False)
@@ -484,13 +493,13 @@
     lower = ids[None, :] < ids[:, None]
     before = (own_dest[:, None] == own_dest[None, :]) & lower
     place = own_dest * CAP + jnp.sum(before.astype(jnp.int32), axis=1)
-    own_words = place * (blocks * blocks) + own_pair
+    own_words = pack(place, 0, own_pair)
 
     arrive = dest_all == myself
     earlier = jnp.sum((arrive[:, None, :] & lower[None]).astype(jnp.int32), axis=2)
     turn = jnp.arange(CAP, dtype=jnp.int32)
     matched = arrive[:, None, :] & (earlier[:, None, :] == turn[None, :, None])
-    word_all = (tile_slot[0].reshape(owners, tile_count) + 1) * (blocks * blocks) + pair_all
+    word_all = pack(tile_slot[0].reshape(owners, tile_count) + 1, 0, pair_all)
     words = jnp.sum(jnp.where(matched, word_all[:, None, :], 0), axis=2).reshape(-1)
     pwords = parent_blocks[0].reshape(-1)
 
@@ -505,8 +514,14 @@
         words, pwords, flipped, sketch_test.reshape(-1, order, width), parent_tiles[0], lanes
     )
     keep, sent = fold(words, pwords, incoming, west, vest, flipped, start)
-    updated = update(words, parent_tiles[0], incoming, basis, flipped)
-    sketch, updated = reduce_sketch(keep, sent, updated, owners, children)
+
+    def decode(partial, cores):
+        count = parent_tiles.shape[1]
+        early = count - count * 3 // 8
+        low, size = (0, early) if partial is None else (early, count - early)
+        return update(low, size, words, parent_tiles[0], partial, cores, basis, flipped)
+
+    sketch, updated = reduce_sketch(keep, sent, decode, incoming, owners, children)
     return updated[None], sketch.T
 
 

time: 89.8 us -> 88.7 us (0.988)
  waiting for transfers between devices: 18 us -> 15.1 us
  Pallas kernels: 41 us -> 43.8 us
  local copies, waits for them, and re-layouts: 4.82 us -> 3.76 us
    ppermute x3, waiting for transfers between devices: 2.28 us -> 0.01 us  [over_chips(): lax.ppermute(x, 'tile', [(t, 2 * partner(t // 2, shift, chips) + t % 2) f...]
    pallas_call x1 -> x2, Pallas kernels: 13.7 us -> 16 us  [update(): pl.pallas_call(body, in_specs=[SCALARS, IN_HBM] + [IN_HBM] * len(given) +...]
    unnamed x13 -> x11, local copies, waits for them, and re-layouts: 3.11 us -> 2.14 us
  transfers between devices with their start and end apart: 17 -> 17, of which waited for: 8 -> 6; matrix products, arithmetic and copies ran while one was open for 5% -> 5% of each run, Pallas kernels for 31% -> 34%
where the time goes in v5:
time: 88.7 us; the launch traced here: 88.4 us
  Pallas kernels  43.8 us (49%)
  starting transfers between devices  20.9 us (24%)
  waiting for transfers between devices  15.1 us (17%)
  other arithmetic  3.92 us (4%)
  local copies, waits for them, and re-layouts  3.76 us (4%)
  between operations  0.95 us (1%)
    pallas_call x2, Pallas kernels, update(): pl.pallas_call(body, in_specs=[SCALARS, IN_HBM] + [IN_HBM] * len(given) +...  16 us
    pallas_call x1, Pallas kernels, prepare(): pl.pallas_call(prepare_kernel, in_specs=[SCALARS, SCALARS, ON_CHIP, ON_CH...  11 us
    ppermute x4, waiting for transfers between devices, along_chips(): lax.ppermute(x, 'tile', [(t, (t + 2 * shift) % owners) for t in range(own...  9.63 us
    ppermute x4, starting transfers between devices, along_chips(): lax.ppermute(x, 'tile', [(t, (t + 2 * shift) % owners) for t in range(own...  8.21 us
    pallas_call x1, Pallas kernels, encode(): pl.pallas_call(body, in_specs=[SCALARS, ON_CHIP] + [ANYWHERE] * len(parts...  5.93 us
    pallas_call x1, Pallas kernels, fold(): pl.pallas_call(fold_kernel, in_specs=[SCALARS, SCALARS] + [ON_CHIP] * 4 +...  5.32 us
    ppermute x3, starting transfers between devices, over_chips(): lax.ppermute(x, 'tile', [(t, 2 * partner(t // 2, shift, chips) + t % 2) f...  4.45 us
    pallas_call x1, Pallas kernels, stage(): pl.pallas_call(stage_kernel, in_specs=[IN_HBM], out_specs=ON_CHIP, scratc...  3.55 us
  transfers between devices with their start and end apart: 17, of which 6 were waited for; matrix products, arithmetic and copies ran while one was open for 5% of the time, Pallas kernels for 34%

profile of v5, /device:TPU:0, one launch (start us, length us, event | category | flops | bytes accessed | tf_op | source)
XLA Modules:
  0.0 88.4 jit_solution(3931214147941667099)
XLA Ops:
  0.6 2.0 %project.1.refs_0_ = bf16[1,256,512]{2,1,0:T(8,128)(2,1)} custom-call(bf16[1,512,512]{2,1,0:T(8,128)(2,1)} %panel_ref.1, bf16[1,512,128]{2,1,0:T(8,128)(2,1)} %basis_ref.1), custom_call_target="tpu_custom_call" | custom-call | tf_op jit(solution)/shard_map/project/pallas_call | solution.py:36
  2.7 3.1 %collective-permute-start = (bf16[1,256,512]{2,1,0:T(8,128)(2,1)}, bf16[1,256,512]{2,1,0:T(8,128)(2,1)S(1)}, u32[]{:S(2)}, u32[]{:S(2)}) collective-permute-start(bf16[1,256,512]{2,1,0:T(8,128)(2,1)} %project.1.refs_0_), channel_id=1, source_target_pairs={{0,2},{1,3},{2,4},{3,5},{4,6},{5,7},{6,0},{7,1},{8,10},{9,11},{10,... | collective-permute-start | bytes 786440 | tf_op jit(solution)/shard_map/ppermute | solution.py:51
  5.7 2.0 %collective-permute-start.1 = (bf16[1,256,512]{2,1,0:T(8,128)(2,1)}, bf16[1,256,512]{2,1,0:T(8,128)(2,1)S(1)}, u32[]{:S(2)}, u32[]{:S(2)}) collective-permute-start(bf16[1,256,512]{2,1,0:T(8,128)(2,1)} %project.1.refs_0_), channel_id=1, source_target_pairs={{0,6},{1,7},{2,0},{3,1},{4,2},{5,3},{6,4},{7,5},{8,14},{9,15},{10,... | collective-permute-start | bytes 786440 | tf_op jit(solution)/shard_map/ppermute | solution.py:51
  7.7 0.0 collective-permute-start.4
  7.7 0.5 broadcast.49
  8.2 1.3 %reduce.11 = s32[128]{0:T(128)S(1)} reduce(s32[1,128,1]{1,2,0:T(1,128)} %param.13, s32[]{:T(128)} %broadcast.49), dimensions={0,2}, to_apply=%param.13.reduce_sub_computation.3 | reduce | bytes 1028 | tf_op args[4]
  9.6 0.1 reshape_squeeze.7
  9.7 0.2 convert_reduce_fusion.1
  9.8 5.3 %collective-permute-done.refs_1_ = bf16[1,256,512]{2,1,0:T(8,128)(2,1)S(1)} collective-permute-done((bf16[1,256,512]{2,1,0:T(8,128)(2,1)}, bf16[1,256,512]{2,1,0:T(8,128)(2,1)S(1)}, u32[]{:S(2)}, u32[]{:S(2)}) %collective-permute-start) | collective-permute-done | bytes 262176 | tf_op jit(solution)/shard_map/ppermute | solution.py:51
  15.2 0.1 collective-permute-start.2
  15.2 4.3 %collective-permute-done.1.refs_2_ = bf16[1,256,512]{2,1,0:T(8,128)(2,1)S(1)} collective-permute-done((bf16[1,256,512]{2,1,0:T(8,128)(2,1)}, bf16[1,256,512]{2,1,0:T(8,128)(2,1)S(1)}, u32[]{:S(2)}, u32[]{:S(2)}) %collective-permute-start.1) | collective-permute-done | bytes 262176 | tf_op jit(solution)/shard_map/ppermute | solution.py:51
  19.6 3.1 %collective-permute-start.3 = (bf16[1,128,512]{2,1,0:T(8,128)(2,1)S(1)}, bf16[1,128,512]{2,1,0:T(8,128)(2,1)S(1)}, u32[]{:S(2)}, u32[]{:S(2)}) collective-permute-start(bf16[1,128,512]{2,1,0:T(8,128)(2,1)S(1)} %slice.17), channel_id=1, source_target_pairs={{0,6},{1,7},{2,0},{3,1},{4,2},{5,3},{6,4},{7,5},{8,14},{9,15},{10,... | collective-permute-start | bytes 393224 | tf_op jit(solution)/shard_map/ppermute | solution.py:51
  22.6 0.0 collective-permute-start.5
  22.6 0.5 collective-permute-start.6
  23.1 0.8 or_reduce_fusion
  23.9 0.1 or.22
  24.0 0.0 copy-start
  24.0 3.6 %stage.1.staged = bf16[16,512,512]{2,1,0:T(8,128)(2,1)S(1)} custom-call(bf16[16,512,512]{2,1,0:T(8,128)(2,1)} %bitcast.26), custom_call_target="tpu_custom_call" | custom-call | flops 268435456 | bytes 16777216 | tf_op jit(solution)/shard_map/stage/pallas_call | solution.py:104
  27.6 0.0 collective-permute-done.2.refs_3_
  27.6 0.1 collective-permute-start.7
  27.6 0.0 collective-permute-done.3.refs_4_
  27.7 0.5 collective-permute-start.8
  28.2 0.0 copy-start.2
  28.2 0.0 collective-permute-done.4.refs_5_
  28.2 0.0 collective-permute-done.5.refs_6_
  28.2 0.0 collective-permute-done.6.refs_7_
  28.2 0.8 collective-permute-done.7.refs_8_
  29.0 0.2 collective-permute-done.8.refs_9_
  29.2 0.0 copy-done
  29.2 5.9 %encode.1 = (bf16[16,128,128]{2,1,0:T(8,128)(2,1)}, bf16[8,128,512]{2,1,0:T(8,128)(2,1)}) custom-call(s32[16]{0:T(128)S(1)} %fusion.3.words, bf16[16,512,512]{2,1,0:T(8,128)(2,1)S(1)} %stage.1.staged, bf16[1,256,512]{2,1,0:T(8,128)(2,1)S(1)} %copy-done, bf16[1,256,512]{2,1,0:T(8,128)(2,1)S(1)} %collective-permute-done.refs_1_, ...), custom_call_target="tpu_custom_call" | custom-call | tf_op jit(solution)/shard_map/encode/pallas_call | solution.py:200
  35.1 3.5 %all-to-all-start = ((bf16[8,2,128,128]{3,2,1,0:T(8,128)(2,1)}), bf16[8,2,128,128]{3,2,1,0:T(8,128)(2,1)S(1)}, u32[]{:S(2)}, u32[]{:S(2)}) async-start(bf16[8,2,128,128]{3,2,1,0:T(8,128)(2,1)} %bitcast.4), calls=%async_computation | async-start | bytes 1048576 | tf_op jit(solution)/shard_map/all_to_all | solution.py:508
  38.6 0.0 copy-done.3
  38.7 0.1 shift_left.30
  38.8 0.2 convert_reduce_fusion
  39.0 0.1 select_reduce_fusion
  39.1 0.1 copy.16
  39.2 0.6 reshape.63.words
  39.8 0.0 copy-done.2
  39.8 0.1 copy.17
  39.9 0.6 reshape_squeeze.8.pwords
  40.5 11.0 %prepare.1 = (bf16[8,512,128]{2,1,0:T(8,128)(2,1)}, bf16[16,128,128]{2,1,0:T(8,128)(2,1)}, bf16[16,128,128]{2,1,0:T(8,128)(2,1)}, f32[32,128,128]{2,1,0:T(8,128)}) custom-call(s32[16]{0:T(128)} %reshape.63.words, s32[16]{0:T(128)} %reshape_squeeze.8.pwords, bf16[8,128,512]{2,1,0:T(8,128)(2,1)} %get-tuple-element.14.flip_ref.refs_1_.refs_2_, ...), custom_call_target="tpu_custom_call" | custom-call | flops 1073741824 | bytes 4194304 | tf_op jit(solution)/shard_map/prepare/pallas_call | solution.py:274
  51.4 2.5 %all-to-all-done = bf16[8,2,128,128]{3,2,1,0:T(8,128)(2,1)S(1)} async-done(((bf16[8,2,128,128]{3,2,1,0:T(8,128)(2,1)}), bf16[8,2,128,128]{3,2,1,0:T(8,128)(2,1)S(1)}, u32[]{:S(2)}, u32[]{:S(2)}) %all-to-all-start) | async-done | bytes 524320 | tf_op jit(solution)/shard_map/all_to_all | solution.py:508
  53.9 0.8 copy-done.1
  54.7 5.3 %fold.1 = (bf16[16,128,128]{2,1,0:T(8,128)(2,1)}, bf16[16,128,128]{2,1,0:T(8,128)(2,1)}) custom-call(s32[16]{0:T(128)} %reshape.63.words, s32[16]{0:T(128)} %reshape_squeeze.8.pwords, bf16[16,128,128]{2,1,0:T(8,128)(2,1)} %bitcast.23, bf16[16,128,128]{2,1,0:T(8,128)(2,1)} %get-tuple-element.15.west, bf16[16,128,128]{2,1,0:T(8,128)(2,1)} %get-tuple-element.16.vest, ...), custom_call_target="tpu_custom_call" | custom-call | tf_op jit(solution)/shard_map/fold/pallas_call | solution.py:330
  60.0 0.1 collective-permute-start.9
  60.1 2.1 %collective-permute-done.9 = bf16[16,128,128]{2,1,0:T(8,128)(2,1)S(1)} collective-permute-done((bf16[16,128,128]{2,1,0:T(8,128)(2,1)}, bf16[16,128,128]{2,1,0:T(8,128)(2,1)S(1)}, u32[]{:S(2)}, u32[]{:S(2)}) %collective-permute-start.9) | collective-permute-done | bytes 524320 | tf_op jit(solution)/shard_map/ppermute | solution.py:55
  62.2 1.2 %convert_add_fusion = f32[16,128,128]{2,1,0:T(8,128)S(1)} fusion(bf16[16,128,128]{2,1,0:T(8,128)(2,1)S(1)} %collective-permute-done.9, bf16[16,128,128]{2,1,0:T(8,128)(2,1)} %get-tuple-element.18), kind=kLoop, calls=%fused_computation | loop fusion | flops 786432 | bytes 2097152 | tf_op jit(solution)/shard_map/add | solution.py:453
  63.4 0.1 dynamic-slice_convert_fusion.2
  63.5 2.5 %collective-permute-start.12 = (bf16[4,128,128]{2,1,0:T(8,128)(2,1)S(1)}, bf16[4,128,128]{2,1,0:T(8,128)(2,1)S(1)}, u32[]{:S(2)}, u32[]{:S(2)}) collective-permute-start(bf16[4,128,128]{2,1,0:T(8,128)(2,1)S(1)} %get-tuple-element.31), channel_id=1, source_target_pairs={{0,24},{8,16},{16,8},{24,0},{1,25},{9,17},{17,9},{25,1},{2,26},{10... | collective-permute-start | bytes 393224 | tf_op jit(solution)/shard_map/ppermute | solution.py:456
  66.0 0.5 collective-permute-start.11
  66.5 0.5 collective-permute-start.10
  67.0 9.0 %update.2.refs_0_ = bf16[8,512,512]{2,1,0:T(8,128)(2,1)} custom-call(s32[16]{0:T(128)} %reshape.63.words, bf16[8,512,512]{2,1,0:T(8,128)(2,1)} %bitcast.20, bf16[16,128,128]{2,1,0:T(8,128)(2,1)} %bitcast.24, bf16[8,128,512]{2,1,0:T(8,128)(2,1)} %get-tuple-element.14.flip_ref.refs_1_.refs_2_, bf16[8,512,128]{2,1,0:T(8,128)(2,1)} %get-tuple-element.20.refs_2_.refs_3_), custom_call_target="tpu_custom_call" | custom-call | flops 2147483648 | bytes 8388608 | tf_op jit(solution)/shard_map/update/pallas_call | solution.py:412
  76.1 0.0 collective-permute-done.12
  76.1 0.0 collective-permute-done.11
  76.1 0.0 collective-permute-done.10
  76.1 0.1 convert_add_fusion.1
  76.2 0.8 collective-permute-start.15
  77.0 1.0 %collective-permute-start.14 = (bf16[1,128,128]{2,1,0:T(8,128)(2,1)S(1)}, bf16[1,128,128]{2,1,0:T(8,128)(2,1)S(1)}, u32[]{:S(2)}, u32[]{:S(2)}) collective-permute-start(bf16[1,128,128]{2,1,0:T(8,128)(2,1)S(1)} %get-tuple-element.35), channel_id=1, source_target_pairs={{0,4},{1,5},{2,6},{3,7},{4,0},{5,1},{6,2},{7,3},{8,12},{9,13},{10,... | collective-permute-start | bytes 98312 | tf_op jit(solution)/shard_map/ppermute | solution.py:461
  78.0 2.7 %collective-permute-start.13 = (bf16[1,128,128]{2,1,0:T(8,128)(2,1)S(1)}, bf16[1,128,128]{2,1,0:T(8,128)(2,1)S(1)}, u32[]{:S(2)}, u32[]{:S(2)}) collective-permute-start(bf16[1,128,128]{2,1,0:T(8,128)(2,1)S(1)} %get-tuple-element.33), channel_id=1, source_target_pairs={{0,2},{1,3},{2,0},{3,1},{4,6},{5,7},{6,4},{7,5},{8,10},{9,11},{10,... | collective-permute-start | bytes 98312 | tf_op jit(solution)/shard_map/ppermute | solution.py:461
  80.6 6.9 %update.3 = bf16[8,512,512]{2,1,0:T(8,128)(2,1)} custom-call(s32[16]{0:T(128)} %reshape.63.words, bf16[8,512,512]{2,1,0:T(8,128)(2,1)} %bitcast.21, bf16[8,512,512]{2,1,0:T(8,128)(2,1)} %update.2.refs_0_, bf16[16,128,128]{2,1,0:T(8,128)(2,1)} %bitcast.25, ...), custom_call_target="tpu_custom_call", output_to_operand_aliasing={{}: (2, {})} | custom-call | flops 2147483648 | bytes 8388608 | tf_op jit(solution)/shard_map/update/pallas_call | solution.py:412
  87.6 0.0 collective-permute-done.15
  87.6 0.0 collective-permute-done.14
  87.6 0.0 collective-permute-done.13
  87.6 0.7 copy.18
  (12 shorter events, 0.1 us)
Async XLA Ops:
  2.7 12.5 %collective-permute-start = (bf16[1,256,512]{2,1,0:T(8,128)(2,1)}, bf16[1,256,512]{2,1,0:T(8,128)(2,1)S(1)}, u32[]{:S(2)}, u32[]{:S(2)}) collective-permute-start(bf16[1,256,512]{2,1,0:T(8,128)(2,1)} %project.1.refs_0_), channel_id=1, source_target_pairs={{0,2},{1,3},{2,4},{3,5},{4,6},{5,7},{6,0},{7,1},{8,10},{9,11},{10,... | collective-permute-start | bytes 786440 | tf_op jit(solution)/shard_map/ppermute | solution.py:51
  5.7 13.8 %collective-permute-start.1 = (bf16[1,256,512]{2,1,0:T(8,128)(2,1)}, bf16[1,256,512]{2,1,0:T(8,128)(2,1)S(1)}, u32[]{:S(2)}, u32[]{:S(2)}) collective-permute-start(bf16[1,256,512]{2,1,0:T(8,128)(2,1)} %project.1.refs_0_), channel_id=1, source_target_pairs={{0,6},{1,7},{2,0},{3,1},{4,2},{5,3},{6,4},{7,5},{8,14},{9,15},{10,... | collective-permute-start | bytes 786440 | tf_op jit(solution)/shard_map/ppermute | solution.py:51
  7.7 20.4 %collective-permute-start.4 = (bf16[1,256,512]{2,1,0:T(8,128)(2,1)}, bf16[1,256,512]{2,1,0:T(8,128)(2,1)S(1)}, u32[]{:S(2)}, u32[]{:S(2)}) collective-permute-start(bf16[1,256,512]{2,1,0:T(8,128)(2,1)} %project.1.refs_0_), channel_id=1, source_target_pairs={{0,1},{1,0},{2,3},{3,2},{4,5},{5,4},{6,7},{7,6},{8,9},{9,8},{10,11... | collective-permute-start | bytes 786440 | tf_op jit(solution)/shard_map/ppermute | solution.py:55
  15.2 12.4 %collective-permute-start.2 = (bf16[1,128,512]{2,1,0:T(8,128)(2,1)S(1)}, bf16[1,128,512]{2,1,0:T(8,128)(2,1)S(1)}, u32[]{:S(2)}, u32[]{:S(2)}) collective-permute-start(bf16[1,128,512]{2,1,0:T(8,128)(2,1)S(1)} %slice.16), channel_id=1, source_target_pairs={{0,2},{1,3},{2,4},{3,5},{4,6},{5,7},{6,0},{7,1},{8,10},{9,11},{10,... | collective-permute-start | bytes 393224 | tf_op jit(solution)/shard_map/ppermute | solution.py:51
  19.6 8.1 %collective-permute-start.3 = (bf16[1,128,512]{2,1,0:T(8,128)(2,1)S(1)}, bf16[1,128,512]{2,1,0:T(8,128)(2,1)S(1)}, u32[]{:S(2)}, u32[]{:S(2)}) collective-permute-start(bf16[1,128,512]{2,1,0:T(8,128)(2,1)S(1)} %slice.17), channel_id=1, source_target_pairs={{0,6},{1,7},{2,0},{3,1},{4,2},{5,3},{6,4},{7,5},{8,14},{9,15},{10,... | collective-permute-start | bytes 393224 | tf_op jit(solution)/shard_map/ppermute | solution.py:51
  22.6 5.6 %collective-permute-start.5 = (bf16[1,256,512]{2,1,0:T(8,128)(2,1)S(1)}, bf16[1,256,512]{2,1,0:T(8,128)(2,1)S(1)}, u32[]{:S(2)}, u32[]{:S(2)}) collective-permute-start(bf16[1,256,512]{2,1,0:T(8,128)(2,1)S(1)} %collective-permute-done.refs_1_), channel_id=1, source_target_pairs={{0,1},{1,0},{2,3},{3,2},{4,5},{5,4},{6,7},{7,6},{8,9},{9,8},{10,11... | collective-permute-start | bytes 786440 | tf_op jit(solution)/shard_map/ppermute | solution.py:55
  22.6 5.6 %collective-permute-start.6 = (bf16[1,256,512]{2,1,0:T(8,128)(2,1)S(1)}, bf16[1,256,512]{2,1,0:T(8,128)(2,1)S(1)}, u32[]{:S(2)}, u32[]{:S(2)}) collective-permute-start(bf16[1,256,512]{2,1,0:T(8,128)(2,1)S(1)} %collective-permute-done.1.refs_2_), channel_id=1, source_target_pairs={{0,1},{1,0},{2,3},{3,2},{4,5},{5,4},{6,7},{7,6},{8,9},{9,8},{10,11... | collective-permute-start | bytes 786440 | tf_op jit(solution)/shard_map/ppermute | solution.py:55
  24.0 5.2 %copy-start = (bf16[1,256,512]{2,1,0:T(8,128)(2,1)S(1)}, bf16[1,256,512]{2,1,0:T(8,128)(2,1)}, u32[]{:S(2)}) copy-start(bf16[1,256,512]{2,1,0:T(8,128)(2,1)} %project.1.refs_0_) | copy-start | bytes 786436
  27.6 1.4 %collective-permute-start.7 = (bf16[1,128,512]{2,1,0:T(8,128)(2,1)S(1)}, bf16[1,128,512]{2,1,0:T(8,128)(2,1)S(1)}, u32[]{:S(2)}, u32[]{:S(2)}) collective-permute-start(bf16[1,128,512]{2,1,0:T(8,128)(2,1)S(1)} %collective-permute-done.2.refs_3_), channel_id=1, source_target_pairs={{0,1},{1,0},{2,3},{3,2},{4,5},{5,4},{6,7},{7,6},{8,9},{9,8},{10,11... | collective-permute-start | bytes 393224 | tf_op jit(solution)/shard_map/ppermute | solution.py:55
  27.7 1.5 %collective-permute-start.8 = (bf16[1,128,512]{2,1,0:T(8,128)(2,1)S(1)}, bf16[1,128,512]{2,1,0:T(8,128)(2,1)S(1)}, u32[]{:S(2)}, u32[]{:S(2)}) collective-permute-start(bf16[1,128,512]{2,1,0:T(8,128)(2,1)S(1)} %collective-permute-done.3.refs_4_), channel_id=1, source_target_pairs={{0,1},{1,0},{2,3},{3,2},{4,5},{5,4},{6,7},{7,6},{8,9},{9,8},{10,11... | collective-permute-start | bytes 393224 | tf_op jit(solution)/shard_map/ppermute | solution.py:55
  28.2 10.5 %copy-start.3 = (s32[1,128]{1,0:T(1,128)S(1)}, s32[1,128]{1,0:T(1,128)}, u32[]{:S(2)}) copy-start(s32[1,128]{1,0:T(1,128)} %param.14) | copy-start | bytes 1540
  28.2 11.7 %copy-start.2 = (s32[1,8,2]{1,2,0:T(2,128)S(1)}, s32[1,8,2]{1,2,0:T(2,128)}, u32[]{:S(2)}) copy-start(s32[1,8,2]{1,2,0:T(2,128)} %param.16) | copy-start | bytes 196
  35.1 18.8 %all-to-all-start = ((bf16[8,2,128,128]{3,2,1,0:T(8,128)(2,1)}), bf16[8,2,128,128]{3,2,1,0:T(8,128)(2,1)S(1)}, u32[]{:S(2)}, u32[]{:S(2)}) async-start(bf16[8,2,128,128]{3,2,1,0:T(8,128)(2,1)} %bitcast.4), calls=%async_computation | async-start | bytes 1048576 | tf_op jit(solution)/shard_map/all_to_all | solution.py:508
  53.9 0.8 copy-start.1
  60.0 2.2 %collective-permute-start.9 = (bf16[16,128,128]{2,1,0:T(8,128)(2,1)}, bf16[16,128,128]{2,1,0:T(8,128)(2,1)S(1)}, u32[]{:S(2)}, u32[]{:S(2)}) collective-permute-start(bf16[16,128,128]{2,1,0:T(8,128)(2,1)} %get-tuple-element.19), channel_id=1, source_target_pairs={{0,1},{1,0},{2,3},{3,2},{4,5},{5,4},{6,7},{7,6},{8,9},{9,8},{10,11... | collective-permute-start | bytes 1572872 | tf_op jit(solution)/shard_map/ppermute | solution.py:55
  63.5 12.6 %collective-permute-start.12 = (bf16[4,128,128]{2,1,0:T(8,128)(2,1)S(1)}, bf16[4,128,128]{2,1,0:T(8,128)(2,1)S(1)}, u32[]{:S(2)}, u32[]{:S(2)}) collective-permute-start(bf16[4,128,128]{2,1,0:T(8,128)(2,1)S(1)} %get-tuple-element.31), channel_id=1, source_target_pairs={{0,24},{8,16},{16,8},{24,0},{1,25},{9,17},{17,9},{25,1},{2,26},{10... | collective-permute-start | bytes 393224 | tf_op jit(solution)/shard_map/ppermute | solution.py:456
  66.0 10.1 %collective-permute-start.11 = (bf16[4,128,128]{2,1,0:T(8,128)(2,1)S(1)}, bf16[4,128,128]{2,1,0:T(8,128)(2,1)S(1)}, u32[]{:S(2)}, u32[]{:S(2)}) collective-permute-start(bf16[4,128,128]{2,1,0:T(8,128)(2,1)S(1)} %get-tuple-element.32), channel_id=1, source_target_pairs={{0,16},{8,24},{16,0},{24,8},{1,17},{9,25},{17,1},{25,9},{2,18},{10... | collective-permute-start | bytes 393224 | tf_op jit(solution)/shard_map/ppermute | solution.py:456
  66.5 9.6 %collective-permute-start.10 = (bf16[4,128,128]{2,1,0:T(8,128)(2,1)S(1)}, bf16[4,128,128]{2,1,0:T(8,128)(2,1)S(1)}, u32[]{:S(2)}, u32[]{:S(2)}) collective-permute-start(bf16[4,128,128]{2,1,0:T(8,128)(2,1)S(1)} %get-tuple-element.30), channel_id=1, source_target_pairs={{0,8},{8,0},{16,24},{24,16},{1,9},{9,1},{17,25},{25,17},{2,10},{10... | collective-permute-start | bytes 393224 | tf_op jit(solution)/shard_map/ppermute | solution.py:456
  76.2 11.4 %collective-permute-start.15 = (bf16[1,128,128]{2,1,0:T(8,128)(2,1)S(1)}, bf16[1,128,128]{2,1,0:T(8,128)(2,1)S(1)}, u32[]{:S(2)}, u32[]{:S(2)}) collective-permute-start(bf16[1,128,128]{2,1,0:T(8,128)(2,1)S(1)} %get-tuple-element.34), channel_id=1, source_target_pairs={{0,6},{1,7},{2,4},{3,5},{4,2},{5,3},{6,0},{7,1},{8,14},{9,15},{10,... | collective-permute-start | bytes 98312 | tf_op jit(solution)/shard_map/ppermute | solution.py:461
  77.0 10.6 %collective-permute-start.14 = (bf16[1,128,128]{2,1,0:T(8,128)(2,1)S(1)}, bf16[1,128,128]{2,1,0:T(8,128)(2,1)S(1)}, u32[]{:S(2)}, u32[]{:S(2)}) collective-permute-start(bf16[1,128,128]{2,1,0:T(8,128)(2,1)S(1)} %get-tuple-element.35), channel_id=1, source_target_pairs={{0,4},{1,5},{2,6},{3,7},{4,0},{5,1},{6,2},{7,3},{8,12},{9,13},{10,... | collective-permute-start | bytes 98312 | tf_op jit(solution)/shard_map/ppermute | solution.py:461
  78.0 9.6 %collective-permute-start.13 = (bf16[1,128,128]{2,1,0:T(8,128)(2,1)S(1)}, bf16[1,128,128]{2,1,0:T(8,128)(2,1)S(1)}, u32[]{:S(2)}, u32[]{:S(2)}) collective-permute-start(bf16[1,128,128]{2,1,0:T(8,128)(2,1)S(1)} %get-tuple-element.33), channel_id=1, source_target_pairs={{0,2},{1,3},{2,0},{3,1},{4,6},{5,7},{6,4},{7,5},{8,10},{9,11},{10,... | collective-permute-start | bytes 98312 | tf_op jit(solution)/shard_map/ppermute | solution.py:461

commit v6 on v5

--- a/solution.py
+++ b/solution.py
@@ -343,59 +343,45 @@
 
 
 def update_kernel(
-    low, words, parents, partial, core_in, flip_in, basis_in, updated,
-    cores, flips, basis, held, total, mixed, sems, in_sems, out_sems,
+    low, words, parents, partial, core_ref, basis_ref, flip_ref, updated,
+    held, total, mixed, made, in_sems, out_sems,
 ):
-    count, items = held.shape[0], cores.shape[0]
+    count, items = held.shape[0], core_ref.shape[0]
     group = grouped(items)
-    loads = [
-        pltpu.make_async_copy(source, target, sems.at[n])
-        for n, (source, target) in enumerate(
-            ((core_in, cores), (flip_in, flips), (basis_in, basis))
-        )
-    ]
 
     def in_copy(p):
         return pltpu.make_async_copy(parents.at[low + p], held.at[p], in_sems.at[p])
 
     def out_copy(p):
-        return pltpu.make_async_copy(held.at[p], updated.at[low + p], out_sems.at[p])
-
-    for load in loads:
-        load.start()
+        return pltpu.make_async_copy(made.at[p], updated.at[low + p], out_sems.at[p])
+
     for p in range(count):
         in_copy(p).start()
-    loads[0].wait()
-    loads[1].wait()
 
     def mix(g, carry):
         for s in [g * group + n for n in range(group)]:
             _, _, col = unpack(words[s])
-            mixed[s] = dot(cores[s], flips[col]).astype(BF16)
+            mixed[s] = dot(core_ref[s], flip_ref[col]).astype(BF16)
         return carry
 
     lax.fori_loop(0, items // group, mix, 0)
-    loads[2].wait()
-
-    def one(p, carry):
+    for p in range(count):
         in_copy(p).wait()
-        total[...] = held[p].astype(F32)
-
-        def item(s, carry):
-            slot, row, _ = unpack(words[s])
-
-            @pl.when(slot == low + p + 1)
-            def _():
-                total[...] += dot(basis[row], mixed[s])
-
-            return carry
-
-        lax.fori_loop(0, items, item, 0)
-        held[p] = total[...].astype(BF16)
+        total[p] = held[p].astype(F32)
+
+    def item(s, carry):
+        slot, row, _ = unpack(words[s])
+
+        @pl.when((slot > low) & (slot <= low + count))
+        def _():
+            total[slot - 1 - low] += dot(basis_ref[row], mixed[s])
+
+        return carry
+
+    lax.fori_loop(0, items, item, 0)
+    for p in range(count):
+        made[p] = total[p].astype(BF16)
         out_copy(p).start()
-        return carry
-
-    lax.fori_loop(0, count, one, 0)
     for p in range(count):
         out_copy(p).wait()
 
@@ -403,6 +389,7 @@
 def update(low, count, words, parents, partial, cores, basis, flipped):
     order = parents.shape[1]
     rank = basis.shape[2]
+    items = cores.shape[0]
     first = partial is None
     given = [] if first else [partial]
 
@@ -411,16 +398,13 @@
 
     return pl.pallas_call(
         body,
-        in_specs=[SCALARS, IN_HBM] + [IN_HBM] * len(given) + [ANYWHERE] * 3,
+        in_specs=[SCALARS, IN_HBM] + [IN_HBM] * len(given) + [ON_CHIP] * 3,
         out_specs=IN_HBM,
         scratch_shapes=[
-            pltpu.VMEM(cores.shape, BF16),
-            pltpu.VMEM(flipped.shape, BF16),
-            pltpu.VMEM(basis.shape, BF16),
             pltpu.VMEM((count, order, order), BF16),
-            pltpu.VMEM((order, order), F32),
-            pltpu.VMEM((cores.shape[0], rank, order), BF16),
-            pltpu.SemaphoreType.DMA((3,)),
+            pltpu.VMEM((count, order, order), F32),
+            pltpu.VMEM((items, rank, order), BF16),
+            pltpu.VMEM((count, order, order), BF16),
             pltpu.SemaphoreType.DMA((count,)),
             pltpu.SemaphoreType.DMA((count,)),
         ],
@@ -431,7 +415,7 @@
             flops=8 * parents.size * rank, bytes_accessed=4 * parents.size, transcendentals=0
         ),
         name="update",
-    )(words, parents, *given, cores, flipped, basis)
+    )(words, parents, *given, cores, basis, flipped)
 
 
 def partner(i, step, size):
@@ -517,7 +501,7 @@
 
     def decode(partial, cores):
         count = parent_tiles.shape[1]
-        early = count - count * 3 // 8
+        early = count - count // 2
         low, size = (0, early) if partial is None else (early, count - early)
         return update(low, size, words, parent_tiles[0], partial, cores, basis, flipped)
 

time: 88.7 us -> 87.1 us (0.982)
  Pallas kernels: 43.8 us -> 41.6 us
    pallas_call x2, Pallas kernels: 16 us -> 14.2 us  [update(): pl.pallas_call(body, in_specs=[SCALARS, IN_HBM] + [IN_HBM] * len(given) +...]
  transfers between devices with their start and end apart: 17 -> 17, of which waited for: 6 -> 6; matrix products, arithmetic and copies ran while one was open for 5% -> 6% of each run, Pallas kernels for 34% -> 33%
where the time goes in v6:
time: 87.1 us; the launch traced here: 86.6 us
  Pallas kernels  41.6 us (48%)
  starting transfers between devices  20.9 us (24%)
  waiting for transfers between devices  15.6 us (18%)
  other arithmetic  3.92 us (5%)
  local copies, waits for them, and re-layouts  3.76 us (4%)
  between operations  0.95 us (1%)
    pallas_call x2, Pallas kernels, update(): pl.pallas_call(body, in_specs=[SCALARS, IN_HBM] + [IN_HBM] * len(given) +...  14.2 us
    pallas_call x1, Pallas kernels, prepare(): pl.pallas_call(prepare_kernel, in_specs=[SCALARS, SCALARS, ON_CHIP, ON_CH...  10.5 us
    ppermute x4, waiting for transfers between devices, along_chips(): lax.ppermute(x, 'tile', [(t, (t + 2 * shift) % owners) for t in range(own...  9.63 us
    ppermute x4, starting transfers between devices, along_chips(): lax.ppermute(x, 'tile', [(t, (t + 2 * shift) % owners) for t in range(own...  8.21 us
    pallas_call x1, Pallas kernels, encode(): pl.pallas_call(body, in_specs=[SCALARS, ON_CHIP] + [ANYWHERE] * len(parts...  5.92 us
    pallas_call x1, Pallas kernels, fold(): pl.pallas_call(fold_kernel, in_specs=[SCALARS, SCALARS] + [ON_CHIP] * 4 +...  5.32 us
    ppermute x3, starting transfers between devices, over_chips(): lax.ppermute(x, 'tile', [(t, 2 * partner(t // 2, shift, chips) + t % 2) f...  4.45 us
    pallas_call x1, Pallas kernels, stage(): pl.pallas_call(stage_kernel, in_specs=[IN_HBM], out_specs=ON_CHIP, scratc...  3.55 us
  transfers between devices with their start and end apart: 17, of which 6 were waited for; matrix products, arithmetic and copies ran while one was open for 6% of the time, Pallas kernels for 33%

profile of v6, /device:TPU:0, one launch (start us, length us, event | category | flops | bytes accessed | tf_op | source)
XLA Modules:
  0.0 86.6 jit_solution(9781879903714618761)
XLA Ops:
  0.6 2.0 %project.1.refs_0_ = bf16[1,256,512]{2,1,0:T(8,128)(2,1)} custom-call(bf16[1,512,512]{2,1,0:T(8,128)(2,1)} %panel_ref.1, bf16[1,512,128]{2,1,0:T(8,128)(2,1)} %basis_ref.1), custom_call_target="tpu_custom_call" | custom-call | tf_op jit(solution)/shard_map/project/pallas_call | solution.py:36
  2.7 3.1 %collective-permute-start = (bf16[1,256,512]{2,1,0:T(8,128)(2,1)}, bf16[1,256,512]{2,1,0:T(8,128)(2,1)S(1)}, u32[]{:S(2)}, u32[]{:S(2)}) collective-permute-start(bf16[1,256,512]{2,1,0:T(8,128)(2,1)} %project.1.refs_0_), channel_id=1, source_target_pairs={{0,2},{1,3},{2,4},{3,5},{4,6},{5,7},{6,0},{7,1},{8,10},{9,11},{10,... | collective-permute-start | bytes 786440 | tf_op jit(solution)/shard_map/ppermute | solution.py:51
  5.7 2.0 %collective-permute-start.1 = (bf16[1,256,512]{2,1,0:T(8,128)(2,1)}, bf16[1,256,512]{2,1,0:T(8,128)(2,1)S(1)}, u32[]{:S(2)}, u32[]{:S(2)}) collective-permute-start(bf16[1,256,512]{2,1,0:T(8,128)(2,1)} %project.1.refs_0_), channel_id=1, source_target_pairs={{0,6},{1,7},{2,0},{3,1},{4,2},{5,3},{6,4},{7,5},{8,14},{9,15},{10,... | collective-permute-start | bytes 786440 | tf_op jit(solution)/shard_map/ppermute | solution.py:51
  7.7 0.0 collective-permute-start.4
  7.7 0.5 broadcast.49
  8.2 1.3 %reduce.11 = s32[128]{0:T(128)S(1)} reduce(s32[1,128,1]{1,2,0:T(1,128)} %param.13, s32[]{:T(128)} %broadcast.49), dimensions={0,2}, to_apply=%param.13.reduce_sub_computation.3 | reduce | bytes 1028 | tf_op args[4]
  9.6 0.1 reshape_squeeze.7
  9.7 0.2 convert_reduce_fusion.1
  9.8 5.3 %collective-permute-done.refs_1_ = bf16[1,256,512]{2,1,0:T(8,128)(2,1)S(1)} collective-permute-done((bf16[1,256,512]{2,1,0:T(8,128)(2,1)}, bf16[1,256,512]{2,1,0:T(8,128)(2,1)S(1)}, u32[]{:S(2)}, u32[]{:S(2)}) %collective-permute-start) | collective-permute-done | bytes 262176 | tf_op jit(solution)/shard_map/ppermute | solution.py:51
  15.2 0.1 collective-permute-start.2
  15.2 4.3 %collective-permute-done.1.refs_2_ = bf16[1,256,512]{2,1,0:T(8,128)(2,1)S(1)} collective-permute-done((bf16[1,256,512]{2,1,0:T(8,128)(2,1)}, bf16[1,256,512]{2,1,0:T(8,128)(2,1)S(1)}, u32[]{:S(2)}, u32[]{:S(2)}) %collective-permute-start.1) | collective-permute-done | bytes 262176 | tf_op jit(solution)/shard_map/ppermute | solution.py:51
  19.6 3.1 %collective-permute-start.3 = (bf16[1,128,512]{2,1,0:T(8,128)(2,1)S(1)}, bf16[1,128,512]{2,1,0:T(8,128)(2,1)S(1)}, u32[]{:S(2)}, u32[]{:S(2)}) collective-permute-start(bf16[1,128,512]{2,1,0:T(8,128)(2,1)S(1)} %slice.17), channel_id=1, source_target_pairs={{0,6},{1,7},{2,0},{3,1},{4,2},{5,3},{6,4},{7,5},{8,14},{9,15},{10,... | collective-permute-start | bytes 393224 | tf_op jit(solution)/shard_map/ppermute | solution.py:51
  22.6 0.0 collective-permute-start.5
  22.6 0.5 collective-permute-start.6
  23.1 0.8 or_reduce_fusion
  23.9 0.1 or.22
  24.0 0.0 copy-start
  24.0 3.6 %stage.1.staged = bf16[16,512,512]{2,1,0:T(8,128)(2,1)S(1)} custom-call(bf16[16,512,512]{2,1,0:T(8,128)(2,1)} %bitcast.26), custom_call_target="tpu_custom_call" | custom-call | flops 268435456 | bytes 16777216 | tf_op jit(solution)/shard_map/stage/pallas_call | solution.py:104
  27.6 0.0 collective-permute-done.2.refs_3_
  27.6 0.1 collective-permute-start.7
  27.6 0.0 collective-permute-done.3.refs_4_
  27.7 0.5 collective-permute-start.8
  28.2 0.0 copy-start.2
  28.2 0.0 collective-permute-done.4.refs_5_
  28.2 0.0 collective-permute-done.5.refs_6_
  28.2 0.0 collective-permute-done.6.refs_7_
  28.2 0.8 collective-permute-done.7.refs_8_
  29.0 0.2 collective-permute-done.8.refs_9_
  29.2 0.0 copy-done
  29.2 5.9 %encode.1 = (bf16[16,128,128]{2,1,0:T(8,128)(2,1)}, bf16[8,128,512]{2,1,0:T(8,128)(2,1)}) custom-call(s32[16]{0:T(128)S(1)} %fusion.3.words, bf16[16,512,512]{2,1,0:T(8,128)(2,1)S(1)} %stage.1.staged, bf16[1,256,512]{2,1,0:T(8,128)(2,1)S(1)} %copy-done, bf16[1,256,512]{2,1,0:T(8,128)(2,1)S(1)} %collective-permute-done.refs_1_, ...), custom_call_target="tpu_custom_call" | custom-call | tf_op jit(solution)/shard_map/encode/pallas_call | solution.py:200
  35.1 3.5 %all-to-all-start = ((bf16[8,2,128,128]{3,2,1,0:T(8,128)(2,1)}), bf16[8,2,128,128]{3,2,1,0:T(8,128)(2,1)S(1)}, u32[]{:S(2)}, u32[]{:S(2)}) async-start(bf16[8,2,128,128]{3,2,1,0:T(8,128)(2,1)} %bitcast.4), calls=%async_computation | async-start | bytes 1048576 | tf_op jit(solution)/shard_map/all_to_all | solution.py:492
  38.6 0.0 copy-done.3
  38.6 0.1 shift_left.30
  38.7 0.2 convert_reduce_fusion
  39.0 0.1 select_reduce_fusion
  39.1 0.1 copy.16
  39.2 0.6 reshape.63.words
  39.8 0.0 copy-done.2
  39.8 0.1 copy.17
  39.9 0.6 reshape_squeeze.8.pwords
  40.5 10.5 %prepare.1 = (bf16[8,512,128]{2,1,0:T(8,128)(2,1)}, bf16[16,128,128]{2,1,0:T(8,128)(2,1)}, bf16[16,128,128]{2,1,0:T(8,128)(2,1)}, f32[32,128,128]{2,1,0:T(8,128)}) custom-call(s32[16]{0:T(128)} %reshape.63.words, s32[16]{0:T(128)} %reshape_squeeze.8.pwords, bf16[8,128,512]{2,1,0:T(8,128)(2,1)} %get-tuple-element.14.flip_ref.refs_2_.refs_3_, ...), custom_call_target="tpu_custom_call" | custom-call | flops 1073741824 | bytes 4194304 | tf_op jit(solution)/shard_map/prepare/pallas_call | solution.py:274
  50.9 2.9 %all-to-all-done = bf16[8,2,128,128]{3,2,1,0:T(8,128)(2,1)S(1)} async-done(((bf16[8,2,128,128]{3,2,1,0:T(8,128)(2,1)}), bf16[8,2,128,128]{3,2,1,0:T(8,128)(2,1)S(1)}, u32[]{:S(2)}, u32[]{:S(2)}) %all-to-all-start) | async-done | bytes 524320 | tf_op jit(solution)/shard_map/all_to_all | solution.py:492
  53.9 0.8 copy-done.1
  54.7 5.3 %fold.1 = (bf16[16,128,128]{2,1,0:T(8,128)(2,1)}, bf16[16,128,128]{2,1,0:T(8,128)(2,1)}) custom-call(s32[16]{0:T(128)} %reshape.63.words, s32[16]{0:T(128)} %reshape_squeeze.8.pwords, bf16[16,128,128]{2,1,0:T(8,128)(2,1)} %bitcast.23, bf16[16,128,128]{2,1,0:T(8,128)(2,1)} %get-tuple-element.15.west, bf16[16,128,128]{2,1,0:T(8,128)(2,1)} %get-tuple-element.16.vest, ...), custom_call_target="tpu_custom_call" | custom-call | tf_op jit(solution)/shard_map/fold/pallas_call | solution.py:330
  60.0 0.1 collective-permute-start.9
  60.1 2.1 %collective-permute-done.9 = bf16[16,128,128]{2,1,0:T(8,128)(2,1)S(1)} collective-permute-done((bf16[16,128,128]{2,1,0:T(8,128)(2,1)}, bf16[16,128,128]{2,1,0:T(8,128)(2,1)S(1)}, u32[]{:S(2)}, u32[]{:S(2)}) %collective-permute-start.9) | collective-permute-done | bytes 524320 | tf_op jit(solution)/shard_map/ppermute | solution.py:55
  62.2 1.2 %convert_add_fusion = f32[16,128,128]{2,1,0:T(8,128)S(1)} fusion(bf16[16,128,128]{2,1,0:T(8,128)(2,1)S(1)} %collective-permute-done.9, bf16[16,128,128]{2,1,0:T(8,128)(2,1)} %get-tuple-element.18), kind=kLoop, calls=%fused_computation | loop fusion | flops 786432 | bytes 2097152 | tf_op jit(solution)/shard_map/add | solution.py:437
  63.4 0.1 dynamic-slice_convert_fusion.2
  63.4 2.5 %collective-permute-start.12 = (bf16[4,128,128]{2,1,0:T(8,128)(2,1)S(1)}, bf16[4,128,128]{2,1,0:T(8,128)(2,1)S(1)}, u32[]{:S(2)}, u32[]{:S(2)}) collective-permute-start(bf16[4,128,128]{2,1,0:T(8,128)(2,1)S(1)} %get-tuple-element.31), channel_id=1, source_target_pairs={{0,24},{8,16},{16,8},{24,0},{1,25},{9,17},{17,9},{25,1},{2,26},{10... | collective-permute-start | bytes 393224 | tf_op jit(solution)/shard_map/ppermute | solution.py:440
  66.0 0.5 collective-permute-start.11
  66.5 0.5 collective-permute-start.10
  67.0 6.9 %update.2.refs_0_ = bf16[8,512,512]{2,1,0:T(8,128)(2,1)} custom-call(s32[16]{0:T(128)} %reshape.63.words, bf16[8,512,512]{2,1,0:T(8,128)(2,1)} %bitcast.20, bf16[16,128,128]{2,1,0:T(8,128)(2,1)} %bitcast.24, bf16[8,512,128]{2,1,0:T(8,128)(2,1)} %get-tuple-element.20.refs_1_.refs_2_, bf16[8,128,512]{2,1,0:T(8,128)(2,1)} %get-tuple-element.14.flip_ref.refs_2_.refs_3_), custom_call_target="tpu_custom_call" | custom-call | flops 2147483648 | bytes 8388608 | tf_op jit(solution)/shard_map/update/pallas_call | solution.py:399
  73.9 0.0 collective-permute-done.12
  73.9 0.0 collective-permute-done.11
  73.9 0.0 collective-permute-done.10
  73.9 0.1 convert_add_fusion.1
  74.0 1.1 %collective-permute-start.15 = (bf16[1,128,128]{2,1,0:T(8,128)(2,1)S(1)}, bf16[1,128,128]{2,1,0:T(8,128)(2,1)S(1)}, u32[]{:S(2)}, u32[]{:S(2)}) collective-permute-start(bf16[1,128,128]{2,1,0:T(8,128)(2,1)S(1)} %get-tuple-element.34), channel_id=1, source_target_pairs={{0,6},{1,7},{2,4},{3,5},{4,2},{5,3},{6,0},{7,1},{8,14},{9,15},{10,... | collective-permute-start | bytes 98312 | tf_op jit(solution)/shard_map/ppermute | solution.py:445
  75.0 1.1 %collective-permute-start.14 = (bf16[1,128,128]{2,1,0:T(8,128)(2,1)S(1)}, bf16[1,128,128]{2,1,0:T(8,128)(2,1)S(1)}, u32[]{:S(2)}, u32[]{:S(2)}) collective-permute-start(bf16[1,128,128]{2,1,0:T(8,128)(2,1)S(1)} %get-tuple-element.35), channel_id=1, source_target_pairs={{0,4},{1,5},{2,6},{3,7},{4,0},{5,1},{6,2},{7,3},{8,12},{9,13},{10,... | collective-permute-start | bytes 98312 | tf_op jit(solution)/shard_map/ppermute | solution.py:445
  76.1 2.3 %collective-permute-start.13 = (bf16[1,128,128]{2,1,0:T(8,128)(2,1)S(1)}, bf16[1,128,128]{2,1,0:T(8,128)(2,1)S(1)}, u32[]{:S(2)}, u32[]{:S(2)}) collective-permute-start(bf16[1,128,128]{2,1,0:T(8,128)(2,1)S(1)} %get-tuple-element.33), channel_id=1, source_target_pairs={{0,2},{1,3},{2,0},{3,1},{4,6},{5,7},{6,4},{7,5},{8,10},{9,11},{10,... | collective-permute-start | bytes 98312 | tf_op jit(solution)/shard_map/ppermute | solution.py:445
  78.4 7.4 %update.3 = bf16[8,512,512]{2,1,0:T(8,128)(2,1)} custom-call(s32[16]{0:T(128)} %reshape.63.words, bf16[8,512,512]{2,1,0:T(8,128)(2,1)} %bitcast.21, bf16[8,512,512]{2,1,0:T(8,128)(2,1)} %update.2.refs_0_, bf16[16,128,128]{2,1,0:T(8,128)(2,1)} %bitcast.25, bf16[8,512,128]{2,1,0:T(8,128)(2,1)} %get-tuple-element.20.refs_1_.refs_2_, ...), custom_call_target="tpu_custom_call", output_to_operand_aliasing={{}: (2, {})} | custom-call | flops 2147483648 | bytes 8388608 | tf_op jit(solution)/shard_map/update/pallas_call | solution.py:399
  85.8 0.0 collective-permute-done.15
  85.9 0.0 collective-permute-done.14
  85.9 0.0 collective-permute-done.13
  85.9 0.7 copy.18
  (12 shorter events, 0.1 us)
Async XLA Ops:
  2.7 12.5 %collective-permute-start = (bf16[1,256,512]{2,1,0:T(8,128)(2,1)}, bf16[1,256,512]{2,1,0:T(8,128)(2,1)S(1)}, u32[]{:S(2)}, u32[]{:S(2)}) collective-permute-start(bf16[1,256,512]{2,1,0:T(8,128)(2,1)} %project.1.refs_0_), channel_id=1, source_target_pairs={{0,2},{1,3},{2,4},{3,5},{4,6},{5,7},{6,0},{7,1},{8,10},{9,11},{10,... | collective-permute-start | bytes 786440 | tf_op jit(solution)/shard_map/ppermute | solution.py:51
  5.7 13.8 %collective-permute-start.1 = (bf16[1,256,512]{2,1,0:T(8,128)(2,1)}, bf16[1,256,512]{2,1,0:T(8,128)(2,1)S(1)}, u32[]{:S(2)}, u32[]{:S(2)}) collective-permute-start(bf16[1,256,512]{2,1,0:T(8,128)(2,1)} %project.1.refs_0_), channel_id=1, source_target_pairs={{0,6},{1,7},{2,0},{3,1},{4,2},{5,3},{6,4},{7,5},{8,14},{9,15},{10,... | collective-permute-start | bytes 786440 | tf_op jit(solution)/shard_map/ppermute | solution.py:51
  7.7 20.4 %collective-permute-start.4 = (bf16[1,256,512]{2,1,0:T(8,128)(2,1)}, bf16[1,256,512]{2,1,0:T(8,128)(2,1)S(1)}, u32[]{:S(2)}, u32[]{:S(2)}) collective-permute-start(bf16[1,256,512]{2,1,0:T(8,128)(2,1)} %project.1.refs_0_), channel_id=1, source_target_pairs={{0,1},{1,0},{2,3},{3,2},{4,5},{5,4},{6,7},{7,6},{8,9},{9,8},{10,11... | collective-permute-start | bytes 786440 | tf_op jit(solution)/shard_map/ppermute | solution.py:55
  15.2 12.4 %collective-permute-start.2 = (bf16[1,128,512]{2,1,0:T(8,128)(2,1)S(1)}, bf16[1,128,512]{2,1,0:T(8,128)(2,1)S(1)}, u32[]{:S(2)}, u32[]{:S(2)}) collective-permute-start(bf16[1,128,512]{2,1,0:T(8,128)(2,1)S(1)} %slice.16), channel_id=1, source_target_pairs={{0,2},{1,3},{2,4},{3,5},{4,6},{5,7},{6,0},{7,1},{8,10},{9,11},{10,... | collective-permute-start | bytes 393224 | tf_op jit(solution)/shard_map/ppermute | solution.py:51
  19.6 8.1 %collective-permute-start.3 = (bf16[1,128,512]{2,1,0:T(8,128)(2,1)S(1)}, bf16[1,128,512]{2,1,0:T(8,128)(2,1)S(1)}, u32[]{:S(2)}, u32[]{:S(2)}) collective-permute-start(bf16[1,128,512]{2,1,0:T(8,128)(2,1)S(1)} %slice.17), channel_id=1, source_target_pairs={{0,6},{1,7},{2,0},{3,1},{4,2},{5,3},{6,4},{7,5},{8,14},{9,15},{10,... | collective-permute-start | bytes 393224 | tf_op jit(solution)/shard_map/ppermute | solution.py:51
  22.6 5.6 %collective-permute-start.5 = (bf16[1,256,512]{2,1,0:T(8,128)(2,1)S(1)}, bf16[1,256,512]{2,1,0:T(8,128)(2,1)S(1)}, u32[]{:S(2)}, u32[]{:S(2)}) collective-permute-start(bf16[1,256,512]{2,1,0:T(8,128)(2,1)S(1)} %collective-permute-done.refs_1_), channel_id=1, source_target_pairs={{0,1},{1,0},{2,3},{3,2},{4,5},{5,4},{6,7},{7,6},{8,9},{9,8},{10,11... | collective-permute-start | bytes 786440 | tf_op jit(solution)/shard_map/ppermute | solution.py:55
  22.6 5.6 %collective-permute-start.6 = (bf16[1,256,512]{2,1,0:T(8,128)(2,1)S(1)}, bf16[1,256,512]{2,1,0:T(8,128)(2,1)S(1)}, u32[]{:S(2)}, u32[]{:S(2)}) collective-permute-start(bf16[1,256,512]{2,1,0:T(8,128)(2,1)S(1)} %collective-permute-done.1.refs_2_), channel_id=1, source_target_pairs={{0,1},{1,0},{2,3},{3,2},{4,5},{5,4},{6,7},{7,6},{8,9},{9,8},{10,11... | collective-permute-start | bytes 786440 | tf_op jit(solution)/shard_map/ppermute | solution.py:55
  24.0 5.2 %copy-start = (bf16[1,256,512]{2,1,0:T(8,128)(2,1)S(1)}, bf16[1,256,512]{2,1,0:T(8,128)(2,1)}, u32[]{:S(2)}) copy-start(bf16[1,256,512]{2,1,0:T(8,128)(2,1)} %project.1.refs_0_) | copy-start | bytes 786436
  27.6 1.4 %collective-permute-start.7 = (bf16[1,128,512]{2,1,0:T(8,128)(2,1)S(1)}, bf16[1,128,512]{2,1,0:T(8,128)(2,1)S(1)}, u32[]{:S(2)}, u32[]{:S(2)}) collective-permute-start(bf16[1,128,512]{2,1,0:T(8,128)(2,1)S(1)} %collective-permute-done.2.refs_3_), channel_id=1, source_target_pairs={{0,1},{1,0},{2,3},{3,2},{4,5},{5,4},{6,7},{7,6},{8,9},{9,8},{10,11... | collective-permute-start | bytes 393224 | tf_op jit(solution)/shard_map/ppermute | solution.py:55
  27.7 1.5 %collective-permute-start.8 = (bf16[1,128,512]{2,1,0:T(8,128)(2,1)S(1)}, bf16[1,128,512]{2,1,0:T(8,128)(2,1)S(1)}, u32[]{:S(2)}, u32[]{:S(2)}) collective-permute-start(bf16[1,128,512]{2,1,0:T(8,128)(2,1)S(1)} %collective-permute-done.3.refs_4_), channel_id=1, source_target_pairs={{0,1},{1,0},{2,3},{3,2},{4,5},{5,4},{6,7},{7,6},{8,9},{9,8},{10,11... | collective-permute-start | bytes 393224 | tf_op jit(solution)/shard_map/ppermute | solution.py:55
  28.2 10.5 %copy-start.3 = (s32[1,128]{1,0:T(1,128)S(1)}, s32[1,128]{1,0:T(1,128)}, u32[]{:S(2)}) copy-start(s32[1,128]{1,0:T(1,128)} %param.14) | copy-start | bytes 1540
  28.2 11.6 %copy-start.2 = (s32[1,8,2]{1,2,0:T(2,128)S(1)}, s32[1,8,2]{1,2,0:T(2,128)}, u32[]{:S(2)}) copy-start(s32[1,8,2]{1,2,0:T(2,128)} %param.16) | copy-start | bytes 196
  35.1 18.8 %all-to-all-start = ((bf16[8,2,128,128]{3,2,1,0:T(8,128)(2,1)}), bf16[8,2,128,128]{3,2,1,0:T(8,128)(2,1)S(1)}, u32[]{:S(2)}, u32[]{:S(2)}) async-start(bf16[8,2,128,128]{3,2,1,0:T(8,128)(2,1)} %bitcast.4), calls=%async_computation | async-start | bytes 1048576 | tf_op jit(solution)/shard_map/all_to_all | solution.py:492
  53.9 0.8 copy-start.1
  60.0 2.2 %collective-permute-start.9 = (bf16[16,128,128]{2,1,0:T(8,128)(2,1)}, bf16[16,128,128]{2,1,0:T(8,128)(2,1)S(1)}, u32[]{:S(2)}, u32[]{:S(2)}) collective-permute-start(bf16[16,128,128]{2,1,0:T(8,128)(2,1)} %get-tuple-element.19), channel_id=1, source_target_pairs={{0,1},{1,0},{2,3},{3,2},{4,5},{5,4},{6,7},{7,6},{8,9},{9,8},{10,11... | collective-permute-start | bytes 1572872 | tf_op jit(solution)/shard_map/ppermute | solution.py:55
  63.4 10.4 %collective-permute-start.12 = (bf16[4,128,128]{2,1,0:T(8,128)(2,1)S(1)}, bf16[4,128,128]{2,1,0:T(8,128)(2,1)S(1)}, u32[]{:S(2)}, u32[]{:S(2)}) collective-permute-start(bf16[4,128,128]{2,1,0:T(8,128)(2,1)S(1)} %get-tuple-element.31), channel_id=1, source_target_pairs={{0,24},{8,16},{16,8},{24,0},{1,25},{9,17},{17,9},{25,1},{2,26},{10... | collective-permute-start | bytes 393224 | tf_op jit(solution)/shard_map/ppermute | solution.py:440
  66.0 7.9 %collective-permute-start.11 = (bf16[4,128,128]{2,1,0:T(8,128)(2,1)S(1)}, bf16[4,128,128]{2,1,0:T(8,128)(2,1)S(1)}, u32[]{:S(2)}, u32[]{:S(2)}) collective-permute-start(bf16[4,128,128]{2,1,0:T(8,128)(2,1)S(1)} %get-tuple-element.32), channel_id=1, source_target_pairs={{0,16},{8,24},{16,0},{24,8},{1,17},{9,25},{17,1},{25,9},{2,18},{10... | collective-permute-start | bytes 393224 | tf_op jit(solution)/shard_map/ppermute | solution.py:440
  66.5 7.4 %collective-permute-start.10 = (bf16[4,128,128]{2,1,0:T(8,128)(2,1)S(1)}, bf16[4,128,128]{2,1,0:T(8,128)(2,1)S(1)}, u32[]{:S(2)}, u32[]{:S(2)}) collective-permute-start(bf16[4,128,128]{2,1,0:T(8,128)(2,1)S(1)} %get-tuple-element.30), channel_id=1, source_target_pairs={{0,8},{8,0},{16,24},{24,16},{1,9},{9,1},{17,25},{25,17},{2,10},{10... | collective-permute-start | bytes 393224 | tf_op jit(solution)/shard_map/ppermute | solution.py:440
  74.0 11.9 %collective-permute-start.15 = (bf16[1,128,128]{2,1,0:T(8,128)(2,1)S(1)}, bf16[1,128,128]{2,1,0:T(8,128)(2,1)S(1)}, u32[]{:S(2)}, u32[]{:S(2)}) collective-permute-start(bf16[1,128,128]{2,1,0:T(8,128)(2,1)S(1)} %get-tuple-element.34), channel_id=1, source_target_pairs={{0,6},{1,7},{2,4},{3,5},{4,2},{5,3},{6,0},{7,1},{8,14},{9,15},{10,... | collective-permute-start | bytes 98312 | tf_op jit(solution)/shard_map/ppermute | solution.py:445
  75.0 10.8 %collective-permute-start.14 = (bf16[1,128,128]{2,1,0:T(8,128)(2,1)S(1)}, bf16[1,128,128]{2,1,0:T(8,128)(2,1)S(1)}, u32[]{:S(2)}, u32[]{:S(2)}) collective-permute-start(bf16[1,128,128]{2,1,0:T(8,128)(2,1)S(1)} %get-tuple-element.35), channel_id=1, source_target_pairs={{0,4},{1,5},{2,6},{3,7},{4,0},{5,1},{6,2},{7,3},{8,12},{9,13},{10,... | collective-permute-start | bytes 98312 | tf_op jit(solution)/shard_map/ppermute | solution.py:445
  76.1 9.7 %collective-permute-start.13 = (bf16[1,128,128]{2,1,0:T(8,128)(2,1)S(1)}, bf16[1,128,128]{2,1,0:T(8,128)(2,1)S(1)}, u32[]{:S(2)}, u32[]{:S(2)}) collective-permute-start(bf16[1,128,128]{2,1,0:T(8,128)(2,1)S(1)} %get-tuple-element.33), channel_id=1, source_target_pairs={{0,2},{1,3},{2,0},{3,1},{4,6},{5,7},{6,4},{7,5},{8,10},{9,11},{10,... | collective-permute-start | bytes 98312 | tf_op jit(solution)/shard_map/ppermute | solution.py:445
